TPU v7x, 32 devices: a whole 2x2x4 slice. The times are simulated.
32 devices in a mesh: dp: 8 (over z, x), ctx: 2 (over core), tensor: 2 (over y).
Axes of the slice: x: 2, y: 2, z: 4, core: 2. Of those that a mesh axis runs over, the one named last changes fastest.
Arguments:
- tokens: bfloat16 [16, 736, 1152], P(('dp', 'tensor'), 'ctx'), may hold values from -6 to 6
- teacher: bfloat16 [16, 736, 1152], P(('dp', 'tensor'), 'ctx'), may hold values from -6 to 6
- valid_len: int32 [16], P(('dp', 'tensor')), may hold values from 0 to 729, as said below
- ln1_gain: bfloat16 [1152], P(('dp', 'ctx')), may hold values from 0.5 to 1.5
- ln1_bias: bfloat16 [1152], P(('dp', 'ctx')), may hold values from -4 to 4
- w_q: bfloat16 [1152, 1152], P(('dp', 'ctx'), 'tensor'), may hold values from -0.25 to 0.25
- b_q: bfloat16 [1152], P('tensor'), may hold values from -4 to 4
- w_k: bfloat16 [1152, 1152], P(('dp', 'ctx'), 'tensor'), may hold values from -0.25 to 0.25
- w_v: bfloat16 [1152, 1152], P(('dp', 'ctx'), 'tensor'), may hold values from -0.1875 to 0.1875
- b_v: bfloat16 [1152], P('tensor'), may hold values from -4 to 4
- w_o: bfloat16 [1152, 1152], P('tensor', ('dp', 'ctx')), may hold values from -1.5 to 1.5
- b_o: bfloat16 [1152], P(('dp', 'ctx')), may hold values from -6 to 6
- ln2_gain: bfloat16 [1152], P(('dp', 'ctx')), may hold values from 0.5 to 1.5
- ln2_bias: bfloat16 [1152], P(('dp', 'ctx')), may hold values from -4 to 4
- w_up: bfloat16 [1152, 4304], P(('dp', 'ctx'), 'tensor'), may hold values from -0.1875 to 0.1875
- b_up: bfloat16 [4304], P('tensor'), may hold values from -6 to 6
- w_down: bfloat16 [4304, 1152], P('tensor', ('dp', 'ctx')), may hold values from -0.09375 to 0.09375
- b_down: bfloat16 [1152], P(('dp', 'ctx')), may hold values from -6 to 6
Outputs:
- layer_out: bfloat16 [16, 736, 1152], P(('dp', 'tensor'), 'ctx')
- loss: float32 [], replicated
- tokens_grad: float32 [16, 736, 1152], P(('dp', 'tensor'), 'ctx')
- ln1_gain_grad: float32 [1152], P(('dp', 'ctx'))
- ln1_bias_grad: float32 [1152], P(('dp', 'ctx'))
- w_q_grad: float32 [1152, 1152], P(('dp', 'ctx'), 'tensor')
- b_q_grad: float32 [1152], P('tensor')
- w_k_grad: float32 [1152, 1152], P(('dp', 'ctx'), 'tensor')
- w_v_grad: float32 [1152, 1152], P(('dp', 'ctx'), 'tensor')
- b_v_grad: float32 [1152], P('tensor')
- w_o_grad: float32 [1152, 1152], P('tensor', ('dp', 'ctx'))
- b_o_grad: float32 [1152], P(('dp', 'ctx'))
- ln2_gain_grad: float32 [1152], P(('dp', 'ctx'))
- ln2_bias_grad: float32 [1152], P(('dp', 'ctx'))
- w_up_grad: float32 [1152, 4304], P(('dp', 'ctx'), 'tensor')
- b_up_grad: float32 [4304], P('tensor')
- w_down_grad: float32 [4304, 1152], P('tensor', ('dp', 'ctx'))
- b_down_grad: float32 [1152], P(('dp', 'ctx'))
Inputs may be any that keep to these rules, and one draw needn't show every extreme that they name: The first valid_len[s] token positions of slot s are valid and the others are not; the last slot has exactly 729 valid tokens.
All inputs are finite; a program needn't handle non-finite values.
Results may differ from a plain program's by a relative error of at most 0.014.
Values may be sent and summed in bfloat16 or wider, within the bound.
A program may use at most 192 MiB of HBM per device.

v0:
```python
import jax
import jax.numpy as jnp
from jax import lax
from jax.sharding import PartitionSpec as P

HD = 72
REAL = 729


EPSILON = 1e-06
GELU_C = 0.7978845608028654
GELU_K = 0.044715


def norm_forward(row_values, gain_vec, shift_vec):
    average = jnp.mean(row_values, axis=-1, keepdims=True)
    centred = row_values - average
    spread = jnp.mean(centred * centred, axis=-1, keepdims=True)
    inverse = lax.rsqrt(spread + EPSILON)
    unit_rows = centred * inverse
    return (unit_rows * gain_vec + shift_vec, unit_rows, inverse)


def norm_backward(upstream, unit_rows, inverse, gain_vec):
    scaled = upstream * gain_vec
    inner_sum = (
        scaled
        - jnp.mean(scaled, axis=-1, keepdims=True)
        - unit_rows * jnp.mean(scaled * unit_rows, axis=-1, keepdims=True)
    )
    return (inner_sum * inverse, jnp.sum(upstream * unit_rows, axis=0), jnp.sum(upstream, axis=0))


def gelu_tanh(values):
    return 0.5 * values * (1.0 + jnp.tanh(GELU_C * (values + GELU_K * values * values * values)))


def gelu_slope(values):
    tanh_part = jnp.tanh(GELU_C * (values + GELU_K * values * values * values))
    return 0.5 * (1.0 + tanh_part) + 0.5 * values * (1.0 - tanh_part * tanh_part) * GELU_C * (
        1.0 + 3.0 * GELU_K * values * values
    )


def gather_rows(row_values):
    return lax.all_gather(row_values, "tensor", axis=0, tiled=True)


def sum_rows(term_rows):
    return lax.psum_scatter(
        term_rows.astype(jnp.bfloat16), "tensor", scatter_dimension=0, tiled=True
    ).astype(jnp.float32)


def gather_grads(row_values):
    return lax.all_gather(row_values, "tensor", axis=0, tiled=True)


def sum_grads(term_rows):
    return lax.psum_scatter(
        term_rows.astype(jnp.bfloat16), "tensor", scatter_dimension=0, tiled=True
    ).astype(jnp.float32)


def on_device(
    tokens,
    teacher,
    valid_len,
    ln1_gain,
    ln1_bias,
    w_q,
    b_q,
    w_k,
    w_v,
    b_v,
    w_o,
    b_o,
    ln2_gain,
    ln2_bias,
    w_up,
    b_up,
    w_down,
    b_down,
):
    own_images, half_len, width = tokens.shape
    seq_len = half_len * lax.axis_size("ctx")
    local_heads = w_q.shape[1] // HD
    head_width = local_heads * HD
    all_heads = head_width * lax.axis_size("tensor")
    layer_parts = (
        lax.all_gather(ln1_gain, ("dp", "ctx"), axis=0, tiled=True),
        lax.all_gather(ln1_bias, ("dp", "ctx"), axis=0, tiled=True),
        lax.all_gather(w_q, ("dp", "ctx"), axis=0, tiled=True),
        lax.all_gather(w_k, ("dp", "ctx"), axis=0, tiled=True),
        lax.all_gather(w_v, ("dp", "ctx"), axis=0, tiled=True),
        lax.all_gather(w_o, ("dp", "ctx"), axis=1, tiled=True),
        lax.all_gather(b_o, ("dp", "ctx"), axis=0, tiled=True),
        lax.all_gather(ln2_gain, ("dp", "ctx"), axis=0, tiled=True),
        lax.all_gather(ln2_bias, ("dp", "ctx"), axis=0, tiled=True),
        lax.all_gather(w_up, ("dp", "ctx"), axis=0, tiled=True),
        lax.all_gather(w_down, ("dp", "ctx"), axis=1, tiled=True),
        lax.all_gather(b_down, ("dp", "ctx"), axis=0, tiled=True),
    )
    (
        gain_one,
        shift_one,
        query_w,
        key_w,
        value_w,
        out_w,
        out_bias,
        gain_two,
        shift_two,
        up_w,
        down_w,
        down_bias,
    ) = layer_parts
    gain_one = gain_one.astype(jnp.float32)
    shift_one = shift_one.astype(jnp.float32)
    out_bias = out_bias.astype(jnp.float32)
    gain_two = gain_two.astype(jnp.float32)
    shift_two = shift_two.astype(jnp.float32)
    down_bias = down_bias.astype(jnp.float32)
    own_rows = own_images * half_len
    query_per_head = query_w.reshape(width, local_heads, HD)
    key_per_head = key_w.reshape(width, local_heads, HD)
    value_per_head = value_w.reshape(width, local_heads, HD)
    output_per_head = out_w.reshape(local_heads, HD, width)
    query_bias = b_q.astype(jnp.float32).reshape(1, local_heads, 1, HD)
    value_bias = b_v.astype(jnp.float32).reshape(1, local_heads, 1, HD)
    inputs = tokens.astype(jnp.float32).reshape(own_rows, width)
    normed, unit_one, inverse_one = norm_forward(inputs, gain_one, shift_one)
    normed_every_row = gather_rows(normed.astype(jnp.bfloat16).reshape(own_images, half_len, width))
    all_images = normed_every_row.shape[0]
    all_rows = all_images * half_len
    queries = (
        jnp.einsum(
            "pro,ojx->pjrx", normed_every_row, query_per_head, preferred_element_type=jnp.float32
        )
        + query_bias
    ).astype(jnp.bfloat16)
    key_rows = jnp.einsum(
        "pro,ojx->pjrx", normed_every_row, key_per_head, preferred_element_type=jnp.float32
    ).astype(jnp.bfloat16)
    value_rows = (
        jnp.einsum(
            "pro,ojx->pjrx", normed_every_row, value_per_head, preferred_element_type=jnp.float32
        )
        + value_bias
    ).astype(jnp.bfloat16)
    key_all, value_all = (
        lax.all_gather(key_rows, "ctx", axis=2, tiled=True),
        lax.all_gather(value_rows, "ctx", axis=2, tiled=True),
    )
    pair_count = all_images // 2
    query_blocks = queries.reshape(pair_count, 2, local_heads, half_len, HD)
    key_blocks = key_all.reshape(pair_count, 2, local_heads, seq_len, HD)
    value_blocks = value_all.reshape(pair_count, 2, local_heads, seq_len, HD)
    usable = jnp.arange(seq_len) < REAL
    score_scale = HD ** (-0.5)

    def attend(block_item):
        query_blk, key_blk, value_blk = block_item
        raw_scores = jnp.einsum(
            "bhqe,bhke->bhqk", query_blk, key_blk, preferred_element_type=jnp.float32
        )
        scores = jnp.where(usable, raw_scores * score_scale, -1e30)
        summit = jnp.max(scores, axis=-1, keepdims=True)
        exp_total = jnp.sum(jnp.exp(scores - summit), axis=-1, keepdims=True)
        log_total = summit + jnp.log(exp_total)
        soft_weights = jnp.exp(scores - log_total).astype(jnp.bfloat16)
        mixed_blk = jnp.einsum(
            "bhqk,bhke->bhqe", soft_weights, value_blk, preferred_element_type=jnp.float32
        )
        return (mixed_blk.astype(jnp.bfloat16), log_total[..., 0])

    mixed_blocks, log_totals = lax.map(attend, (query_blocks, key_blocks, value_blocks))
    mixed_per_head = mixed_blocks.reshape(all_images, local_heads, half_len, HD)
    attn_terms = jnp.einsum(
        "lscm,smt->lct", mixed_per_head, output_per_head, preferred_element_type=jnp.float32
    )
    attn_sum = sum_rows(attn_terms).reshape(own_rows, width)
    hidden = inputs + attn_sum + out_bias
    normed_two, unit_two, inverse_two = norm_forward(hidden, gain_two, shift_two)
    normed_two_all = gather_rows(
        normed_two.astype(jnp.bfloat16).reshape(own_images, half_len, width)
    ).reshape(all_rows, width)
    before = jnp.dot(normed_two_all, up_w, preferred_element_type=jnp.float32) + b_up.astype(
        jnp.float32
    )
    active = gelu_tanh(before).astype(jnp.bfloat16)
    mlp_terms = jnp.dot(active, down_w, preferred_element_type=jnp.float32).reshape(
        all_images, half_len, width
    )
    result = hidden + sum_rows(mlp_terms).reshape(own_rows, width) + down_bias
    layer_out = result.astype(jnp.bfloat16).reshape(own_images, half_len, width)
    position = lax.axis_index("ctx") * half_len + jnp.arange(half_len)
    valid_rows = (position[None, :] < valid_len[:, None]).astype(jnp.float32).reshape(own_rows)
    error_rows = result - teacher.astype(jnp.float32).reshape(own_rows, width)
    partial_value = 0.5 * jnp.sum(valid_rows * jnp.mean(error_rows * error_rows, axis=-1))
    loss_sum, valid_count = lax.psum((partial_value, jnp.sum(valid_rows)), ("dp", "ctx", "tensor"))
    loss_value = loss_sum / valid_count
    slot_total = own_images * lax.axis_size("dp") * lax.axis_size("tensor")
    factor = slot_total * seq_len / valid_count
    grad_out = error_rows * (valid_rows[:, None] * factor)
    grad_rows = gather_grads(
        grad_out.astype(jnp.bfloat16).reshape(own_images, half_len, width)
    ).reshape(all_rows, width)
    down_grad = jnp.einsum("rf,rd->fd", active, grad_rows, preferred_element_type=jnp.float32)
    active_grad = jnp.einsum("rd,fd->rf", grad_rows, down_w, preferred_element_type=jnp.float32)
    before_grad = (active_grad * gelu_slope(before)).astype(jnp.bfloat16)
    up_bias_grad = jnp.sum(before_grad, axis=0, dtype=jnp.float32)
    up_grad = jnp.einsum(
        "rd,rf->df", normed_two_all, before_grad, preferred_element_type=jnp.float32
    )
    norm_two_terms = jnp.einsum("rf,df->rd", before_grad, up_w, preferred_element_type=jnp.float32)
    norm_two_grad = sum_grads(norm_two_terms.reshape(all_images, half_len, width)).reshape(
        own_rows, width
    )
    hidden_back, gain_two_grad, shift_two_grad = norm_backward(
        norm_two_grad, unit_two, inverse_two, gain_two
    )
    hidden_grad = grad_out + hidden_back
    down_bias_grad = jnp.sum(grad_out, axis=0)
    out_bias_grad = jnp.sum(hidden_grad, axis=0)
    hidden_token_rows = gather_grads(
        hidden_grad.astype(jnp.bfloat16).reshape(own_images, half_len, width)
    )
    out_grad = jnp.einsum(
        "nvli,nlp->vip", mixed_per_head, hidden_token_rows, preferred_element_type=jnp.float32
    ).reshape(head_width, width)
    mixed_grad = jnp.einsum(
        "fyk,swk->fsyw", hidden_token_rows, output_per_head, preferred_element_type=jnp.float32
    ).astype(jnp.bfloat16)

    def attend_back(block_item):
        query_blk, key_blk, value_blk, log_blk, grad_blk = block_item
        raw_scores = jnp.einsum(
            "bhqe,bhke->bhqk", query_blk, key_blk, preferred_element_type=jnp.float32
        )
        scores = jnp.where(usable, raw_scores * score_scale, -1e30)
        soft_full = jnp.exp(scores - log_blk[..., None])
        soft_grad = jnp.einsum(
            "bhqe,bhke->bhqk", grad_blk, value_blk, preferred_element_type=jnp.float32
        )
        value_grad = jnp.einsum(
            "bhqk,bhqe->bhke",
            soft_full.astype(jnp.bfloat16),
            grad_blk,
            preferred_element_type=jnp.float32,
        )
        inner_sum = jnp.sum(soft_full * soft_grad, axis=-1, keepdims=True)
        score_grad = (soft_full * (soft_grad - inner_sum)).astype(jnp.bfloat16)
        query_grad = (
            jnp.einsum("bhqk,bhke->bhqe", score_grad, key_blk, preferred_element_type=jnp.float32)
            * score_scale
        )
        key_grad = (
            jnp.einsum("bhqk,bhqe->bhke", score_grad, query_blk, preferred_element_type=jnp.float32)
            * score_scale
        )
        return (query_grad, key_grad, value_grad)

    query_grads, key_grads, value_grads = lax.map(
        attend_back,
        (
            query_blocks,
            key_blocks,
            value_blocks,
            log_totals,
            mixed_grad.reshape(pair_count, 2, local_heads, half_len, HD),
        ),
    )
    key_sum, value_sum = (
        lax.psum_scatter(
            key_grads.reshape(all_images, local_heads, seq_len, HD).astype(jnp.bfloat16),
            "ctx",
            scatter_dimension=2,
            tiled=True,
        ).astype(jnp.float32),
        lax.psum_scatter(
            value_grads.reshape(all_images, local_heads, seq_len, HD).astype(jnp.bfloat16),
            "ctx",
            scatter_dimension=2,
            tiled=True,
        ).astype(jnp.float32),
    )
    query_reduced_precision = query_grads.reshape(all_images, local_heads, half_len, HD).astype(
        jnp.bfloat16
    )
    key_reduced_precision = key_sum.astype(jnp.bfloat16)
    value_reduced_precision = value_sum.astype(jnp.bfloat16)
    query_bias_grad = jnp.sum(query_reduced_precision, axis=(0, 2), dtype=jnp.float32).reshape(
        head_width
    )
    value_bias_grad = jnp.sum(value_reduced_precision, axis=(0, 2), dtype=jnp.float32).reshape(
        head_width
    )
    query_weight_grad = jnp.einsum(
        "okz,oaks->zas",
        normed_every_row,
        query_reduced_precision,
        preferred_element_type=jnp.float32,
    ).reshape(width, head_width)
    key_weight_grad = jnp.einsum(
        "okz,oaks->zas", normed_every_row, key_reduced_precision, preferred_element_type=jnp.float32
    ).reshape(width, head_width)
    value_weight_grad = jnp.einsum(
        "okz,oaks->zas",
        normed_every_row,
        value_reduced_precision,
        preferred_element_type=jnp.float32,
    ).reshape(width, head_width)
    norm_one_terms = jnp.einsum(
        "tivw,niw->tvn", query_reduced_precision, query_per_head, preferred_element_type=jnp.float32
    )
    norm_one_terms = norm_one_terms + jnp.einsum(
        "tivw,niw->tvn", key_reduced_precision, key_per_head, preferred_element_type=jnp.float32
    )
    norm_one_terms = norm_one_terms + jnp.einsum(
        "tivw,niw->tvn", value_reduced_precision, value_per_head, preferred_element_type=jnp.float32
    )
    norm_one_grad = sum_grads(norm_one_terms).reshape(own_rows, width)
    input_back, gain_one_grad, shift_one_grad = norm_backward(
        norm_one_grad, unit_one, inverse_one, gain_one
    )
    tokens_grad = (hidden_grad + input_back).reshape(own_images, half_len, width)
    query_shard, key_shard, value_shard, out_shard, up_shard, down_shard = (
        lax.psum_scatter(
            query_weight_grad.astype(jnp.bfloat16), ("dp", "ctx"), scatter_dimension=0, tiled=True
        ).astype(jnp.float32),
        lax.psum_scatter(
            key_weight_grad.astype(jnp.bfloat16), ("dp", "ctx"), scatter_dimension=0, tiled=True
        ).astype(jnp.float32),
        lax.psum_scatter(
            value_weight_grad.astype(jnp.bfloat16), ("dp", "ctx"), scatter_dimension=0, tiled=True
        ).astype(jnp.float32),
        lax.psum_scatter(
            out_grad.astype(jnp.bfloat16), ("dp", "ctx"), scatter_dimension=1, tiled=True
        ).astype(jnp.float32),
        lax.psum_scatter(
            up_grad.astype(jnp.bfloat16), ("dp", "ctx"), scatter_dimension=0, tiled=True
        ).astype(jnp.float32),
        lax.psum_scatter(
            down_grad.astype(jnp.bfloat16), ("dp", "ctx"), scatter_dimension=1, tiled=True
        ).astype(jnp.float32),
    )
    tensor_pos = lax.axis_index("tensor")
    hidden_width = up_bias_grad.shape[0]

    def spread_out(local_vec, total_len):
        return lax.dynamic_update_slice_in_dim(
            jnp.zeros((total_len,), jnp.float32), local_vec, tensor_pos * local_vec.shape[0], 0
        )

    query_bias_full = spread_out(query_bias_grad, all_heads)
    value_bias_full = spread_out(value_bias_grad, all_heads)
    up_bias_full = spread_out(up_bias_grad, hidden_width * lax.axis_size("tensor"))
    vector_sums = lax.psum(
        (
            gain_one_grad,
            shift_one_grad,
            out_bias_grad,
            gain_two_grad,
            shift_two_grad,
            down_bias_grad,
            query_bias_full,
            value_bias_full,
            up_bias_full,
        ),
        ("dp", "ctx", "tensor"),
    )
    piece_len = width // lax.axis_size(("dp", "ctx"))
    piece_start = lax.axis_index(("dp", "ctx")) * piece_len
    vector_shards = [
        lax.dynamic_slice_in_dim(summed_vec, piece_start, piece_len)
        for summed_vec in vector_sums[:6]
    ]
    query_bias_sum = lax.dynamic_slice_in_dim(vector_sums[6], tensor_pos * head_width, head_width)
    value_bias_sum = lax.dynamic_slice_in_dim(vector_sums[7], tensor_pos * head_width, head_width)
    up_bias_sum = lax.dynamic_slice_in_dim(vector_sums[8], tensor_pos * hidden_width, hidden_width)
    return (
        layer_out,
        loss_value,
        tokens_grad,
        vector_shards[0],
        vector_shards[1],
        query_shard,
        query_bias_sum,
        key_shard,
        value_shard,
        value_bias_sum,
        out_shard,
        vector_shards[2],
        vector_shards[3],
        vector_shards[4],
        up_shard,
        up_bias_sum,
        down_shard,
        vector_shards[5],
    )


def solution(mesh):
    return jax.shard_map(
        on_device,
        mesh=mesh,
        in_specs=(
            P(("dp", "tensor"), "ctx", None),
            P(("dp", "tensor"), "ctx", None),
            P(("dp", "tensor")),
            P(("dp", "ctx")),
            P(("dp", "ctx")),
            P(("dp", "ctx"), "tensor"),
            P("tensor"),
            P(("dp", "ctx"), "tensor"),
            P(("dp", "ctx"), "tensor"),
            P("tensor"),
            P("tensor", ("dp", "ctx")),
            P(("dp", "ctx")),
            P(("dp", "ctx")),
            P(("dp", "ctx")),
            P(("dp", "ctx"), "tensor"),
            P("tensor"),
            P("tensor", ("dp", "ctx")),
            P(("dp", "ctx")),
        ),
        out_specs=(
            P(("dp", "tensor"), "ctx", None),
            P(),
            P(("dp", "tensor"), "ctx", None),
            P(("dp", "ctx")),
            P(("dp", "ctx")),
            P(("dp", "ctx"), "tensor"),
            P("tensor"),
            P(("dp", "ctx"), "tensor"),
            P(("dp", "ctx"), "tensor"),
            P("tensor"),
            P("tensor", ("dp", "ctx")),
            P(("dp", "ctx")),
            P(("dp", "ctx")),
            P(("dp", "ctx")),
            P(("dp", "ctx"), "tensor"),
            P("tensor"),
            P("tensor", ("dp", "ctx")),
            P(("dp", "ctx")),
        ),
        check_vma=False,
    )
```

profile of v0, /device:TPU:0, one launch (start us, length us, event | category | flops | bytes accessed | tf_op | source)
XLA Modules:
  0.0 1190.0 jit_solution(12876756764609822542)
XLA Ops:
  15.0 63.1 %all-reduce.13 = (bf16[1152]{0:T(1024)(128)(2,1)S(1)}, bf16[1152]{0:T(1024)(128)(2,1)S(1)}, bf16[1152]{0:T(1024)(128)(2,1)S(1)}, bf16[1152]{0:T(1024)(128)(2,1)S...) all-reduce(bf16[1152]{0:T(1024)(128)(2,1)S(1)} %dynamic-update-slic, ...), channel_id=1, replica_groups=mesh['dp'=8,'ctx'=2,'tensor'=2] {'dp','ctx'}, use_global_device_ids=true, to_apply=%add.1 | all-reduce | flops 6912 | bytes 27648
  86.2 22.1 %all-gather.13.cloned.1.call-done = bf16[2,368,1152]{2,1,0:T(8,128)(2,1)} async-done(((bf16[1,368,1152]{2,1,0:T(8,128)(2,1)}), bf16[2,368,1152]{2,1,0:T(8,128)(2,1)}) %all-gather.13.cloned.1.call-update) | async-done | bytes 1695760 | tf_op jit(solution)/shard_map/all_gather | solution.py:46
  115.2 34.5 %all-gather.21.cloned.1.call-done = bf16[1152,576]{1,0:T(8,128)(2,1)} async-done(((bf16[72,576]{1,0:T(8,128)(2,1)}), bf16[1152,576]{1,0:T(8,128)(2,1)}) %all-gather.21.cloned.1.call-update) | async-done | bytes 1327120 | tf_op jit(solution)/shard_map/all_gather | solution.py:95
  159.1 30.5 %all-gather.15.cloned.1.call-done = bf16[1152,576]{1,0:T(8,128)(2,1)} async-done(((bf16[72,576]{1,0:T(8,128)(2,1)}), bf16[1152,576]{1,0:T(8,128)(2,1)}) %all-gather.15.cloned.1.call-update) | async-done | bytes 1327120 | tf_op jit(solution)/shard_map/all_gather | solution.py:93
  191.6 38.1 %all-gather.25.cloned.1.call-done = bf16[576,1152]{0,1:T(8,128)(2,1)} async-done(((bf16[576,72]{0,1:T(8,128)(2,1)}), bf16[576,1152]{0,1:T(8,128)(2,1)}) %all-gather.25.cloned.1.call-update) | async-done | bytes 1327120 | tf_op jit(solution)/shard_map/all_gather | solution.py:96
  276.2 28.6 %reduce-scatter.29.cloned.1.call-done = bf16[1,368,1152]{2,1,0:T(8,128)(2,1)} async-done(((bf16[2,368,1152]{2,1,0:T(8,128)(2,1)}), bf16[1,368,1152]{2,1,0:T(8,128)(2,1)}) %reduce-scatter.29.cloned.1.call-update) | async-done | bytes 847888 | tf_op jit(solution)/shard_map/reduce_scatter | solution.py:50
  309.7 27.3 %all-gather.27.cloned.1.call-done = bf16[2,368,1152]{2,1,0:T(8,128)(2,1)} async-done(((bf16[1,368,1152]{2,1,0:T(8,128)(2,1)}), bf16[2,368,1152]{2,1,0:T(8,128)(2,1)}) %all-gather.27.cloned.1.call-update) | async-done | bytes 1695760 | tf_op jit(solution)/shard_map/all_gather | solution.py:46
  337.0 56.5 %all-gather.29.cloned.1.call-done = bf16[1152,2152]{1,0:T(8,128)(2,1)} async-done(((bf16[72,2152]{1,0:T(8,128)(2,1)}), bf16[1152,2152]{1,0:T(8,128)(2,1)}) %all-gather.29.cloned.1.call-update) | async-done | bytes 4958224 | tf_op jit(solution)/shard_map/all_gather | solution.py:100
  403.7 45.1 %all-gather.31.cloned.1.call-done = bf16[2152,1152]{0,1:T(8,128)(2,1)} async-done(((bf16[2152,72]{0,1:T(8,128)(2,1)}), bf16[2152,1152]{0,1:T(8,128)(2,1)}) %all-gather.31.cloned.1.call-update) | async-done | bytes 4958224 | tf_op jit(solution)/shard_map/all_gather | solution.py:101
  448.8 11.1 convolution_convert_fusion.3
  461.4 39.8 %psum.78 = f32[]{:T(128)} all-reduce(f32[]{:T(128)} %convert_reduce_fusion.6), channel_id=1, replica_groups=mesh['dp'=8,'ctx'=2,'tensor'=2] {'dp','ctx','tensor'}, use_global_device_ids=true, to_apply=%region_12.13 | all-reduce | flops 1 | bytes 8 | tf_op jit(solution)/shard_map/psum | solution.py:201
  505.0 29.1 %all-gather.33.cloned.1.call-done = bf16[2,368,1152]{2,1,0:T(8,128)(2,1)} async-done(((bf16[1,368,1152]{2,1,0:T(8,128)(2,1)}), bf16[2,368,1152]{2,1,0:T(8,128)(2,1)}) %all-gather.33.cloned.1.call-update) | async-done | bytes 1695760 | tf_op jit(solution)/shard_map/all_gather | solution.py:56
  534.0 11.0 convert_reduce_fusion
  551.1 27.6 %reduce-scatter.33.cloned.1.call-done = bf16[1,368,1152]{2,1,0:T(8,128)(2,1)} async-done(((bf16[2,368,1152]{2,1,0:T(8,128)(2,1)}), bf16[1,368,1152]{2,1,0:T(8,128)(2,1)}) %reduce-scatter.33.cloned.1.call-update) | async-done | bytes 847888 | tf_op jit(solution)/shard_map/reduce_scatter | solution.py:60
  585.0 28.7 %all-gather.35.cloned.1.call-done = bf16[2,368,1152]{2,1,0:T(8,128)(2,1)} async-done(((bf16[1,368,1152]{2,1,0:T(8,128)(2,1)}), bf16[2,368,1152]{2,1,0:T(8,128)(2,1)}) %all-gather.35.cloned.1.call-update) | async-done | bytes 1695760 | tf_op jit(solution)/shard_map/all_gather | solution.py:56
  638.3 14.1 %multiply_reduce_fusion = (f32[2,8,368]{2,1,0:T(8,128)S(1)}, f32[2,8,368,736]{3,2,1,0:T(8,128)}) fusion(f32[2,8,368,736]{3,2,1,0:T(8,128)} %copy-done, f32[2,8,368]{2,1,0:T(8,128)S(1)} %log_add_fusion, pred[736]{0:T(1024)(128)(4,1)S(1)} %iota_compare_fusion, bf16[2,8,368,72]{2,3,1,0:T(8,128)(2,1)} %copy-done.13, bf16[2,8,736,72]{2,3,1,0:T(8,128)(2,1)} %copy-done.7), kind=kOutput, calls=%fused_computation.1 | convolution fusion | flops 645695744 | bytes 37260000 | tf_op jit(solution)/shard_map/while/body/eval_jaxpr/bhqe,bhke->bhqk/dot_general | solution.py:243
  652.3 12.8 %multiply_convert_fusion = bf16[2,8,368,736]{3,2,1,0:T(8,128)(2,1)S(1)} fusion(f32[2,8,368,736]{3,2,1,0:T(8,128)} %get-tuple-element.106, f32[2,8,368,736]{3,2,1,0:T(8,128)} %copy-done, f32[2,8,368]{2,1,0:T(8,128)S(1)} %get-tuple-element.105, f32[2,8,368]{2,1,0:T(8,128)S(1)} %log_add_fusion, pred[736]{0:T(1024)(128)(4,1)S(1)} %iota_compare_fusion), kind=kLoop, calls=%fused_computation | loop fusion | flops 26001408 | bytes 43383520 | tf_op jit(solution)/shard_map/while/body/eval_jaxpr/convert_element_type | solution.py:253
  761.3 55.0 %reduce-scatter.41.cloned.1.call-done = bf16[72,576]{1,0:T(8,128)(2,1)} async-done(((bf16[1152,576]{1,0:T(8,128)(2,1)}), bf16[72,576]{1,0:T(8,128)(2,1)}) %reduce-scatter.41.cloned.1.call-update) | async-done | bytes 82960
  817.8 77.5 %reduce-scatter.51.cloned.1.call-done = bf16[2152,72]{0,1:T(8,128)(2,1)} async-done(((bf16[2152,1152]{0,1:T(8,128)(2,1)}), bf16[2152,72]{0,1:T(8,128)(2,1)}) %reduce-scatter.51.cloned.1.call-update) | async-done | bytes 309904
  897.2 77.6 %reduce-scatter.49.cloned.1.call-done = bf16[72,2152]{1,0:T(8,128)(2,1)} async-done(((bf16[1152,2152]{1,0:T(8,128)(2,1)}), bf16[72,2152]{1,0:T(8,128)(2,1)}) %reduce-scatter.49.cloned.1.call-update) | async-done | bytes 309904
  978.4 57.0 %reduce-scatter.45.cloned.1.call-done = bf16[72,576]{1,0:T(8,128)(2,1)} async-done(((bf16[1152,576]{1,0:T(8,128)(2,1)}), bf16[72,576]{1,0:T(8,128)(2,1)}) %reduce-scatter.45.cloned.1.call-update) | async-done | bytes 82960
  1036.9 59.0 %reduce-scatter.43.cloned.1.call-done = bf16[72,576]{1,0:T(8,128)(2,1)} async-done(((bf16[1152,576]{1,0:T(8,128)(2,1)}), bf16[72,576]{1,0:T(8,128)(2,1)}) %reduce-scatter.43.cloned.1.call-update) | async-done | bytes 82960
  1097.5 27.0 %reduce-scatter.35.cloned.1.call-done = bf16[1,368,1152]{2,1,0:T(8,128)(2,1)} async-done(((bf16[2,368,1152]{2,1,0:T(8,128)(2,1)}), bf16[1,368,1152]{2,1,0:T(8,128)(2,1)}) %reduce-scatter.35.cloned.1.call-update) | async-done | bytes 847888 | tf_op jit(solution)/shard_map/reduce_scatter | solution.py:60
  1133.4 41.3 %all-reduce.12 = (f32[]{:T(128)}, f32[1152]{0:T(1024)S(1)}, f32[1152]{0:T(1024)S(1)}, f32[1152]{0:T(1024)S(1)}, f32[1152]{0:T(1024)S(1)}, /*index=5*/f32[1152]{0...) all-reduce(f32[]{:T(128)S(6)} %mul.273, ...), channel_id=1, replica_groups=mesh['dp'=8,'ctx'=2,'tensor'=2] {'dp','ctx','tensor'}, use_global_device_ids=true, to_apply=%region_10.11 | all-reduce | flops 13521 | bytes 108168 | tf_op jit(solution)/shard_map/psum | solution.py:201
  (223 shorter events, 254.9 us)
Async XLA Ops:
  7.2 77.1 %all-gather.17.cloned.1.call-start = ((), (), s32[]{:S(2)}) async-start(), calls=%async_computation.14 | async-start | bytes 1566720 | tf_op jit(solution)/shard_map/all_gather | solution.py:94
  7.9 100.4 %all-gather.13.cloned.1.call-start = ((), (), s32[]{:S(2)}) async-start(), calls=%async_computation.12 | async-start | bytes 2543616 | tf_op jit(solution)/shard_map/all_gather | solution.py:46
  82.3 67.3 %all-gather.21.cloned.1.call-start = ((), (), s32[]{:S(2)}) async-start(), calls=%async_computation.16 | async-start | bytes 1566720 | tf_op jit(solution)/shard_map/all_gather | solution.py:95
  83.1 106.6 %all-gather.15.cloned.1.call-start = ((), (), s32[]{:S(2)}) async-start(), calls=%async_computation.13 | async-start | bytes 1566720 | tf_op jit(solution)/shard_map/all_gather | solution.py:93
  83.6 146.0 %all-gather.25.cloned.1.call-start = ((), (), s32[]{:S(2)}) async-start(), calls=%async_computation.18 | async-start | bytes 1566720 | tf_op jit(solution)/shard_map/all_gather | solution.py:96
  84.2 157.6 %all-gather.19.cloned.1.call-start = ((), (), s32[]{:S(2)}) async-start(), calls=%async_computation.15 | async-start | bytes 4521984 | tf_op jit(solution)/shard_map/all_gather | solution.py:152
  115.0 143.1 %all-gather.23.cloned.1.call-start = ((), (), s32[]{:S(2)}) async-start(), calls=%async_computation.17 | async-start | bytes 4521984 | tf_op jit(solution)/shard_map/all_gather | solution.py:153
  158.6 146.2 %reduce-scatter.29.cloned.1.call-start = ((), (), s32[]{:S(2)}) async-start(), calls=%async_computation.19 | async-start | bytes 2543616 | tf_op jit(solution)/shard_map/reduce_scatter | solution.py:50
  275.9 61.1 %all-gather.27.cloned.1.call-start = ((), (), s32[]{:S(2)}) async-start(), calls=%async_computation.20 | async-start | bytes 2543616 | tf_op jit(solution)/shard_map/all_gather | solution.py:46
  308.3 85.3 %all-gather.29.cloned.1.call-start = ((), (), s32[]{:S(2)}) async-start(), calls=%async_computation.21 | async-start | bytes 5326848 | tf_op jit(solution)/shard_map/all_gather | solution.py:100
  308.9 139.9 %all-gather.31.cloned.1.call-start = ((), (), s32[]{:S(2)}) async-start(), calls=%async_computation.22 | async-start | bytes 5326848 | tf_op jit(solution)/shard_map/all_gather | solution.py:101
  309.6 192.3 %reduce-scatter.31.cloned.1.call-start = ((), (), s32[]{:S(2)}) async-start(), calls=%async_computation.23 | async-start | bytes 2543616 | tf_op jit(solution)/shard_map/reduce_scatter | solution.py:50
  460.0 74.0 %all-gather.33.cloned.1.call-start = ((), (), s32[]{:S(2)}) async-start(), calls=%async_computation.24 | async-start | bytes 2543616 | tf_op jit(solution)/shard_map/all_gather | solution.py:56
  504.7 74.0 %reduce-scatter.33.cloned.1.call-start = ((), (), s32[]{:S(2)}) async-start(), calls=%async_computation.25 | async-start | bytes 2543616 | tf_op jit(solution)/shard_map/reduce_scatter | solution.py:60
  551.0 62.6 %all-gather.35.cloned.1.call-start = ((), (), s32[]{:S(2)}) async-start(), calls=%async_computation.26 | async-start | bytes 2543616 | tf_op jit(solution)/shard_map/all_gather | solution.py:56
  585.0 136.3 %reduce-scatter.39.cloned.1.call-start = ((), (), s32[]{:S(2)}) async-start(), calls=%async_computation.29 | async-start | bytes 2543616
  637.8 94.9 %reduce-scatter.37.cloned.1.call-start = ((), (), s32[]{:S(2)}) async-start(), calls=%async_computation.28 | async-start | bytes 2543616
  683.5 76.2 %reduce-scatter.47.cloned.1.call-start = ((), (), s32[]{:S(2)}) async-start(), calls=%async_computation.33 | async-start | bytes 1566720
  690.3 125.9 %reduce-scatter.41.cloned.1.call-start = ((), (), s32[]{:S(2)}) async-start(), calls=%async_computation.30 | async-start | bytes 1566720
  701.5 193.9 %reduce-scatter.51.cloned.1.call-start = ((), (), s32[]{:S(2)}) async-start(), calls=%async_computation.35 | async-start | bytes 5326848
  711.7 263.0 %reduce-scatter.49.cloned.1.call-start = ((), (), s32[]{:S(2)}) async-start(), calls=%async_computation.34 | async-start | bytes 5326848
  721.2 314.2 %reduce-scatter.45.cloned.1.call-start = ((), (), s32[]{:S(2)}) async-start(), calls=%async_computation.32 | async-start | bytes 1566720
  732.7 363.3 %reduce-scatter.43.cloned.1.call-start = ((), (), s32[]{:S(2)}) async-start(), calls=%async_computation.31 | async-start | bytes 1566720
  744.3 380.2 %reduce-scatter.35.cloned.1.call-start = ((), (), s32[]{:S(2)}) async-start(), calls=%async_computation.27 | async-start | bytes 2543616 | tf_op jit(solution)/shard_map/reduce_scatter | solution.py:60
  (29 other events, 1241.3 us)
Sparse Core Ops, SparseCore 0:
  10.2 42.0 all-gather.16
  82.4 25.8 all-gather.12
  110.5 39.1 all-gather.20
  151.7 37.9 all-gather.14
  191.7 37.9 all-gather.24
  231.1 10.7 all-gather.18
  244.0 13.0 all-gather.22
  276.0 28.6 reduce-scatter.28
  308.4 28.5 all-gather.26
  339.0 54.4 all-gather.28
  395.7 53.0 all-gather.30
  460.1 26.7 reduce-scatter.30
  504.8 29.1 all-gather.32
  551.2 27.5 reduce-scatter.32
  585.1 28.5 all-gather.34
  637.9 9.1 reduce-scatter.38
  683.6 9.1 reduce-scatter.36
  696.4 59.1 reduce-scatter.46
  759.4 56.8 reduce-scatter.40
  820.1 75.2 reduce-scatter.50
  899.3 75.3 reduce-scatter.48
  978.5 56.7 reduce-scatter.44
  1039.1 56.8 reduce-scatter.42
  1098.1 26.4 reduce-scatter.34
where the time goes:
time: 1200 us; the launch traced here: 1190 us
  waiting for transfers between devices  731 us (61%)
  matrix products  154 us (13%)
  blocking collectives  144 us (12%)
  local copies, waits for them, and re-layouts  83.2 us (7%)
  other arithmetic  54.4 us (5%)
  between operations  20.6 us (2%)
    unnamed x32, waiting for transfers between devices  330 us
    psum x2, blocking collectives, on_device(): lax.psum((partial_value, jnp.sum(valid_rows)), ('dp', 'ctx', 'tensor'))  81.1 us
    unnamed x1, blocking collectives  63.1 us
    all_gather x2, waiting for transfers between devices, gather_grads(): return lax.all_gather(row_values, 'tensor', axis=0, tiled=True)  57.7 us
    all_gather x1, waiting for transfers between devices, on_device(): lax.all_gather(w_up, ('dp', 'ctx'), axis=0, tiled=True)  56.5 us
    reduce_scatter x2, waiting for transfers between devices, sum_grads(): lax.psum_scatter(term_rows.astype(jnp.bfloat16), 'tensor', scatter_dimens...  54.6 us
    all_gather x2, waiting for transfers between devices, gather_rows(): return lax.all_gather(row_values, 'tensor', axis=0, tiled=True)  49.4 us
    unnamed x78, local copies, waits for them, and re-layouts  47.4 us
  transfers between devices with their start and end apart: 24, of which 18 were waited for; matrix products, arithmetic and copies ran while one was open for 16% of the time, Pallas kernels for 0%

commit v1 on v0

v1 whole, which is shorter than its diff:
```python
import jax
import jax.numpy as jnp
from jax import lax
from jax.sharding import PartitionSpec as P

HD = 72
REAL = 729


EPSILON = 1e-06
GELU_C = 0.7978845608028654
GELU_K = 0.044715
BF = jnp.bfloat16
F32 = jnp.float32


def norm_forward(row_values, gain_vec, shift_vec):
    average = jnp.mean(row_values, axis=-1, keepdims=True)
    centred = row_values - average
    spread = jnp.mean(centred * centred, axis=-1, keepdims=True)
    inverse = lax.rsqrt(spread + EPSILON)
    unit_rows = centred * inverse
    return (unit_rows * gain_vec + shift_vec, unit_rows, inverse)


def norm_backward(upstream, unit_rows, inverse, gain_vec):
    scaled = upstream * gain_vec
    inner_sum = (
        scaled
        - jnp.mean(scaled, axis=-1, keepdims=True)
        - unit_rows * jnp.mean(scaled * unit_rows, axis=-1, keepdims=True)
    )
    return (inner_sum * inverse, jnp.sum(upstream * unit_rows, axis=0), jnp.sum(upstream, axis=0))


def gelu_tanh(values):
    return 0.5 * values * (1.0 + jnp.tanh(GELU_C * (values + GELU_K * values * values * values)))


def gelu_slope(values):
    tanh_part = jnp.tanh(GELU_C * (values + GELU_K * values * values * values))
    return 0.5 * (1.0 + tanh_part) + 0.5 * values * (1.0 - tanh_part * tanh_part) * GELU_C * (
        1.0 + 3.0 * GELU_K * values * values
    )


def swap(values, axis):
    return lax.ppermute(values, axis, [(0, 1), (1, 0)])


def tensor_gather(values):
    if lax.axis_size("tensor") == 2:
        return jnp.stack([values, swap(values, "tensor")])
    return lax.all_gather(values, "tensor", axis=0)


def tensor_reduce(partials):
    if lax.axis_size("tensor") == 2:
        return partials[0] + swap(partials[1].astype(BF), "tensor").astype(F32)
    return lax.psum_scatter(partials.astype(BF), "tensor", scatter_dimension=0).astype(F32)


def ctx_gather(values):
    if lax.axis_size("ctx") == 2:
        return jnp.concatenate([values, swap(values, "ctx")], axis=2)
    return lax.all_gather(values, "ctx", axis=2, tiled=True)


def ctx_reduce(values, half_len):
    if lax.axis_size("ctx") == 2:
        other = swap(values[:, :, half_len:].astype(BF), "ctx")
        return values[:, :, :half_len] + other.astype(F32)
    return lax.psum_scatter(
        values.astype(BF), "ctx", scatter_dimension=2, tiled=True
    ).astype(F32)


def key_positions(half_len):
    n_ctx = lax.axis_size("ctx")
    local = jnp.arange(half_len * n_ctx)
    if n_ctx == 2:
        me = lax.axis_index("ctx")
        block = jnp.where(local < half_len, me, 1 - me)
        return block * half_len + local % half_len
    return local


def tree_sum(values, axes):
    for axis in axes:
        size = lax.axis_size(axis)
        if size & (size - 1):
            values = jax.tree.map(lambda v: lax.psum(v, axis), values)
            continue
        step = 1
        while step < size:
            perm = [(i, i ^ step) for i in range(size)]
            values = jax.tree.map(lambda v: v + lax.ppermute(v, axis, perm), values)
            step *= 2
    return values


def on_device(
    tokens,
    teacher,
    valid_len,
    ln1_gain,
    ln1_bias,
    w_q,
    b_q,
    w_k,
    w_v,
    b_v,
    w_o,
    b_o,
    ln2_gain,
    ln2_bias,
    w_up,
    b_up,
    w_down,
    b_down,
):
    own_images, half_len, width = tokens.shape
    n_t = lax.axis_size("tensor")
    piece, head_width = w_q.shape
    local_heads = head_width // HD
    hidden_width = w_up.shape[1]
    rows = own_images * half_len
    images = n_t * own_images

    valid_count = tree_sum(jnp.sum(valid_len.astype(jnp.int32)), ("tensor", "dp")).astype(F32)

    vector_rows = jnp.stack([ln1_gain, ln1_bias, b_o, ln2_gain, ln2_bias, b_down], axis=1)
    vector_slot = jnp.pad(vector_rows, ((0, 0), (0, head_width - vector_rows.shape[1])))
    attn_pack = jnp.stack([w_q, w_k, w_v, w_o.T, vector_slot])
    attn_full = lax.all_gather(attn_pack, ("dp", "ctx"), axis=1, tiled=True)
    mlp_pack = jnp.stack([w_up, w_down.T])
    mlp_full = lax.all_gather(mlp_pack, ("dp", "ctx"), axis=1, tiled=True)
    query_w, key_w, value_w, out_wt = attn_full[0], attn_full[1], attn_full[2], attn_full[3]
    vectors = attn_full[4][:, :6].astype(F32)
    gain_one, shift_one, out_bias, gain_two, shift_two, down_bias = [
        vectors[:, i] for i in range(6)
    ]
    up_w, down_wt = mlp_full[0], mlp_full[1]

    query_per_head = query_w.reshape(width, local_heads, HD)
    key_per_head = key_w.reshape(width, local_heads, HD)
    value_per_head = value_w.reshape(width, local_heads, HD)
    out_per_head = out_wt.reshape(width, local_heads, HD)
    query_bias = b_q.astype(F32).reshape(1, local_heads, 1, HD)
    value_bias = b_v.astype(F32).reshape(1, local_heads, 1, HD)

    inputs = tokens.astype(F32).reshape(rows, width)
    normed, unit_one, inverse_one = norm_forward(inputs, gain_one, shift_one)
    normed_every_row = tensor_gather(normed.astype(BF)).reshape(images, half_len, width)
    queries = (
        jnp.einsum("pro,ojx->pjrx", normed_every_row, query_per_head, preferred_element_type=F32)
        + query_bias
    ).astype(BF)
    key_rows = jnp.einsum(
        "pro,ojx->pjrx", normed_every_row, key_per_head, preferred_element_type=F32
    ).astype(BF)
    value_rows = (
        jnp.einsum("pro,ojx->pjrx", normed_every_row, value_per_head, preferred_element_type=F32)
        + value_bias
    ).astype(BF)
    key_all = ctx_gather(key_rows)
    value_all = ctx_gather(value_rows)
    usable = key_positions(half_len) < REAL
    score_scale = HD ** (-0.5)

    raw_scores = jnp.einsum("bhqe,bhke->bhqk", queries, key_all, preferred_element_type=F32)
    scores = jnp.where(usable, raw_scores * score_scale, -1e30)
    summit = jnp.max(scores, axis=-1, keepdims=True)
    exp_total = jnp.sum(jnp.exp(scores - summit), axis=-1, keepdims=True)
    log_totals = summit + jnp.log(exp_total)
    soft_weights = jnp.exp(scores - log_totals).astype(BF)
    mixed_per_head = jnp.einsum(
        "bhqk,bhke->bhqe", soft_weights, value_all, preferred_element_type=F32
    ).astype(BF)

    attn_terms = jnp.einsum(
        "lscm,dsm->lcd", mixed_per_head, out_per_head, preferred_element_type=F32
    )
    attn_sum = tensor_reduce(attn_terms.reshape(n_t, rows, width))
    hidden = inputs + attn_sum + out_bias
    normed_two, unit_two, inverse_two = norm_forward(hidden, gain_two, shift_two)
    normed_two_all = tensor_gather(normed_two.astype(BF)).reshape(images * half_len, width)
    before = jnp.dot(normed_two_all, up_w, preferred_element_type=F32) + b_up.astype(F32)
    active = gelu_tanh(before).astype(BF)
    mlp_terms = jnp.einsum("rf,df->rd", active, down_wt, preferred_element_type=F32)
    result = hidden + tensor_reduce(mlp_terms.reshape(n_t, rows, width)) + down_bias
    layer_out = result.astype(BF).reshape(own_images, half_len, width)

    position = lax.axis_index("ctx") * half_len + jnp.arange(half_len)
    valid_rows = (position[None, :] < valid_len[:, None]).astype(F32).reshape(rows)
    error_rows = result - teacher.astype(F32).reshape(rows, width)
    partial_value = 0.5 * jnp.sum(valid_rows * jnp.mean(error_rows * error_rows, axis=-1))
    slot_total = own_images * lax.axis_size("dp") * n_t
    factor = slot_total * (half_len * lax.axis_size("ctx")) / valid_count
    grad_out = error_rows * (valid_rows[:, None] * factor)

    grad_rows = tensor_gather(grad_out.astype(BF)).reshape(images * half_len, width)
    down_grad_t = jnp.einsum("rd,rf->df", grad_rows, active, preferred_element_type=F32)
    active_grad = jnp.einsum("rd,df->rf", grad_rows, down_wt, preferred_element_type=F32)
    before_grad = (active_grad * gelu_slope(before)).astype(BF)
    up_bias_grad = jnp.sum(before_grad, axis=0, dtype=F32)
    up_grad = jnp.einsum("rd,rf->df", normed_two_all, before_grad, preferred_element_type=F32)
    mlp_grads = lax.psum_scatter(
        jnp.concatenate([up_grad, down_grad_t], axis=1).astype(BF),
        ("dp", "ctx"),
        scatter_dimension=0,
        tiled=True,
    )
    norm_two_terms = jnp.einsum("rf,df->rd", before_grad, up_w, preferred_element_type=F32)
    norm_two_grad = tensor_reduce(norm_two_terms.reshape(n_t, rows, width))
    hidden_back, gain_two_grad, shift_two_grad = norm_backward(
        norm_two_grad, unit_two, inverse_two, gain_two
    )
    hidden_grad = grad_out + hidden_back
    down_bias_grad = jnp.sum(grad_out, axis=0)
    out_bias_grad = jnp.sum(hidden_grad, axis=0)
    hidden_token_rows = tensor_gather(hidden_grad.astype(BF)).reshape(images, half_len, width)
    out_grad_t = jnp.einsum(
        "lcd,lscm->dsm", hidden_token_rows, mixed_per_head, preferred_element_type=F32
    ).reshape(width, head_width)
    mixed_grad = jnp.einsum(
        "lcd,dsm->lscm", hidden_token_rows, out_per_head, preferred_element_type=F32
    ).astype(BF)

    soft_full = jnp.exp(scores - log_totals)
    soft_grad = jnp.einsum("bhqe,bhke->bhqk", mixed_grad, value_all, preferred_element_type=F32)
    value_grads = jnp.einsum(
        "bhqk,bhqe->bhke", soft_full.astype(BF), mixed_grad, preferred_element_type=F32
    )
    inner_sum = jnp.sum(soft_full * soft_grad, axis=-1, keepdims=True)
    score_grad = (soft_full * (soft_grad - inner_sum)).astype(BF)
    query_grads = (
        jnp.einsum("bhqk,bhke->bhqe", score_grad, key_all, preferred_element_type=F32)
        * score_scale
    )
    key_grads = (
        jnp.einsum("bhqk,bhqe->bhke", score_grad, queries, preferred_element_type=F32)
        * score_scale
    )
    key_reduced_precision = ctx_reduce(key_grads, half_len).astype(BF)
    value_reduced_precision = ctx_reduce(value_grads, half_len).astype(BF)
    query_reduced_precision = query_grads.astype(BF)
    query_bias_grad = jnp.sum(query_reduced_precision, axis=(0, 2), dtype=F32).reshape(head_width)
    value_bias_grad = jnp.sum(value_reduced_precision, axis=(0, 2), dtype=F32).reshape(head_width)
    query_weight_grad = jnp.einsum(
        "okz,oaks->zas", normed_every_row, query_reduced_precision, preferred_element_type=F32
    ).reshape(width, head_width)
    key_weight_grad = jnp.einsum(
        "okz,oaks->zas", normed_every_row, key_reduced_precision, preferred_element_type=F32
    ).reshape(width, head_width)
    value_weight_grad = jnp.einsum(
        "okz,oaks->zas", normed_every_row, value_reduced_precision, preferred_element_type=F32
    ).reshape(width, head_width)
    attn_grads = lax.psum_scatter(
        jnp.concatenate(
            [query_weight_grad, key_weight_grad, value_weight_grad, out_grad_t], axis=1
        ).astype(BF),
        ("dp", "ctx"),
        scatter_dimension=0,
        tiled=True,
    )
    norm_one_terms = jnp.einsum(
        "tivw,niw->tvn", query_reduced_precision, query_per_head, preferred_element_type=F32
    )
    norm_one_terms = norm_one_terms + jnp.einsum(
        "tivw,niw->tvn", key_reduced_precision, key_per_head, preferred_element_type=F32
    )
    norm_one_terms = norm_one_terms + jnp.einsum(
        "tivw,niw->tvn", value_reduced_precision, value_per_head, preferred_element_type=F32
    )
    norm_one_grad = tensor_reduce(norm_one_terms.reshape(n_t, rows, width))
    input_back, gain_one_grad, shift_one_grad = norm_backward(
        norm_one_grad, unit_one, inverse_one, gain_one
    )
    tokens_grad = (hidden_grad + input_back).reshape(own_images, half_len, width)

    row_sums = jnp.concatenate(
        [
            gain_one_grad,
            shift_one_grad,
            out_bias_grad,
            gain_two_grad,
            shift_two_grad,
            down_bias_grad,
            partial_value.reshape(1),
        ]
    )
    head_sums = jnp.concatenate([query_bias_grad, value_bias_grad, up_bias_grad])
    row_sums, head_sums = tree_sum((row_sums, head_sums), ("ctx", "dp"))
    row_sums = tree_sum(row_sums, ("tensor",))
    loss_value = row_sums[6 * width] / valid_count
    piece_start = lax.axis_index(("dp", "ctx")) * piece
    vector_shards = [
        lax.dynamic_slice_in_dim(row_sums, i * width + piece_start, piece) for i in range(6)
    ]
    query_bias_sum = head_sums[:head_width]
    value_bias_sum = head_sums[head_width : 2 * head_width]
    up_bias_sum = head_sums[2 * head_width :]
    attn_grads = attn_grads.astype(F32).reshape(piece, 4, head_width)
    mlp_grads = mlp_grads.astype(F32)
    attn_grads = [attn_grads[:, i] for i in range(4)]
    mlp_grads = [mlp_grads[:, :hidden_width], mlp_grads[:, hidden_width:]]
    return (
        layer_out,
        loss_value,
        tokens_grad,
        vector_shards[0],
        vector_shards[1],
        attn_grads[0],
        query_bias_sum,
        attn_grads[1],
        attn_grads[2],
        value_bias_sum,
        attn_grads[3].T,
        vector_shards[2],
        vector_shards[3],
        vector_shards[4],
        mlp_grads[0],
        up_bias_sum,
        mlp_grads[1].T,
        vector_shards[5],
    )


def solution(mesh):
    return jax.shard_map(
        on_device,
        mesh=mesh,
        in_specs=(
            P(("dp", "tensor"), "ctx", None),
            P(("dp", "tensor"), "ctx", None),
            P(("dp", "tensor")),
            P(("dp", "ctx")),
            P(("dp", "ctx")),
            P(("dp", "ctx"), "tensor"),
            P("tensor"),
            P(("dp", "ctx"), "tensor"),
            P(("dp", "ctx"), "tensor"),
            P("tensor"),
            P("tensor", ("dp", "ctx")),
            P(("dp", "ctx")),
            P(("dp", "ctx")),
            P(("dp", "ctx")),
            P(("dp", "ctx"), "tensor"),
            P("tensor"),
            P("tensor", ("dp", "ctx")),
            P(("dp", "ctx")),
        ),
        out_specs=(
            P(("dp", "tensor"), "ctx", None),
            P(),
            P(("dp", "tensor"), "ctx", None),
            P(("dp", "ctx")),
            P(("dp", "ctx")),
            P(("dp", "ctx"), "tensor"),
            P("tensor"),
            P(("dp", "ctx"), "tensor"),
            P(("dp", "ctx"), "tensor"),
            P("tensor"),
            P("tensor", ("dp", "ctx")),
            P(("dp", "ctx")),
            P(("dp", "ctx")),
            P(("dp", "ctx")),
            P(("dp", "ctx"), "tensor"),
            P("tensor"),
            P("tensor", ("dp", "ctx")),
            P(("dp", "ctx")),
        ),
        check_vma=False,
    )
```

time: 1200 us -> 620 us (0.52)
  waiting for transfers between devices: 731 us -> 294 us
  blocking collectives: 144 us -> 0 us
  starting transfers between devices: 2.87 us -> 32.4 us
  matrix products: 154 us -> 125 us
    unnamed x32 -> x5, waiting for transfers between devices: 330 us -> 80.7 us
    all_gather x12 -> x2, waiting for transfers between devices: 318 us -> 69.1 us  [the longest x1 69.1 us: on_device(): attn_full = lax.all_gather(attn_pack, ('dp', 'ctx'), axis=1, tiled=True)]
    ppermute x0 -> x25, waiting for transfers between devices: none -> 144 us  [the longest x12 111 us: swap(): return lax.ppermute(values, axis, [(0, 1), (1, 0)])]
    reduce_scatter x4 -> x1, waiting for transfers between devices: 83.2 us -> 0.01 us  [on_device(): lax.psum_scatter(jnp.concatenate([query_weight_grad, key_weight_grad, val...]
    psum x2 -> x0, blocking collectives: 81.1 us -> none  [on_device(): lax.psum((partial_value, jnp.sum(valid_rows)), ('dp', 'ctx', 'tensor'))]
    unnamed x1 -> x0, blocking collectives: 63.1 us -> none
    ppermute x0 -> x25, starting transfers between devices: none -> 31.8 us  [the longest x13 18.8 us: tree_sum(): values = jax.tree.map(lambda v: v + lax.ppermute(v, axis, perm), values)]
    slice x0 -> x15, local copies, waits for them, and re-layouts: none -> 24 us  [the longest x2 7.98 us: on_device(): attn_full[3]]
  transfers between devices with their start and end apart: 24 -> 29, of which waited for: 18 -> 18; matrix products, arithmetic and copies ran while one was open for 16% -> 29% of each run, Pallas kernels for 0% -> 0%
where the time goes in v1:
time: 620 us; the launch traced here: 615 us
  waiting for transfers between devices  294 us (47%)
  matrix products  125 us (20%)
  local copies, waits for them, and re-layouts  85.5 us (14%)
  other arithmetic  57.2 us (9%)
  starting transfers between devices  32.4 us (5%)
  between operations  20.7 us (3%)
    ppermute x12, waiting for transfers between devices, swap(): return lax.ppermute(values, axis, [(0, 1), (1, 0)])  111 us
    unnamed x5, waiting for transfers between devices  80.7 us
    all_gather x1, waiting for transfers between devices, on_device(): attn_full = lax.all_gather(attn_pack, ('dp', 'ctx'), axis=1, tiled=True)  69.1 us
    unnamed x154, local copies, waits for them, and re-layouts  35.7 us
    ppermute x13, waiting for transfers between devices, tree_sum(): values = jax.tree.map(lambda v: v + lax.ppermute(v, axis, perm), values)  32.8 us
    ppermute x13, starting transfers between devices, tree_sum(): values = jax.tree.map(lambda v: v + lax.ppermute(v, axis, perm), values)  18.8 us
    concatenate x1, other arithmetic, on_device(): jnp.concatenate([up_grad, down_grad_t], axis=1).astype(BF)  14.5 us
    dot_general x1, matrix products, on_device(): jnp.einsum('bhqe,bhke->bhqk', mixed_grad, value_all, preferred_element_ty...  13.6 us
  transfers between devices with their start and end apart: 29, of which 18 were waited for; matrix products, arithmetic and copies ran while one was open for 29% of the time, Pallas kernels for 0%

profile of v1, /device:TPU:0, one launch (start us, length us, event | category | flops | bytes accessed | tf_op | source)
XLA Modules:
  0.0 615.0 jit_solution(10146939695829817996)
XLA Ops:
  14.5 69.1 %all-gather.3.cloned.1.call-done = bf16[5,1152,576]{2,1,0:T(8,128)(2,1)} async-done(((bf16[5,72,576]{2,1,0:T(8,128)(2,1)}), bf16[5,1152,576]{2,1,0:T(8,128)(2,1)}) %all-gather.3.cloned.1.call-update) | async-done | bytes 6635536 | tf_op jit(solution)/shard_map/all_gather | solution.py:135
  97.1 16.3 %collective-permute-done = bf16[368,1152]{1,0:T(8,128)(2,1)} collective-permute-done((bf16[368,1152]{1,0:T(8,128)(2,1)}, bf16[368,1152]{1,0:T(8,128)(2,1)}, u32[]{:S(2)}, u32[]{:S(2)}) %collective-permute-start) | collective-permute-done | bytes 847904 | tf_op jit(solution)/shard_map/ppermute | solution.py:48
  130.9 5.8 fusion
  143.3 6.2 %fusion.66 = bf16[2,8,368,72]{2,3,1,0:T(8,128)(2,1)} fusion(f32[2,8,368,736]{3,2,1,0:T(8,128)S(1)} %get-tuple-element.132, f32[2,8,368]{2,1,0:T(8,128)S(1)} %log_add_fusion, pred[736]{0:T(1024)(128)(4,1)S(1)} %fusion.103, bf16[2,8,368,72]{2,3,0,1:T(8,128)(2,1)S(1)} %collective-permute-done.2, bf16[2,8,368,72]{2,3,0,1:T(8,128)(2,1)S(1)} %fusion.90), kind=kOutput, calls=%fused_computation.128 | convolution fusion | flops 645183488 | bytes 19902176 | tf_op jit(solution)/shard_map/bhqk,bhke->bhqe/dot_general | solution.py:177
  154.0 19.6 %collective-permute-done.3 = bf16[368,1152]{1,0:T(8,128)(2,1)S(1)} collective-permute-done((bf16[368,1152]{1,0:T(8,128)(2,1)S(1)}, bf16[368,1152]{1,0:T(8,128)(2,1)S(1)}, u32[]{:S(2)}, u32[]{:S(2)}) %collective-permute-start.3) | collective-permute-done | bytes 847904 | tf_op jit(solution)/shard_map/ppermute | solution.py:48
  176.7 18.3 %collective-permute-done.4 = bf16[368,1152]{1,0:T(8,128)(2,1)S(1)} collective-permute-done((bf16[368,1152]{1,0:T(8,128)(2,1)S(1)}, bf16[368,1152]{1,0:T(8,128)(2,1)S(1)}, u32[]{:S(2)}, u32[]{:S(2)}) %collective-permute-start.4) | collective-permute-done | bytes 847904 | tf_op jit(solution)/shard_map/ppermute | solution.py:48
  196.4 7.6 %fusion.10 = f32[736,2152]{1,0:T(8,128)S(1)} fusion(bf16[736,1152]{1,0:T(8,128)(2,1)} %bitcast.289, bf16[2,1152,2152]{2,1,0:T(8,128)(2,1)} %all-gather.5.cloned.1.call-done), kind=kOutput, calls=%fused_computation.24 | convolution fusion | flops 3649241088 | bytes 13044736 | tf_op jit(solution)/shard_map/dot_general | solution.py:188
  204.0 5.8 fusion.11
  214.4 16.7 %collective-permute-done.6 = s32[]{:T(128)} collective-permute-done((s32[]{:T(128)}, s32[]{:T(128)}, u32[]{:S(2)}, u32[]{:S(2)}) %collective-permute-start.6) | collective-permute-done | bytes 36 | tf_op jit(solution)/shard_map/ppermute | solution.py:97
  250.7 14.0 %collective-permute-done.10 = bf16[368,1152]{1,0:T(8,128)(2,1)S(1)} collective-permute-done((bf16[368,1152]{1,0:T(8,128)(2,1)S(1)}, bf16[368,1152]{1,0:T(8,128)(2,1)S(1)}, u32[]{:S(2)}, u32[]{:S(2)}) %collective-permute-start.10) | collective-permute-done | bytes 847904 | tf_op jit(solution)/shard_map/ppermute | solution.py:48
  264.9 10.9 %convert_reduce_fusion = (f32[2152]{0:T(1024)}, bf16[736,2152]{1,0:T(8,128)(2,1)S(1)}) fusion(f32[736,2152]{1,0:T(8,128)} %copy-done.59, f32[2152]{0:T(1024)S(1)} %convert_element_type.150, bf16[736,1152]{1,0:T(8,128)(2,1)S(1)} %bitcast.291, bf16[2,1152,2152]{2,1,0:T(8,128)(2,1)S(1)} %copy-done.56), kind=kOutput, calls=%fused_computation.19 | convolution fusion | flops 3684084224 | bytes 16233376 | tf_op jit(solution)/shard_map/rd,df->rf/dot_general | solution.py:204
  275.8 8.2 %fusion.9 = f32[736,1152]{1,0:T(8,128)S(1)} fusion(bf16[736,2152]{1,0:T(8,128)(2,1)S(1)} %get-tuple-element.138, bf16[2,1152,2152]{2,1,0:T(8,128)(2,1)} %all-gather.5.cloned.1.call-done), kind=kOutput, calls=%fused_computation.23 | convolution fusion | flops 3649241088 | bytes 11572736 | tf_op jit(solution)/shard_map/rf,df->rd/dot_general | solution.py:214
  285.8 13.1 %collective-permute-done.11 = bf16[368,1152]{1,0:T(8,128)(2,1)S(1)} collective-permute-done((bf16[368,1152]{1,0:T(8,128)(2,1)S(1)}, bf16[368,1152]{1,0:T(8,128)(2,1)S(1)}, u32[]{:S(2)}, u32[]{:S(2)}) %collective-permute-start.11) | collective-permute-done | bytes 847904 | tf_op jit(solution)/shard_map/ppermute | solution.py:48
  306.0 12.1 %collective-permute-done.12 = bf16[368,1152]{1,0:T(8,128)(2,1)S(1)} collective-permute-done((bf16[368,1152]{1,0:T(8,128)(2,1)S(1)}, bf16[368,1152]{1,0:T(8,128)(2,1)S(1)}, u32[]{:S(2)}, u32[]{:S(2)}) %collective-permute-start.12) | collective-permute-done | bytes 847904 | tf_op jit(solution)/shard_map/ppermute | solution.py:48
  321.4 5.9 fusion.95
  330.1 13.6 %multiply_reduce_fusion = (f32[2,8,368]{2,1,0:T(8,128)S(1)}, f32[2,8,368,736]{3,2,1,0:T(8,128)}) fusion(f32[2,8,368,736]{3,2,1,0:T(8,128)} %copy-done, f32[2,8,368]{2,1,0:T(8,128)S(1)} %log_add_fusion, pred[736]{0:T(1024)(128)(4,1)S(1)} %fusion.103, bf16[2,8,368,72]{2,3,0,1:T(8,128)(2,1)} %fusion.81, bf16[2,8,368,72]{2,3,0,1:T(8,128)(2,1)S(1)} %copy-done.25, ...), kind=kOutput, calls=%fused_computation.1 | convolution fusion | flops 649087232 | bytes 37260000 | tf_op jit(solution)/shard_map/bhqe,bhke->bhqk/dot_general | solution.py:231
  343.7 12.9 %multiply_convert_fusion = bf16[2,8,368,736]{3,2,1,0:T(8,128)(2,1)S(1)} fusion(f32[2,8,368,736]{3,2,1,0:T(8,128)} %get-tuple-element.134, f32[2,8,368,736]{3,2,1,0:T(8,128)} %copy-done, f32[2,8,368]{2,1,0:T(8,128)S(1)} %get-tuple-element.133, f32[2,8,368]{2,1,0:T(8,128)S(1)} %log_add_fusion, pred[736]{0:T(1024)(128)(4,1)S(1)} %fusion.103), kind=kLoop, calls=%fused_computation | loop fusion | flops 26001408 | bytes 43383520 | tf_op jit(solution)/shard_map/convert_element_type | solution.py:236
  395.5 9.9 %concatenate.23 = bf16[1152,2304]{1,0:T(8,128)(2,1)} concatenate(bf16[1152,576]{1,0:T(8,128)(2,1)} %copy.124, bf16[1152,576]{1,0:T(8,128)(2,1)} %copy.125, bf16[1152,576]{1,0:T(8,128)(2,1)} %copy.126, bf16[1152,576]{1,0:T(8,128)(2,1)S(1)} %copy.127), dimensions={1} | concatenate | bytes 10616832 | tf_op jit(solution)/shard_map/concatenate | solution.py:260
  406.8 6.6 %convolution_convert_fusion.1 = bf16[1152,2152]{0,1:T(8,128)(2,1)S(1)} fusion(bf16[736,1152]{1,0:T(8,128)(2,1)S(1)} %bitcast.290, bf16[736,2152]{1,0:T(8,128)(2,1)} %copy-done.60), kind=kOutput, calls=%fused_computation.7 | convolution fusion | flops 3651720192 | bytes 9821696 | tf_op jit(solution)/shard_map/rd,rf->df/dot_general | solution.py:207
  413.4 8.6 %convolution_convert_fusion = bf16[1152,2152]{0,1:T(8,128)(2,1)S(1)} fusion(bf16[736,1152]{1,0:T(8,128)(2,1)S(1)} %bitcast.292, f32[736,2152]{1,0:T(8,128)} %copy-done.59, f32[2152]{0:T(1024)S(1)} %copy-done.43), kind=kOutput, calls=%fused_computation.6 | convolution fusion | flops 3667558912 | bytes 12998048 | tf_op jit(solution)/shard_map/rd,rf->df/dot_general | solution.py:203
  422.0 14.5 %pad_maximum_fusion = bf16[1152,4304]{0,1:T(8,128)(2,1)} fusion(bf16[1152,2152]{0,1:T(8,128)(2,1)S(1)} %convolution_convert_fusion, bf16[1152,2152]{0,1:T(8,128)(2,1)S(1)} %convolution_convert_fusion.1), kind=kLoop, calls=%fused_computation.8 | loop fusion | flops 19832832 | bytes 19832832 | tf_op jit(solution)/shard_map/concatenate | solution.py:209
  436.5 14.1 %copy.142 = bf16[1152,4304]{1,0:T(8,128)(2,1)} copy(bf16[1152,4304]{0,1:T(8,128)(2,1)} %pad_maximum_fusion) | data formatting | bytes 19832832
  466.2 17.7 %collective-permute-done.15 = bf16[368,1152]{1,0:T(8,128)(2,1)S(1)} collective-permute-done((bf16[368,1152]{1,0:T(8,128)(2,1)}, bf16[368,1152]{1,0:T(8,128)(2,1)S(1)}, u32[]{:S(2)}, u32[]{:S(2)}) %collective-permute-start.15) | collective-permute-done | bytes 847904 | tf_op jit(solution)/shard_map/ppermute | solution.py:48
  519.3 80.6 %reduce-scatter.7.cloned.1.call-done = bf16[72,4304]{1,0:T(8,128)(2,1)} async-done(((bf16[1152,4304]{1,0:T(8,128)(2,1)}), bf16[72,4304]{1,0:T(8,128)(2,1)}) %reduce-scatter.7.cloned.1.call-update) | async-done | bytes 619792
  (298 shorter events, 186.2 us)
Async XLA Ops:
  7.3 76.4 %all-gather.3.cloned.1.call-start = ((), (), s32[]{:S(2)}) async-start(), calls=%async_computation.2 | async-start | bytes 7833600 | tf_op jit(solution)/shard_map/all_gather | solution.py:135
  12.9 183.5 %all-gather.5.cloned.1.call-start = ((), (), s32[]{:S(2)}) async-start(), calls=%async_computation.3 | async-start | bytes 10653696 | tf_op jit(solution)/shard_map/all_gather | solution.py:137
  13.9 500.6 %reduce-scatter.5.cloned.1.call-start = ((), (), s32[]{:S(2)}) async-start(), calls=%async_computation.4 | async-start | bytes 5640192 | tf_op jit(solution)/shard_map/reduce_scatter | solution.py:259
  92.1 21.3 %collective-permute-start = (bf16[368,1152]{1,0:T(8,128)(2,1)}, bf16[368,1152]{1,0:T(8,128)(2,1)}, u32[]{:S(2)}, u32[]{:S(2)}) collective-permute-start(bf16[368,1152]{1,0:T(8,128)(2,1)} %fusion.29), channel_id=1, source_target_pairs={{0,1},{1,0},{2,3},{3,2},{4,5},{5,4},{6,7},{7,6},{8,9},{9,8},{10,11... | collective-permute-start | bytes 2543624 | tf_op jit(solution)/shard_map/ppermute | solution.py:48
  117.3 13.6 %collective-permute-start.1 = (bf16[2,8,368,72]{2,3,0,1:T(8,128)(2,1)}, bf16[2,8,368,72]{2,3,0,1:T(8,128)(2,1)}, u32[]{:S(2)}, u32[]{:S(2)}) collective-permute-start(bf16[2,8,368,72]{2,3,0,1:T(8,128)(2,1)} %fusion.84), channel_id=1, source_target_pairs={{0,2},{2,0},{1,3},{3,1},{4,6},{6,4},{5,7},{7,5},{8,10},{10,8},{9,1... | collective-permute-start | bytes 2543624 | tf_op jit(solution)/shard_map/ppermute | solution.py:48
  127.5 14.0 %collective-permute-start.2 = (bf16[2,8,368,72]{2,3,0,1:T(8,128)(2,1)S(1)}, bf16[2,8,368,72]{2,3,0,1:T(8,128)(2,1)S(1)}, u32[]{:S(2)}, u32[]{:S(2)}) collective-permute-start(bf16[2,8,368,72]{2,3,0,1:T(8,128)(2,1)S(1)} %fusion.90), channel_id=1, source_target_pairs={{0,2},{2,0},{1,3},{3,1},{4,6},{6,4},{5,7},{7,5},{8,10},{10,8},{9,1... | collective-permute-start | bytes 2543624 | tf_op jit(solution)/shard_map/ppermute | solution.py:48
  152.5 21.1 %collective-permute-start.3 = (bf16[368,1152]{1,0:T(8,128)(2,1)S(1)}, bf16[368,1152]{1,0:T(8,128)(2,1)S(1)}, u32[]{:S(2)}, u32[]{:S(2)}) collective-permute-start(bf16[368,1152]{1,0:T(8,128)(2,1)S(1)} %fusion.93), channel_id=1, source_target_pairs={{0,1},{1,0},{2,3},{3,2},{4,5},{5,4},{6,7},{7,6},{8,9},{9,8},{10,11... | collective-permute-start | bytes 2543624 | tf_op jit(solution)/shard_map/ppermute | solution.py:48
  174.8 20.3 %collective-permute-start.4 = (bf16[368,1152]{1,0:T(8,128)(2,1)S(1)}, bf16[368,1152]{1,0:T(8,128)(2,1)S(1)}, u32[]{:S(2)}, u32[]{:S(2)}) collective-permute-start(bf16[368,1152]{1,0:T(8,128)(2,1)S(1)} %add_convert_fusion.2), channel_id=1, source_target_pairs={{0,1},{1,0},{2,3},{3,2},{4,5},{5,4},{6,7},{7,6},{8,9},{9,8},{10,11... | collective-permute-start | bytes 2543624 | tf_op jit(solution)/shard_map/ppermute | solution.py:48
  211.7 34.1 %collective-permute-start.5 = (bf16[368,1152]{1,0:T(8,128)(2,1)S(1)}, bf16[368,1152]{1,0:T(8,128)(2,1)}, u32[]{:S(2)}, u32[]{:S(2)}) collective-permute-start(bf16[368,1152]{1,0:T(8,128)(2,1)S(1)} %slice.260), channel_id=1, source_target_pairs={{0,1},{1,0},{2,3},{3,2},{4,5},{5,4},{6,7},{7,6},{8,9},{9,8},{10,11... | collective-permute-start | bytes 2543624 | tf_op jit(solution)/shard_map/ppermute | solution.py:48
  213.2 17.9 %collective-permute-start.6 = (s32[]{:T(128)}, s32[]{:T(128)}, u32[]{:S(2)}, u32[]{:S(2)}) collective-permute-start(s32[]{:T(128)} %bitcast.46), channel_id=1, source_target_pairs={{0,1},{1,0},{2,3},{3,2},{4,5},{5,4},{6,7},{7,6},{8,9},{9,8},{10,11... | collective-permute-start | bytes 20 | tf_op jit(solution)/shard_map/ppermute | solution.py:97
  240.6 4.5 collective-permute-start.9
  249.1 15.6 %collective-permute-start.10 = (bf16[368,1152]{1,0:T(8,128)(2,1)S(1)}, bf16[368,1152]{1,0:T(8,128)(2,1)S(1)}, u32[]{:S(2)}, u32[]{:S(2)}) collective-permute-start(bf16[368,1152]{1,0:T(8,128)(2,1)S(1)} %multiply_convert_fusion.3), channel_id=1, source_target_pairs={{0,1},{1,0},{2,3},{3,2},{4,5},{5,4},{6,7},{7,6},{8,9},{9,8},{10,11... | collective-permute-start | bytes 2543624 | tf_op jit(solution)/shard_map/ppermute | solution.py:48
  284.2 14.7 %collective-permute-start.11 = (bf16[368,1152]{1,0:T(8,128)(2,1)S(1)}, bf16[368,1152]{1,0:T(8,128)(2,1)S(1)}, u32[]{:S(2)}, u32[]{:S(2)}) collective-permute-start(bf16[368,1152]{1,0:T(8,128)(2,1)S(1)} %slice.259), channel_id=1, source_target_pairs={{0,1},{1,0},{2,3},{3,2},{4,5},{5,4},{6,7},{7,6},{8,9},{9,8},{10,11... | collective-permute-start | bytes 2543624 | tf_op jit(solution)/shard_map/ppermute | solution.py:48
  304.3 13.8 %collective-permute-start.12 = (bf16[368,1152]{1,0:T(8,128)(2,1)S(1)}, bf16[368,1152]{1,0:T(8,128)(2,1)S(1)}, u32[]{:S(2)}, u32[]{:S(2)}) collective-permute-start(bf16[368,1152]{1,0:T(8,128)(2,1)S(1)} %convert_element_type.158), channel_id=1, source_target_pairs={{0,1},{1,0},{2,3},{3,2},{4,5},{5,4},{6,7},{7,6},{8,9},{9,8},{10,11... | collective-permute-start | bytes 2543624 | tf_op jit(solution)/shard_map/ppermute | solution.py:48
  328.6 51.7 %collective-permute-start.14 = (bf16[2,8,368,72]{2,3,1,0:T(8,128)(2,1)}, bf16[2,8,368,72]{2,3,1,0:T(8,128)(2,1)}, u32[]{:S(2)}, u32[]{:S(2)}) collective-permute-start(bf16[2,8,368,72]{2,3,1,0:T(8,128)(2,1)} %slice.257), channel_id=1, source_target_pairs={{0,2},{2,0},{1,3},{3,1},{4,6},{6,4},{5,7},{7,5},{8,10},{10,8},{9,1... | collective-permute-start | bytes 2543624 | tf_op jit(solution)/shard_map/ppermute | solution.py:48
  362.9 25.6 %collective-permute-start.13 = (bf16[2,8,368,72]{2,3,1,0:T(8,128)(2,1)}, bf16[2,8,368,72]{2,3,1,0:T(8,128)(2,1)}, u32[]{:S(2)}, u32[]{:S(2)}) collective-permute-start(bf16[2,8,368,72]{2,3,1,0:T(8,128)(2,1)} %slice.258), channel_id=1, source_target_pairs={{0,2},{2,0},{1,3},{3,1},{4,6},{6,4},{5,7},{7,5},{8,10},{10,8},{9,1... | collective-permute-start | bytes 2543624 | tf_op jit(solution)/shard_map/ppermute | solution.py:48
  405.4 194.6 %reduce-scatter.7.cloned.1.call-start = ((), (), s32[]{:S(2)}) async-start(), calls=%async_computation.5 | async-start | bytes 10653696
  462.4 21.4 %collective-permute-start.15 = (bf16[368,1152]{1,0:T(8,128)(2,1)}, bf16[368,1152]{1,0:T(8,128)(2,1)S(1)}, u32[]{:S(2)}, u32[]{:S(2)}) collective-permute-start(bf16[368,1152]{1,0:T(8,128)(2,1)} %fusion.94), channel_id=1, source_target_pairs={{0,1},{1,0},{2,3},{3,2},{4,5},{5,4},{6,7},{7,6},{8,9},{9,8},{10,11... | collective-permute-start | bytes 2543624 | tf_op jit(solution)/shard_map/ppermute | solution.py:48
  465.7 20.8 %collective-permute-start.22 = (f32[3304]{0:T(1024)S(1)}, f32[3304]{0:T(1024)S(1)}, u32[]{:S(2)}, u32[]{:S(2)}) collective-permute-start(f32[3304]{0:T(1024)S(1)} %add.312), channel_id=1, source_target_pairs={{0,4},{4,0},{8,12},{12,8},{16,20},{20,16},{24,28},{28,24},{1,5},{5... | collective-permute-start | bytes 39656 | tf_op jit(solution)/shard_map/ppermute | solution.py:97
  486.4 8.6 %collective-permute-start.16 = (f32[6913]{0:T(1024)S(1)}, f32[6913]{0:T(1024)S(1)}, u32[]{:S(2)}, u32[]{:S(2)}) collective-permute-start(f32[6913]{0:T(1024)S(1)} %constant_dynamic-update-slice_fusion.1), channel_id=1, source_target_pairs={{0,2},{2,0},{1,3},{3,1},{4,6},{6,4},{5,7},{7,5},{8,10},{10,8},{9,1... | collective-permute-start | bytes 82964 | tf_op jit(solution)/shard_map/ppermute | solution.py:97
  490.3 4.6 collective-permute-start.24
  498.9 4.2 collective-permute-start.18
  503.1 4.8 collective-permute-start.19
  507.8 4.9 collective-permute-start.20
  (71 other events, 1028.3 us)
Sparse Core Ops, SparseCore 0:
  13.0 70.5 all-gather.2
  86.4 83.3 all-gather.4
  405.5 77.1 reduce-scatter.4
  486.7 113.2 reduce-scatter.6

commit v2 on v1

--- a/solution.py
+++ b/solution.py
@@ -128,41 +128,38 @@
     images = n_t * own_images
 
     valid_count = tree_sum(jnp.sum(valid_len.astype(jnp.int32)), ("tensor", "dp")).astype(F32)
-
+    valid_count, tokens = lax.optimization_barrier((valid_count, tokens))
+
+    pad_hidden = (-hidden_width) % 128
+    pad_out = (-head_width) % 128
     vector_rows = jnp.stack([ln1_gain, ln1_bias, b_o, ln2_gain, ln2_bias, b_down], axis=1)
     vector_slot = jnp.pad(vector_rows, ((0, 0), (0, head_width - vector_rows.shape[1])))
     attn_pack = jnp.stack([w_q, w_k, w_v, w_o.T, vector_slot])
     attn_full = lax.all_gather(attn_pack, ("dp", "ctx"), axis=1, tiled=True)
-    mlp_pack = jnp.stack([w_up, w_down.T])
+    mlp_pack = jnp.pad(jnp.stack([w_up, w_down.T]), ((0, 0), (0, 0), (0, pad_hidden)))
     mlp_full = lax.all_gather(mlp_pack, ("dp", "ctx"), axis=1, tiled=True)
-    query_w, key_w, value_w, out_wt = attn_full[0], attn_full[1], attn_full[2], attn_full[3]
+    qkv_w = attn_full[:3].reshape(3, width, local_heads, HD)
+    out_wt = attn_full[3]
     vectors = attn_full[4][:, :6].astype(F32)
     gain_one, shift_one, out_bias, gain_two, shift_two, down_bias = [
         vectors[:, i] for i in range(6)
     ]
     up_w, down_wt = mlp_full[0], mlp_full[1]
-
-    query_per_head = query_w.reshape(width, local_heads, HD)
-    key_per_head = key_w.reshape(width, local_heads, HD)
-    value_per_head = value_w.reshape(width, local_heads, HD)
+    up_b = jnp.pad(b_up.astype(F32), (0, pad_hidden))
+
     out_per_head = out_wt.reshape(width, local_heads, HD)
-    query_bias = b_q.astype(F32).reshape(1, local_heads, 1, HD)
-    value_bias = b_v.astype(F32).reshape(1, local_heads, 1, HD)
+    qkv_bias = jnp.stack(
+        [b_q.astype(F32), jnp.zeros((head_width,), F32), b_v.astype(F32)]
+    ).reshape(3, 1, local_heads, 1, HD)
 
     inputs = tokens.astype(F32).reshape(rows, width)
     normed, unit_one, inverse_one = norm_forward(inputs, gain_one, shift_one)
     normed_every_row = tensor_gather(normed.astype(BF)).reshape(images, half_len, width)
-    queries = (
-        jnp.einsum("pro,ojx->pjrx", normed_every_row, query_per_head, preferred_element_type=F32)
-        + query_bias
+    qkv_rows = (
+        jnp.einsum("pro,tojx->tpjrx", normed_every_row, qkv_w, preferred_element_type=F32)
+        + qkv_bias
     ).astype(BF)
-    key_rows = jnp.einsum(
-        "pro,ojx->pjrx", normed_every_row, key_per_head, preferred_element_type=F32
-    ).astype(BF)
-    value_rows = (
-        jnp.einsum("pro,ojx->pjrx", normed_every_row, value_per_head, preferred_element_type=F32)
-        + value_bias
-    ).astype(BF)
+    queries, key_rows, value_rows = qkv_rows[0], qkv_rows[1], qkv_rows[2]
     key_all = ctx_gather(key_rows)
     value_all = ctx_gather(value_rows)
     usable = key_positions(half_len) < REAL
@@ -185,7 +182,7 @@
     hidden = inputs + attn_sum + out_bias
     normed_two, unit_two, inverse_two = norm_forward(hidden, gain_two, shift_two)
     normed_two_all = tensor_gather(normed_two.astype(BF)).reshape(images * half_len, width)
-    before = jnp.dot(normed_two_all, up_w, preferred_element_type=F32) + b_up.astype(F32)
+    before = jnp.dot(normed_two_all, up_w, preferred_element_type=F32) + up_b
     active = gelu_tanh(before).astype(BF)
     mlp_terms = jnp.einsum("rf,df->rd", active, down_wt, preferred_element_type=F32)
     result = hidden + tensor_reduce(mlp_terms.reshape(n_t, rows, width)) + down_bias
@@ -203,20 +200,17 @@
     down_grad_t = jnp.einsum("rd,rf->df", grad_rows, active, preferred_element_type=F32)
     active_grad = jnp.einsum("rd,df->rf", grad_rows, down_wt, preferred_element_type=F32)
     before_grad = (active_grad * gelu_slope(before)).astype(BF)
-    up_bias_grad = jnp.sum(before_grad, axis=0, dtype=F32)
+    up_bias_grad = jnp.sum(before_grad[:, :hidden_width], axis=0, dtype=F32)
     up_grad = jnp.einsum("rd,rf->df", normed_two_all, before_grad, preferred_element_type=F32)
-    mlp_grads = lax.psum_scatter(
-        jnp.concatenate([up_grad, down_grad_t], axis=1).astype(BF),
-        ("dp", "ctx"),
-        scatter_dimension=0,
-        tiled=True,
-    )
+    mlp_grad_pack = jnp.concatenate([up_grad.astype(BF), down_grad_t.astype(BF)], axis=1)
     norm_two_terms = jnp.einsum("rf,df->rd", before_grad, up_w, preferred_element_type=F32)
     norm_two_grad = tensor_reduce(norm_two_terms.reshape(n_t, rows, width))
     hidden_back, gain_two_grad, shift_two_grad = norm_backward(
         norm_two_grad, unit_two, inverse_two, gain_two
     )
     hidden_grad = grad_out + hidden_back
+    mlp_grad_pack, hidden_grad = lax.optimization_barrier((mlp_grad_pack, hidden_grad))
+    mlp_grads = lax.psum_scatter(mlp_grad_pack, ("dp", "ctx"), scatter_dimension=0, tiled=True)
     down_bias_grad = jnp.sum(grad_out, axis=0)
     out_bias_grad = jnp.sum(hidden_grad, axis=0)
     hidden_token_rows = tensor_gather(hidden_grad.astype(BF)).reshape(images, half_len, width)
@@ -247,31 +241,23 @@
     query_reduced_precision = query_grads.astype(BF)
     query_bias_grad = jnp.sum(query_reduced_precision, axis=(0, 2), dtype=F32).reshape(head_width)
     value_bias_grad = jnp.sum(value_reduced_precision, axis=(0, 2), dtype=F32).reshape(head_width)
-    query_weight_grad = jnp.einsum(
-        "okz,oaks->zas", normed_every_row, query_reduced_precision, preferred_element_type=F32
-    ).reshape(width, head_width)
-    key_weight_grad = jnp.einsum(
-        "okz,oaks->zas", normed_every_row, key_reduced_precision, preferred_element_type=F32
-    ).reshape(width, head_width)
-    value_weight_grad = jnp.einsum(
-        "okz,oaks->zas", normed_every_row, value_reduced_precision, preferred_element_type=F32
-    ).reshape(width, head_width)
+    qkv_grads = jnp.stack(
+        [query_reduced_precision, key_reduced_precision, value_reduced_precision]
+    )
+    qkv_weight_grad = jnp.einsum(
+        "okz,toaks->ztas", normed_every_row, qkv_grads, preferred_element_type=F32
+    ).reshape(width, 3 * head_width)
     attn_grads = lax.psum_scatter(
         jnp.concatenate(
-            [query_weight_grad, key_weight_grad, value_weight_grad, out_grad_t], axis=1
-        ).astype(BF),
+            [jnp.pad(out_grad_t.astype(BF), ((0, 0), (0, pad_out))), qkv_weight_grad.astype(BF)],
+            axis=1,
+        ),
         ("dp", "ctx"),
         scatter_dimension=0,
         tiled=True,
     )
     norm_one_terms = jnp.einsum(
-        "tivw,niw->tvn", query_reduced_precision, query_per_head, preferred_element_type=F32
-    )
-    norm_one_terms = norm_one_terms + jnp.einsum(
-        "tivw,niw->tvn", key_reduced_precision, key_per_head, preferred_element_type=F32
-    )
-    norm_one_terms = norm_one_terms + jnp.einsum(
-        "tivw,niw->tvn", value_reduced_precision, value_per_head, preferred_element_type=F32
+        "toaks,tzas->okz", qkv_grads, qkv_w, preferred_element_type=F32
     )
     norm_one_grad = tensor_reduce(norm_one_terms.reshape(n_t, rows, width))
     input_back, gain_one_grad, shift_one_grad = norm_backward(
@@ -301,10 +287,18 @@
     query_bias_sum = head_sums[:head_width]
     value_bias_sum = head_sums[head_width : 2 * head_width]
     up_bias_sum = head_sums[2 * head_width :]
-    attn_grads = attn_grads.astype(F32).reshape(piece, 4, head_width)
+    attn_grads = attn_grads.astype(F32)
     mlp_grads = mlp_grads.astype(F32)
-    attn_grads = [attn_grads[:, i] for i in range(4)]
-    mlp_grads = [mlp_grads[:, :hidden_width], mlp_grads[:, hidden_width:]]
+    out_cols = head_width + pad_out
+    attn_grads = [
+        attn_grads[:, out_cols + i * head_width : out_cols + (i + 1) * head_width]
+        for i in range(3)
+    ] + [attn_grads[:, :head_width]]
+    hidden_cols = hidden_width + pad_hidden
+    mlp_grads = [
+        mlp_grads[:, :hidden_width],
+        mlp_grads[:, hidden_cols : hidden_cols + hidden_width],
+    ]
     return (
         layer_out,
         loss_value,

time: 620 us -> 608 us (0.981)
  waiting for transfers between devices: 294 us -> 326 us
  local copies, waits for them, and re-layouts: 85.5 us -> 58.2 us
  matrix products: 125 us -> 109 us
    reduce_scatter x1, waiting for transfers between devices: 0.01 us -> 113 us  [on_device(): lax.psum_scatter(mlp_grad_pack, ('dp', 'ctx'), scatter_dimension=0, tiled...]
    unnamed x5, waiting for transfers between devices: 80.7 us -> 17.6 us
    all_gather x1, waiting for transfers between devices: 69.1 us -> 49.4 us  [on_device(): attn_full = lax.all_gather(attn_pack, ('dp', 'ctx'), axis=1, tiled=True)]
    unnamed x154 -> x128, local copies, waits for them, and re-layouts: 35.7 us -> 16.5 us
    ppermute x12, waiting for transfers between devices: 111 us -> 126 us  [swap(): return lax.ppermute(values, axis, [(0, 1), (1, 0)])]
    ppermute x13, waiting for transfers between devices: 32.8 us -> 19.3 us  [tree_sum(): values = jax.tree.map(lambda v: v + lax.ppermute(v, axis, perm), values)]
    reshape x5 -> x0, local copies, waits for them, and re-layouts: 11.4 us -> none  [the longest x1 2.62 us: on_device(): query_weight_grad = jnp.einsum('okz,oaks->zas', normed_every_row, query_r...]
    concatenate x1 -> x0, local copies, waits for them, and re-layouts: 9.89 us -> none  [on_device(): jnp.concatenate([query_weight_grad, key_weight_grad, value_weight_grad, o...]
  transfers between devices with their start and end apart: 29 -> 29, of which waited for: 18 -> 23; matrix products, arithmetic and copies ran while one was open for 29% -> 20% of each run, Pallas kernels for 0% -> 0%
where the time goes in v2:
time: 608 us; the launch traced here: 603 us
  waiting for transfers between devices  326 us (54%)
  matrix products  109 us (18%)
  local copies, waits for them, and re-layouts  58.2 us (10%)
  other arithmetic  54 us (9%)
  starting transfers between devices  35.7 us (6%)
  between operations  20.7 us (3%)
    ppermute x12, waiting for transfers between devices, swap(): return lax.ppermute(values, axis, [(0, 1), (1, 0)])  126 us
    reduce_scatter x1, waiting for transfers between devices, on_device(): lax.psum_scatter(mlp_grad_pack, ('dp', 'ctx'), scatter_dimension=0, tiled...  113 us
    all_gather x1, waiting for transfers between devices, on_device(): attn_full = lax.all_gather(attn_pack, ('dp', 'ctx'), axis=1, tiled=True)  49.4 us
    ppermute x13, starting transfers between devices, tree_sum(): values = jax.tree.map(lambda v: v + lax.ppermute(v, axis, perm), values)  22.5 us
    ppermute x13, waiting for transfers between devices, tree_sum(): values = jax.tree.map(lambda v: v + lax.ppermute(v, axis, perm), values)  19.3 us
    unnamed x5, waiting for transfers between devices  17.6 us
    unnamed x128, local copies, waits for them, and re-layouts  16.5 us
    dot_general x1, matrix products, on_device(): jnp.einsum('bhqe,bhke->bhqk', mixed_grad, value_all, preferred_element_ty...  14.7 us
  transfers between devices with their start and end apart: 29, of which 23 were waited for; matrix products, arithmetic and copies ran while one was open for 20% of the time, Pallas kernels for 0%

profile of v2, /device:TPU:0, one launch (start us, length us, event | category | flops | bytes accessed | tf_op | source)
XLA Modules:
  0.0 603.0 jit_solution(12647250671530605282)
XLA Ops:
  34.9 49.4 %all-gather.3.cloned.1.call-done = bf16[5,1152,576]{2,1,0:T(8,128)(2,1)} async-done(((bf16[5,72,576]{2,1,0:T(8,128)(2,1)}), bf16[5,1152,576]{2,1,0:T(8,128)(2,1)}) %all-gather.3.cloned.1.call-update) | async-done | bytes 6635536 | tf_op jit(solution)/shard_map/all_gather | solution.py:138
  95.2 6.7 %copy.80 = bf16[3,1152,576]{1,2,0:T(8,128)(2,1)} copy(bf16[3,1152,576]{2,1,0:T(8,128)(2,1)} %slice.162) | data formatting | bytes 7962624 | tf_op jit(solution)/shard_map/slice | solution.py:141
  102.4 7.5 %collective-permute-done.4 = bf16[368,1152]{1,0:T(8,128)(2,1)} collective-permute-done((bf16[368,1152]{1,0:T(8,128)(2,1)S(1)}, bf16[368,1152]{1,0:T(8,128)(2,1)}, u32[]{:S(2)}, u32[]{:S(2)}) %collective-permute-start.4) | collective-permute-done | bytes 847904 | tf_op jit(solution)/shard_map/ppermute | solution.py:48
  109.8 6.1 %fusion.15 = bf16[3,2,8,368,72]{3,4,1,2,0:T(8,128)(2,1)S(1)} fusion(f32[3,8,72]{2,1,0:T(8,128)S(1)} %maximum_bitcast_fusion, bf16[3,1152,8,72,1]{1,3,4,2,0:T(8,128)(2,1)} %bitcast.218, bf16[1,368,1152]{2,1,0:T(8,128)(2,1)} %bitcast.18, bf16[1,368,1152]{2,1,0:T(8,128)(2,1)S(1)} %fusion.39), kind=kOutput, calls=%fused_computation.35 | convolution fusion | flops 2936180736 | bytes 8227584 | tf_op jit(solution)/shard_map/pro,tojx->tpjrx/dot_general | solution.py:159
  132.5 6.5 %fusion.57 = bf16[2,8,368,72]{2,3,1,0:T(8,128)(2,1)} fusion(f32[2,8,368,736]{3,2,1,0:T(8,128)S(1)} %get-tuple-element.68, f32[2,8,368]{2,1,0:T(8,128)S(1)} %log_add_fusion, pred[736]{0:T(1024)(128)(4,1)S(1)} %fusion.82, bf16[2,8,368,72]{2,3,0,1:T(8,128)(2,1)S(1)} %collective-permute-done.6, bf16[2,8,368,72]{2,3,0,1:T(8,128)(2,1)S(1)} %copy-done.15), kind=kOutput, calls=%fused_computation.116 | convolution fusion | flops 645183488 | bytes 19902176 | tf_op jit(solution)/shard_map/bhqk,bhke->bhqe/dot_general | solution.py:174
  143.6 19.4 %collective-permute-done.7 = bf16[368,1152]{1,0:T(8,128)(2,1)S(1)} collective-permute-done((bf16[368,1152]{1,0:T(8,128)(2,1)S(1)}, bf16[368,1152]{1,0:T(8,128)(2,1)S(1)}, u32[]{:S(2)}, u32[]{:S(2)}) %collective-permute-start.7) | collective-permute-done | bytes 847904 | tf_op jit(solution)/shard_map/ppermute | solution.py:48
  166.0 18.3 %collective-permute-done.8 = bf16[368,1152]{1,0:T(8,128)(2,1)S(1)} collective-permute-done((bf16[368,1152]{1,0:T(8,128)(2,1)S(1)}, bf16[368,1152]{1,0:T(8,128)(2,1)S(1)}, u32[]{:S(2)}, u32[]{:S(2)}) %collective-permute-start.8) | collective-permute-done | bytes 847904 | tf_op jit(solution)/shard_map/ppermute | solution.py:48
  185.7 7.6 %fusion.12 = f32[736,2176]{1,0:T(8,128)S(1)} fusion(bf16[736,1152]{1,0:T(8,128)(2,1)} %bitcast.222, bf16[2,1152,2176]{2,1,0:T(8,128)(2,1)} %all-gather.5.cloned.1.call-done), kind=kOutput, calls=%fused_computation.29 | convolution fusion | flops 3689938944 | bytes 13115392 | tf_op jit(solution)/shard_map/dot_general | solution.py:185
  193.3 5.8 fusion.13
  203.4 18.1 %collective-permute-done.9 = bf16[368,1152]{1,0:T(8,128)(2,1)} collective-permute-done((bf16[368,1152]{1,0:T(8,128)(2,1)}, bf16[368,1152]{1,0:T(8,128)(2,1)}, u32[]{:S(2)}, u32[]{:S(2)}) %collective-permute-start.9) | collective-permute-done | bytes 847904 | tf_op jit(solution)/shard_map/ppermute | solution.py:48
  226.6 17.0 %collective-permute-done.10 = bf16[368,1152]{1,0:T(8,128)(2,1)S(1)} collective-permute-done((bf16[368,1152]{1,0:T(8,128)(2,1)S(1)}, bf16[368,1152]{1,0:T(8,128)(2,1)S(1)}, u32[]{:S(2)}, u32[]{:S(2)}) %collective-permute-start.10) | collective-permute-done | bytes 847904 | tf_op jit(solution)/shard_map/ppermute | solution.py:48
  249.4 9.5 %fusion.9 = bf16[736,2176]{1,0:T(8,128)(2,1)S(1)} fusion(bf16[736,1152]{1,0:T(8,128)(2,1)S(1)} %bitcast.225, f32[736,2176]{1,0:T(8,128)} %copy-done.51, bf16[2,1152,2176]{2,1,0:T(8,128)(2,1)S(1)} %bitcast.240, f32[2176]{0:T(1024)S(1)} %pad_convert_fusion), kind=kOutput, calls=%fused_computation.21 | convolution fusion | flops 3721969664 | bytes 16330752 | tf_op jit(solution)/shard_map/rd,df->rf/dot_general | solution.py:201
  277.3 11.7 %collective-permute-done.11 = bf16[368,1152]{1,0:T(8,128)(2,1)} collective-permute-done((bf16[368,1152]{1,0:T(8,128)(2,1)}, bf16[368,1152]{1,0:T(8,128)(2,1)}, u32[]{:S(2)}, u32[]{:S(2)}) %collective-permute-start.11) | collective-permute-done | bytes 847904 | tf_op jit(solution)/shard_map/ppermute | solution.py:48
  297.3 15.2 %collective-permute-done.12 = bf16[368,1152]{1,0:T(8,128)(2,1)S(1)} collective-permute-done((bf16[368,1152]{1,0:T(8,128)(2,1)S(1)}, bf16[368,1152]{1,0:T(8,128)(2,1)S(1)}, u32[]{:S(2)}, u32[]{:S(2)}) %collective-permute-start.12) | collective-permute-done | bytes 847904 | tf_op jit(solution)/shard_map/ppermute | solution.py:48
  313.9 8.4 %fusion.73 = f32[2,8,736,72]{2,3,1,0:T(8,128)S(1)} fusion(bf16[2,8,368,72]{2,3,0,1:T(8,128)(2,1)S(1)} %fusion.65, f32[2,8,368,736]{3,2,1,0:T(8,128)} %copy-done, f32[2,8,368]{2,1,0:T(8,128)S(1)} %log_add_fusion, pred[736]{0:T(1024)(128)(4,1)S(1)} %fusion.82), kind=kOutput, calls=%fused_computation.129 | convolution fusion | flops 641368064 | bytes 21597920 | tf_op jit(solution)/shard_map/bhqk,bhqe->bhke/dot_general | solution.py:226
  325.4 14.7 %multiply_reduce_fusion = (f32[2,8,368]{2,1,0:T(8,128)S(1)}, f32[2,8,368,736]{3,2,1,0:T(8,128)}) fusion(f32[2,8,368,736]{3,2,1,0:T(8,128)} %copy-done, f32[2,8,368]{2,1,0:T(8,128)S(1)} %log_add_fusion, pred[736]{0:T(1024)(128)(4,1)S(1)} %fusion.82, bf16[2,8,368,72]{2,3,0,1:T(8,128)(2,1)S(1)} %fusion.65, bf16[2,8,368,72]{2,3,0,1:T(8,128)(2,1)S(1)} %copy-done.30, ...), kind=kOutput, calls=%fused_computation.1 | convolution fusion | flops 649087232 | bytes 37260000 | tf_op jit(solution)/shard_map/bhqe,bhke->bhqk/dot_general | solution.py:225
  340.0 12.9 %multiply_convert_fusion = bf16[2,8,368,736]{3,2,1,0:T(8,128)(2,1)S(1)} fusion(f32[2,8,368,736]{3,2,1,0:T(8,128)} %get-tuple-element.70, f32[2,8,368,736]{3,2,1,0:T(8,128)} %copy-done, f32[2,8,368]{2,1,0:T(8,128)S(1)} %get-tuple-element.69, f32[2,8,368]{2,1,0:T(8,128)S(1)} %log_add_fusion, pred[736]{0:T(1024)(128)(4,1)S(1)} %fusion.82), kind=kLoop, calls=%fused_computation | loop fusion | flops 26001408 | bytes 43383520 | tf_op jit(solution)/shard_map/convert_element_type | solution.py:230
  364.0 7.5 %convert_reduce_fusion.3 = (f32[8,72]{1,0:T(8,128)}, bf16[2,8,368,72]{2,3,1,0:T(8,128)(2,1)S(1)}) fusion(bf16[2,8,368,736]{3,2,1,0:T(8,128)(2,1)} %copy-done.3, bf16[2,8,368,72]{2,3,0,1:T(8,128)(2,1)} %collective-permute-done.5, bf16[2,8,368,72]{2,3,0,1:T(8,128)(2,1)} %get-tuple-element.51), kind=kOutput, calls=%fused_computation.58 | convolution fusion | flops 629120448 | bytes 11213056 | tf_op jit(solution)/shard_map/bhqk,bhke->bhqe/dot_general | solution.py:232
  374.3 6.6 %bitcast_convert_fusion = bf16[1152,3,8,72]{0,3,2,1:T(8,128)(2,1)} fusion(bf16[1,368,1152]{2,1,0:T(8,128)(2,1)} %bitcast.18, bf16[1,368,1152]{2,1,0:T(8,128)(2,1)S(1)} %copy-done.32, bf16[1,2,8,368,72]{3,4,2,1,0:T(8,128)(2,1)S(1)} %get-tuple-element.48, bf16[1,2,8,368,72]{3,4,2,1,0:T(8,128)(2,1)S(1)} %fusion.70, bf16[1,2,8,368,72]{3,4,2,1,0:T(8,128)(2,1)S(1)} %bitcast.243), kind=kOutput, calls=%fused_computation.14 | convolution fusion | flops 2943258624 | bytes 8220672 | tf_op jit(solution)/shard_map/okz,toaks->ztas/dot_general | solution.py:247
  381.0 6.6 %copy.93 = bf16[1152,1728]{1,0:T(8,128)(2,1)} copy(bf16[1152,1728]{0,1:T(8,128)(2,1)} %bitcast.220) | data formatting | bytes 7962624 | tf_op jit(solution)/shard_map/convert_element_type | solution.py:252
  394.4 6.3 %convolution_bitcast_fusion.1 = f32[2,368,1152]{2,1,0:T(8,128)S(1)} fusion(bf16[3,1152,8,72,1]{1,3,2,4,0:T(8,128)(2,1)} %bitcast.219, bf16[1,2,8,368,72]{3,4,2,1,0:T(8,128)(2,1)S(1)} %copy-done.28, bf16[1,2,8,368,72]{3,4,2,1,0:T(8,128)(2,1)S(1)} %copy-done.26, bf16[1,2,8,368,72]{3,4,2,1,0:T(8,128)(2,1)} %bitcast.244), kind=kOutput, calls=%fused_computation.32 | convolution fusion | flops 2932789248 | bytes 9916416 | tf_op jit(solution)/shard_map/toaks,tzas->okz/dot_general | solution.py:259
  406.1 18.2 %collective-permute-done.15 = bf16[368,1152]{1,0:T(8,128)(2,1)S(1)} collective-permute-done((bf16[368,1152]{1,0:T(8,128)(2,1)}, bf16[368,1152]{1,0:T(8,128)(2,1)S(1)}, u32[]{:S(2)}, u32[]{:S(2)}) %collective-permute-start.15) | collective-permute-done | bytes 847904 | tf_op jit(solution)/shard_map/ppermute | solution.py:48
  457.9 17.1 %reduce-scatter.7.cloned.1.call-done = bf16[72,2368]{1,0:T(8,128)(2,1)} async-done(((bf16[1152,2368]{1,0:T(8,128)(2,1)}), bf16[72,2368]{1,0:T(8,128)(2,1)}) %reduce-scatter.7.cloned.1.call-update) | async-done | bytes 341008
  478.5 113.4 %reduce-scatter.5.cloned.1.call-done = bf16[72,4352]{1,0:T(8,128)(2,1)} async-done(((bf16[1152,4352]{1,0:T(8,128)(2,1)}), bf16[72,4352]{1,0:T(8,128)(2,1)}) %reduce-scatter.5.cloned.1.call-update) | async-done | bytes 626704 | tf_op jit(solution)/shard_map/reduce_scatter | solution.py:213
  (270 shorter events, 171.9 us)
Async XLA Ops:
  7.2 77.1 %all-gather.3.cloned.1.call-start = ((), (), s32[]{:S(2)}) async-start(), calls=%async_computation.2 | async-start | bytes 7833600 | tf_op jit(solution)/shard_map/all_gather | solution.py:138
  13.6 172.1 %all-gather.5.cloned.1.call-start = ((), (), s32[]{:S(2)}) async-start(), calls=%async_computation.3 | async-start | bytes 10653696 | tf_op jit(solution)/shard_map/all_gather | solution.py:140
  14.5 460.4 %reduce-scatter.7.cloned.1.call-start = ((), (), s32[]{:S(2)}) async-start(), calls=%async_computation.5 | async-start | bytes 5953536
  14.6 4.9 collective-permute-start
  24.3 3.8 collective-permute-start.2
  28.7 5.0 collective-permute-start.3
  88.6 21.2 %collective-permute-start.4 = (bf16[368,1152]{1,0:T(8,128)(2,1)S(1)}, bf16[368,1152]{1,0:T(8,128)(2,1)}, u32[]{:S(2)}, u32[]{:S(2)}) collective-permute-start(bf16[368,1152]{1,0:T(8,128)(2,1)S(1)} %fusion.27), channel_id=1, source_target_pairs={{0,1},{1,0},{2,3},{3,2},{4,5},{5,4},{6,7},{7,6},{8,9},{9,8},{10,11... | collective-permute-start | bytes 2543624 | tf_op jit(solution)/shard_map/ppermute | solution.py:48
  119.2 11.3 %collective-permute-start.6 = (bf16[2,8,368,72]{2,3,0,1:T(8,128)(2,1)}, bf16[2,8,368,72]{2,3,0,1:T(8,128)(2,1)S(1)}, u32[]{:S(2)}, u32[]{:S(2)}) collective-permute-start(bf16[2,8,368,72]{2,3,0,1:T(8,128)(2,1)} %get-tuple-element.50), channel_id=1, source_target_pairs={{0,2},{2,0},{1,3},{3,1},{4,6},{6,4},{5,7},{7,5},{8,10},{10,8},{9,1... | collective-permute-start | bytes 2543624 | tf_op jit(solution)/shard_map/ppermute | solution.py:48
  142.0 21.0 %collective-permute-start.7 = (bf16[368,1152]{1,0:T(8,128)(2,1)S(1)}, bf16[368,1152]{1,0:T(8,128)(2,1)S(1)}, u32[]{:S(2)}, u32[]{:S(2)}) collective-permute-start(bf16[368,1152]{1,0:T(8,128)(2,1)S(1)} %fusion.71), channel_id=1, source_target_pairs={{0,1},{1,0},{2,3},{3,2},{4,5},{5,4},{6,7},{7,6},{8,9},{9,8},{10,11... | collective-permute-start | bytes 2543624 | tf_op jit(solution)/shard_map/ppermute | solution.py:48
  164.1 20.2 %collective-permute-start.8 = (bf16[368,1152]{1,0:T(8,128)(2,1)S(1)}, bf16[368,1152]{1,0:T(8,128)(2,1)S(1)}, u32[]{:S(2)}, u32[]{:S(2)}) collective-permute-start(bf16[368,1152]{1,0:T(8,128)(2,1)S(1)} %add_convert_fusion.1), channel_id=1, source_target_pairs={{0,1},{1,0},{2,3},{3,2},{4,5},{5,4},{6,7},{7,6},{8,9},{9,8},{10,11... | collective-permute-start | bytes 2543624 | tf_op jit(solution)/shard_map/ppermute | solution.py:48
  201.9 19.6 %collective-permute-start.9 = (bf16[368,1152]{1,0:T(8,128)(2,1)}, bf16[368,1152]{1,0:T(8,128)(2,1)}, u32[]{:S(2)}, u32[]{:S(2)}) collective-permute-start(bf16[368,1152]{1,0:T(8,128)(2,1)} %slice.279), channel_id=1, source_target_pairs={{0,1},{1,0},{2,3},{3,2},{4,5},{5,4},{6,7},{7,6},{8,9},{9,8},{10,11... | collective-permute-start | bytes 2543624 | tf_op jit(solution)/shard_map/ppermute | solution.py:48
  225.1 18.5 %collective-permute-start.10 = (bf16[368,1152]{1,0:T(8,128)(2,1)S(1)}, bf16[368,1152]{1,0:T(8,128)(2,1)S(1)}, u32[]{:S(2)}, u32[]{:S(2)}) collective-permute-start(bf16[368,1152]{1,0:T(8,128)(2,1)S(1)} %multiply_convert_fusion.3), channel_id=1, source_target_pairs={{0,1},{1,0},{2,3},{3,2},{4,5},{5,4},{6,7},{7,6},{8,9},{9,8},{10,11... | collective-permute-start | bytes 2543624 | tf_op jit(solution)/shard_map/ppermute | solution.py:48
  271.1 17.9 %collective-permute-start.11 = (bf16[368,1152]{1,0:T(8,128)(2,1)}, bf16[368,1152]{1,0:T(8,128)(2,1)}, u32[]{:S(2)}, u32[]{:S(2)}) collective-permute-start(bf16[368,1152]{1,0:T(8,128)(2,1)} %slice.278), channel_id=1, source_target_pairs={{0,1},{1,0},{2,3},{3,2},{4,5},{5,4},{6,7},{7,6},{8,9},{9,8},{10,11... | collective-permute-start | bytes 2543624 | tf_op jit(solution)/shard_map/ppermute | solution.py:48
  295.7 16.8 %collective-permute-start.12 = (bf16[368,1152]{1,0:T(8,128)(2,1)S(1)}, bf16[368,1152]{1,0:T(8,128)(2,1)S(1)}, u32[]{:S(2)}, u32[]{:S(2)}) collective-permute-start(bf16[368,1152]{1,0:T(8,128)(2,1)S(1)} %convert_element_type.165), channel_id=1, source_target_pairs={{0,1},{1,0},{2,3},{3,2},{4,5},{5,4},{6,7},{7,6},{8,9},{9,8},{10,11... | collective-permute-start | bytes 2543624 | tf_op jit(solution)/shard_map/ppermute | solution.py:48
  325.4 46.2 %collective-permute-start.14 = (bf16[2,8,368,72]{2,3,1,0:T(8,128)(2,1)}, bf16[2,8,368,72]{2,3,1,0:T(8,128)(2,1)}, u32[]{:S(2)}, u32[]{:S(2)}) collective-permute-start(bf16[2,8,368,72]{2,3,1,0:T(8,128)(2,1)} %slice.276), channel_id=1, source_target_pairs={{0,2},{2,0},{1,3},{3,1},{4,6},{6,4},{5,7},{7,5},{8,10},{10,8},{9,1... | collective-permute-start | bytes 2543624 | tf_op jit(solution)/shard_map/ppermute | solution.py:48
  363.5 10.6 %collective-permute-start.13 = (bf16[2,8,368,72]{2,3,1,0:T(8,128)(2,1)S(1)}, bf16[2,8,368,72]{2,3,1,0:T(8,128)(2,1)S(1)}, u32[]{:S(2)}, u32[]{:S(2)}) collective-permute-start(bf16[2,8,368,72]{2,3,1,0:T(8,128)(2,1)S(1)} %slice.277), channel_id=1, source_target_pairs={{0,2},{2,0},{1,3},{3,1},{4,6},{6,4},{5,7},{7,5},{8,10},{10,8},{9,1... | collective-permute-start | bytes 2543624 | tf_op jit(solution)/shard_map/ppermute | solution.py:48
  392.9 199.0 %reduce-scatter.5.cloned.1.call-start = ((), (), s32[]{:S(2)}) async-start(), calls=%async_computation.4 | async-start | bytes 10653696 | tf_op jit(solution)/shard_map/reduce_scatter | solution.py:213
  403.4 20.9 %collective-permute-start.15 = (bf16[368,1152]{1,0:T(8,128)(2,1)}, bf16[368,1152]{1,0:T(8,128)(2,1)S(1)}, u32[]{:S(2)}, u32[]{:S(2)}) collective-permute-start(bf16[368,1152]{1,0:T(8,128)(2,1)} %fusion.72), channel_id=1, source_target_pairs={{0,1},{1,0},{2,3},{3,2},{4,5},{5,4},{6,7},{7,6},{8,9},{9,8},{10,11... | collective-permute-start | bytes 2543624 | tf_op jit(solution)/shard_map/ppermute | solution.py:48
  430.1 4.6 collective-permute-start.17
  434.7 3.9 collective-permute-start.18
  438.5 13.6 %collective-permute-start.19 = (f32[6913]{0:T(1024)S(1)}, f32[6913]{0:T(1024)S(1)}, u32[]{:S(2)}, u32[]{:S(2)}) collective-permute-start(f32[6913]{0:T(1024)S(1)} %add.281), channel_id=1, source_target_pairs={{0,16},{4,20},{8,24},{12,28},{16,0},{20,4},{24,8},{28,12},{1,17},{... | collective-permute-start | bytes 82964 | tf_op jit(solution)/shard_map/ppermute | solution.py:97
  441.4 5.2 collective-permute-start.23
  446.7 5.4 collective-permute-start.24
  452.1 3.9 collective-permute-start.20
  (62 other events, 706.7 us)
Sparse Core Ops, SparseCore 0:
  13.7 70.5 all-gather.2
  87.1 83.4 all-gather.4
  393.0 81.8 reduce-scatter.6
  478.9 112.8 reduce-scatter.4

commit v3 on v2

--- a/solution.py
+++ b/solution.py
@@ -2,6 +2,7 @@
 import jax.numpy as jnp
 from jax import lax
 from jax.sharding import PartitionSpec as P
+
 
 HD = 72
 REAL = 729
@@ -99,7 +100,7 @@
     return values
 
 
-def on_device(
+def on_device_body(
     tokens,
     teacher,
     valid_len,
@@ -210,7 +211,9 @@
     )
     hidden_grad = grad_out + hidden_back
     mlp_grad_pack, hidden_grad = lax.optimization_barrier((mlp_grad_pack, hidden_grad))
-    mlp_grads = lax.psum_scatter(mlp_grad_pack, ("dp", "ctx"), scatter_dimension=0, tiled=True)
+    mlp_grads = lax.psum_scatter(
+        mlp_grad_pack, ("dp", "ctx"), scatter_dimension=0, tiled=True
+    )
     down_bias_grad = jnp.sum(grad_out, axis=0)
     out_bias_grad = jnp.sum(hidden_grad, axis=0)
     hidden_token_rows = tensor_gather(hidden_grad.astype(BF)).reshape(images, half_len, width)
@@ -323,7 +326,7 @@
 
 def solution(mesh):
     return jax.shard_map(
-        on_device,
+        on_device_body,
         mesh=mesh,
         in_specs=(
             P(("dp", "tensor"), "ctx", None),

time: 608 us -> 608 us (level)
  no operation moved by 1% of the time
where the time goes in v3:
time: 608 us; the launch traced here: 603 us
  waiting for transfers between devices  326 us (54%)
  matrix products  109 us (18%)
  local copies, waits for them, and re-layouts  58.2 us (10%)
  other arithmetic  54 us (9%)
  starting transfers between devices  35.7 us (6%)
  between operations  20.7 us (3%)
    ppermute x12, waiting for transfers between devices, swap(): return lax.ppermute(values, axis, [(0, 1), (1, 0)])  126 us
    reduce_scatter x1, waiting for transfers between devices, on_device_body(): lax.psum_scatter(mlp_grad_pack, ('dp', 'ctx'), scatter_dimension=0, tiled...  113 us
    all_gather x1, waiting for transfers between devices, on_device_body(): attn_full = lax.all_gather(attn_pack, ('dp', 'ctx'), axis=1, tiled=True)  49.4 us
    ppermute x13, starting transfers between devices, tree_sum(): values = jax.tree.map(lambda v: v + lax.ppermute(v, axis, perm), values)  22.5 us
    ppermute x13, waiting for transfers between devices, tree_sum(): values = jax.tree.map(lambda v: v + lax.ppermute(v, axis, perm), values)  19.3 us
    unnamed x5, waiting for transfers between devices  17.6 us
    unnamed x128, local copies, waits for them, and re-layouts  16.5 us
    dot_general x1, matrix products, on_device_body(): jnp.einsum('bhqe,bhke->bhqk', mixed_grad, value_all, preferred_element_ty...  14.7 us
  transfers between devices with their start and end apart: 29, of which 23 were waited for; matrix products, arithmetic and copies ran while one was open for 20% of the time, Pallas kernels for 0%

profile of v3, /device:TPU:0, one launch (start us, length us, event | category | flops | bytes accessed | tf_op | source)
XLA Modules:
  0.0 603.0 jit_solution(12647250671530605282)
XLA Ops:
  34.9 49.4 %all-gather.3.cloned.1.call-done = bf16[5,1152,576]{2,1,0:T(8,128)(2,1)} async-done(((bf16[5,72,576]{2,1,0:T(8,128)(2,1)}), bf16[5,1152,576]{2,1,0:T(8,128)(2,1)}) %all-gather.3.cloned.1.call-update) | async-done | bytes 6635536 | tf_op jit(solution)/shard_map/all_gather | solution.py:139
  95.2 6.7 %copy.80 = bf16[3,1152,576]{1,2,0:T(8,128)(2,1)} copy(bf16[3,1152,576]{2,1,0:T(8,128)(2,1)} %slice.162) | data formatting | bytes 7962624 | tf_op jit(solution)/shard_map/slice | solution.py:142
  102.4 7.5 %collective-permute-done.4 = bf16[368,1152]{1,0:T(8,128)(2,1)} collective-permute-done((bf16[368,1152]{1,0:T(8,128)(2,1)S(1)}, bf16[368,1152]{1,0:T(8,128)(2,1)}, u32[]{:S(2)}, u32[]{:S(2)}) %collective-permute-start.4) | collective-permute-done | bytes 847904 | tf_op jit(solution)/shard_map/ppermute | solution.py:49
  109.8 6.1 %fusion.15 = bf16[3,2,8,368,72]{3,4,1,2,0:T(8,128)(2,1)S(1)} fusion(f32[3,8,72]{2,1,0:T(8,128)S(1)} %maximum_bitcast_fusion, bf16[3,1152,8,72,1]{1,3,4,2,0:T(8,128)(2,1)} %bitcast.218, bf16[1,368,1152]{2,1,0:T(8,128)(2,1)} %bitcast.18, bf16[1,368,1152]{2,1,0:T(8,128)(2,1)S(1)} %fusion.39), kind=kOutput, calls=%fused_computation.35 | convolution fusion | flops 2936180736 | bytes 8227584 | tf_op jit(solution)/shard_map/pro,tojx->tpjrx/dot_general | solution.py:160
  132.5 6.5 %fusion.57 = bf16[2,8,368,72]{2,3,1,0:T(8,128)(2,1)} fusion(f32[2,8,368,736]{3,2,1,0:T(8,128)S(1)} %get-tuple-element.68, f32[2,8,368]{2,1,0:T(8,128)S(1)} %log_add_fusion, pred[736]{0:T(1024)(128)(4,1)S(1)} %fusion.82, bf16[2,8,368,72]{2,3,0,1:T(8,128)(2,1)S(1)} %collective-permute-done.6, bf16[2,8,368,72]{2,3,0,1:T(8,128)(2,1)S(1)} %copy-done.15), kind=kOutput, calls=%fused_computation.116 | convolution fusion | flops 645183488 | bytes 19902176 | tf_op jit(solution)/shard_map/bhqk,bhke->bhqe/dot_general | solution.py:175
  143.6 19.4 %collective-permute-done.7 = bf16[368,1152]{1,0:T(8,128)(2,1)S(1)} collective-permute-done((bf16[368,1152]{1,0:T(8,128)(2,1)S(1)}, bf16[368,1152]{1,0:T(8,128)(2,1)S(1)}, u32[]{:S(2)}, u32[]{:S(2)}) %collective-permute-start.7) | collective-permute-done | bytes 847904 | tf_op jit(solution)/shard_map/ppermute | solution.py:49
  166.0 18.3 %collective-permute-done.8 = bf16[368,1152]{1,0:T(8,128)(2,1)S(1)} collective-permute-done((bf16[368,1152]{1,0:T(8,128)(2,1)S(1)}, bf16[368,1152]{1,0:T(8,128)(2,1)S(1)}, u32[]{:S(2)}, u32[]{:S(2)}) %collective-permute-start.8) | collective-permute-done | bytes 847904 | tf_op jit(solution)/shard_map/ppermute | solution.py:49
  185.7 7.6 %fusion.12 = f32[736,2176]{1,0:T(8,128)S(1)} fusion(bf16[736,1152]{1,0:T(8,128)(2,1)} %bitcast.222, bf16[2,1152,2176]{2,1,0:T(8,128)(2,1)} %all-gather.5.cloned.1.call-done), kind=kOutput, calls=%fused_computation.29 | convolution fusion | flops 3689938944 | bytes 13115392 | tf_op jit(solution)/shard_map/dot_general | solution.py:186
  193.3 5.8 fusion.13
  203.4 18.1 %collective-permute-done.9 = bf16[368,1152]{1,0:T(8,128)(2,1)} collective-permute-done((bf16[368,1152]{1,0:T(8,128)(2,1)}, bf16[368,1152]{1,0:T(8,128)(2,1)}, u32[]{:S(2)}, u32[]{:S(2)}) %collective-permute-start.9) | collective-permute-done | bytes 847904 | tf_op jit(solution)/shard_map/ppermute | solution.py:49
  226.6 17.0 %collective-permute-done.10 = bf16[368,1152]{1,0:T(8,128)(2,1)S(1)} collective-permute-done((bf16[368,1152]{1,0:T(8,128)(2,1)S(1)}, bf16[368,1152]{1,0:T(8,128)(2,1)S(1)}, u32[]{:S(2)}, u32[]{:S(2)}) %collective-permute-start.10) | collective-permute-done | bytes 847904 | tf_op jit(solution)/shard_map/ppermute | solution.py:49
  249.4 9.5 %fusion.9 = bf16[736,2176]{1,0:T(8,128)(2,1)S(1)} fusion(bf16[736,1152]{1,0:T(8,128)(2,1)S(1)} %bitcast.225, f32[736,2176]{1,0:T(8,128)} %copy-done.51, bf16[2,1152,2176]{2,1,0:T(8,128)(2,1)S(1)} %bitcast.240, f32[2176]{0:T(1024)S(1)} %pad_convert_fusion), kind=kOutput, calls=%fused_computation.21 | convolution fusion | flops 3721969664 | bytes 16330752 | tf_op jit(solution)/shard_map/rd,df->rf/dot_general | solution.py:202
  277.3 11.7 %collective-permute-done.11 = bf16[368,1152]{1,0:T(8,128)(2,1)} collective-permute-done((bf16[368,1152]{1,0:T(8,128)(2,1)}, bf16[368,1152]{1,0:T(8,128)(2,1)}, u32[]{:S(2)}, u32[]{:S(2)}) %collective-permute-start.11) | collective-permute-done | bytes 847904 | tf_op jit(solution)/shard_map/ppermute | solution.py:49
  297.3 15.2 %collective-permute-done.12 = bf16[368,1152]{1,0:T(8,128)(2,1)S(1)} collective-permute-done((bf16[368,1152]{1,0:T(8,128)(2,1)S(1)}, bf16[368,1152]{1,0:T(8,128)(2,1)S(1)}, u32[]{:S(2)}, u32[]{:S(2)}) %collective-permute-start.12) | collective-permute-done | bytes 847904 | tf_op jit(solution)/shard_map/ppermute | solution.py:49
  313.9 8.4 %fusion.73 = f32[2,8,736,72]{2,3,1,0:T(8,128)S(1)} fusion(bf16[2,8,368,72]{2,3,0,1:T(8,128)(2,1)S(1)} %fusion.65, f32[2,8,368,736]{3,2,1,0:T(8,128)} %copy-done, f32[2,8,368]{2,1,0:T(8,128)S(1)} %log_add_fusion, pred[736]{0:T(1024)(128)(4,1)S(1)} %fusion.82), kind=kOutput, calls=%fused_computation.129 | convolution fusion | flops 641368064 | bytes 21597920 | tf_op jit(solution)/shard_map/bhqk,bhqe->bhke/dot_general | solution.py:229
  325.4 14.7 %multiply_reduce_fusion = (f32[2,8,368]{2,1,0:T(8,128)S(1)}, f32[2,8,368,736]{3,2,1,0:T(8,128)}) fusion(f32[2,8,368,736]{3,2,1,0:T(8,128)} %copy-done, f32[2,8,368]{2,1,0:T(8,128)S(1)} %log_add_fusion, pred[736]{0:T(1024)(128)(4,1)S(1)} %fusion.82, bf16[2,8,368,72]{2,3,0,1:T(8,128)(2,1)S(1)} %fusion.65, bf16[2,8,368,72]{2,3,0,1:T(8,128)(2,1)S(1)} %copy-done.30, ...), kind=kOutput, calls=%fused_computation.1 | convolution fusion | flops 649087232 | bytes 37260000 | tf_op jit(solution)/shard_map/bhqe,bhke->bhqk/dot_general | solution.py:228
  340.0 12.9 %multiply_convert_fusion = bf16[2,8,368,736]{3,2,1,0:T(8,128)(2,1)S(1)} fusion(f32[2,8,368,736]{3,2,1,0:T(8,128)} %get-tuple-element.70, f32[2,8,368,736]{3,2,1,0:T(8,128)} %copy-done, f32[2,8,368]{2,1,0:T(8,128)S(1)} %get-tuple-element.69, f32[2,8,368]{2,1,0:T(8,128)S(1)} %log_add_fusion, pred[736]{0:T(1024)(128)(4,1)S(1)} %fusion.82), kind=kLoop, calls=%fused_computation | loop fusion | flops 26001408 | bytes 43383520 | tf_op jit(solution)/shard_map/convert_element_type | solution.py:233
  364.0 7.5 %convert_reduce_fusion.3 = (f32[8,72]{1,0:T(8,128)}, bf16[2,8,368,72]{2,3,1,0:T(8,128)(2,1)S(1)}) fusion(bf16[2,8,368,736]{3,2,1,0:T(8,128)(2,1)} %copy-done.3, bf16[2,8,368,72]{2,3,0,1:T(8,128)(2,1)} %collective-permute-done.5, bf16[2,8,368,72]{2,3,0,1:T(8,128)(2,1)} %get-tuple-element.51), kind=kOutput, calls=%fused_computation.58 | convolution fusion | flops 629120448 | bytes 11213056 | tf_op jit(solution)/shard_map/bhqk,bhke->bhqe/dot_general | solution.py:235
  374.3 6.6 %bitcast_convert_fusion = bf16[1152,3,8,72]{0,3,2,1:T(8,128)(2,1)} fusion(bf16[1,368,1152]{2,1,0:T(8,128)(2,1)} %bitcast.18, bf16[1,368,1152]{2,1,0:T(8,128)(2,1)S(1)} %copy-done.32, bf16[1,2,8,368,72]{3,4,2,1,0:T(8,128)(2,1)S(1)} %get-tuple-element.48, bf16[1,2,8,368,72]{3,4,2,1,0:T(8,128)(2,1)S(1)} %fusion.70, bf16[1,2,8,368,72]{3,4,2,1,0:T(8,128)(2,1)S(1)} %bitcast.243), kind=kOutput, calls=%fused_computation.14 | convolution fusion | flops 2943258624 | bytes 8220672 | tf_op jit(solution)/shard_map/okz,toaks->ztas/dot_general | solution.py:250
  381.0 6.6 %copy.93 = bf16[1152,1728]{1,0:T(8,128)(2,1)} copy(bf16[1152,1728]{0,1:T(8,128)(2,1)} %bitcast.220) | data formatting | bytes 7962624 | tf_op jit(solution)/shard_map/convert_element_type | solution.py:255
  394.4 6.3 %convolution_bitcast_fusion.1 = f32[2,368,1152]{2,1,0:T(8,128)S(1)} fusion(bf16[3,1152,8,72,1]{1,3,2,4,0:T(8,128)(2,1)} %bitcast.219, bf16[1,2,8,368,72]{3,4,2,1,0:T(8,128)(2,1)S(1)} %copy-done.28, bf16[1,2,8,368,72]{3,4,2,1,0:T(8,128)(2,1)S(1)} %copy-done.26, bf16[1,2,8,368,72]{3,4,2,1,0:T(8,128)(2,1)} %bitcast.244), kind=kOutput, calls=%fused_computation.32 | convolution fusion | flops 2932789248 | bytes 9916416 | tf_op jit(solution)/shard_map/toaks,tzas->okz/dot_general | solution.py:262
  406.1 18.2 %collective-permute-done.15 = bf16[368,1152]{1,0:T(8,128)(2,1)S(1)} collective-permute-done((bf16[368,1152]{1,0:T(8,128)(2,1)}, bf16[368,1152]{1,0:T(8,128)(2,1)S(1)}, u32[]{:S(2)}, u32[]{:S(2)}) %collective-permute-start.15) | collective-permute-done | bytes 847904 | tf_op jit(solution)/shard_map/ppermute | solution.py:49
  457.9 17.1 %reduce-scatter.7.cloned.1.call-done = bf16[72,2368]{1,0:T(8,128)(2,1)} async-done(((bf16[1152,2368]{1,0:T(8,128)(2,1)}), bf16[72,2368]{1,0:T(8,128)(2,1)}) %reduce-scatter.7.cloned.1.call-update) | async-done | bytes 341008
  478.5 113.4 %reduce-scatter.5.cloned.1.call-done = bf16[72,4352]{1,0:T(8,128)(2,1)} async-done(((bf16[1152,4352]{1,0:T(8,128)(2,1)}), bf16[72,4352]{1,0:T(8,128)(2,1)}) %reduce-scatter.5.cloned.1.call-update) | async-done | bytes 626704 | tf_op jit(solution)/shard_map/reduce_scatter | solution.py:214
  (270 shorter events, 171.9 us)
Async XLA Ops:
  7.2 77.1 %all-gather.3.cloned.1.call-start = ((), (), s32[]{:S(2)}) async-start(), calls=%async_computation.2 | async-start | bytes 7833600 | tf_op jit(solution)/shard_map/all_gather | solution.py:139
  13.6 172.1 %all-gather.5.cloned.1.call-start = ((), (), s32[]{:S(2)}) async-start(), calls=%async_computation.3 | async-start | bytes 10653696 | tf_op jit(solution)/shard_map/all_gather | solution.py:141
  14.5 460.4 %reduce-scatter.7.cloned.1.call-start = ((), (), s32[]{:S(2)}) async-start(), calls=%async_computation.5 | async-start | bytes 5953536
  14.6 4.9 collective-permute-start
  24.3 3.8 collective-permute-start.2
  28.7 5.0 collective-permute-start.3
  88.6 21.2 %collective-permute-start.4 = (bf16[368,1152]{1,0:T(8,128)(2,1)S(1)}, bf16[368,1152]{1,0:T(8,128)(2,1)}, u32[]{:S(2)}, u32[]{:S(2)}) collective-permute-start(bf16[368,1152]{1,0:T(8,128)(2,1)S(1)} %fusion.27), channel_id=1, source_target_pairs={{0,1},{1,0},{2,3},{3,2},{4,5},{5,4},{6,7},{7,6},{8,9},{9,8},{10,11... | collective-permute-start | bytes 2543624 | tf_op jit(solution)/shard_map/ppermute | solution.py:49
  119.2 11.3 %collective-permute-start.6 = (bf16[2,8,368,72]{2,3,0,1:T(8,128)(2,1)}, bf16[2,8,368,72]{2,3,0,1:T(8,128)(2,1)S(1)}, u32[]{:S(2)}, u32[]{:S(2)}) collective-permute-start(bf16[2,8,368,72]{2,3,0,1:T(8,128)(2,1)} %get-tuple-element.50), channel_id=1, source_target_pairs={{0,2},{2,0},{1,3},{3,1},{4,6},{6,4},{5,7},{7,5},{8,10},{10,8},{9,1... | collective-permute-start | bytes 2543624 | tf_op jit(solution)/shard_map/ppermute | solution.py:49
  142.0 21.0 %collective-permute-start.7 = (bf16[368,1152]{1,0:T(8,128)(2,1)S(1)}, bf16[368,1152]{1,0:T(8,128)(2,1)S(1)}, u32[]{:S(2)}, u32[]{:S(2)}) collective-permute-start(bf16[368,1152]{1,0:T(8,128)(2,1)S(1)} %fusion.71), channel_id=1, source_target_pairs={{0,1},{1,0},{2,3},{3,2},{4,5},{5,4},{6,7},{7,6},{8,9},{9,8},{10,11... | collective-permute-start | bytes 2543624 | tf_op jit(solution)/shard_map/ppermute | solution.py:49
  164.1 20.2 %collective-permute-start.8 = (bf16[368,1152]{1,0:T(8,128)(2,1)S(1)}, bf16[368,1152]{1,0:T(8,128)(2,1)S(1)}, u32[]{:S(2)}, u32[]{:S(2)}) collective-permute-start(bf16[368,1152]{1,0:T(8,128)(2,1)S(1)} %add_convert_fusion.1), channel_id=1, source_target_pairs={{0,1},{1,0},{2,3},{3,2},{4,5},{5,4},{6,7},{7,6},{8,9},{9,8},{10,11... | collective-permute-start | bytes 2543624 | tf_op jit(solution)/shard_map/ppermute | solution.py:49
  201.9 19.6 %collective-permute-start.9 = (bf16[368,1152]{1,0:T(8,128)(2,1)}, bf16[368,1152]{1,0:T(8,128)(2,1)}, u32[]{:S(2)}, u32[]{:S(2)}) collective-permute-start(bf16[368,1152]{1,0:T(8,128)(2,1)} %slice.279), channel_id=1, source_target_pairs={{0,1},{1,0},{2,3},{3,2},{4,5},{5,4},{6,7},{7,6},{8,9},{9,8},{10,11... | collective-permute-start | bytes 2543624 | tf_op jit(solution)/shard_map/ppermute | solution.py:49
  225.1 18.5 %collective-permute-start.10 = (bf16[368,1152]{1,0:T(8,128)(2,1)S(1)}, bf16[368,1152]{1,0:T(8,128)(2,1)S(1)}, u32[]{:S(2)}, u32[]{:S(2)}) collective-permute-start(bf16[368,1152]{1,0:T(8,128)(2,1)S(1)} %multiply_convert_fusion.3), channel_id=1, source_target_pairs={{0,1},{1,0},{2,3},{3,2},{4,5},{5,4},{6,7},{7,6},{8,9},{9,8},{10,11... | collective-permute-start | bytes 2543624 | tf_op jit(solution)/shard_map/ppermute | solution.py:49
  271.1 17.9 %collective-permute-start.11 = (bf16[368,1152]{1,0:T(8,128)(2,1)}, bf16[368,1152]{1,0:T(8,128)(2,1)}, u32[]{:S(2)}, u32[]{:S(2)}) collective-permute-start(bf16[368,1152]{1,0:T(8,128)(2,1)} %slice.278), channel_id=1, source_target_pairs={{0,1},{1,0},{2,3},{3,2},{4,5},{5,4},{6,7},{7,6},{8,9},{9,8},{10,11... | collective-permute-start | bytes 2543624 | tf_op jit(solution)/shard_map/ppermute | solution.py:49
  295.7 16.8 %collective-permute-start.12 = (bf16[368,1152]{1,0:T(8,128)(2,1)S(1)}, bf16[368,1152]{1,0:T(8,128)(2,1)S(1)}, u32[]{:S(2)}, u32[]{:S(2)}) collective-permute-start(bf16[368,1152]{1,0:T(8,128)(2,1)S(1)} %convert_element_type.165), channel_id=1, source_target_pairs={{0,1},{1,0},{2,3},{3,2},{4,5},{5,4},{6,7},{7,6},{8,9},{9,8},{10,11... | collective-permute-start | bytes 2543624 | tf_op jit(solution)/shard_map/ppermute | solution.py:49
  325.4 46.2 %collective-permute-start.14 = (bf16[2,8,368,72]{2,3,1,0:T(8,128)(2,1)}, bf16[2,8,368,72]{2,3,1,0:T(8,128)(2,1)}, u32[]{:S(2)}, u32[]{:S(2)}) collective-permute-start(bf16[2,8,368,72]{2,3,1,0:T(8,128)(2,1)} %slice.276), channel_id=1, source_target_pairs={{0,2},{2,0},{1,3},{3,1},{4,6},{6,4},{5,7},{7,5},{8,10},{10,8},{9,1... | collective-permute-start | bytes 2543624 | tf_op jit(solution)/shard_map/ppermute | solution.py:49
  363.5 10.6 %collective-permute-start.13 = (bf16[2,8,368,72]{2,3,1,0:T(8,128)(2,1)S(1)}, bf16[2,8,368,72]{2,3,1,0:T(8,128)(2,1)S(1)}, u32[]{:S(2)}, u32[]{:S(2)}) collective-permute-start(bf16[2,8,368,72]{2,3,1,0:T(8,128)(2,1)S(1)} %slice.277), channel_id=1, source_target_pairs={{0,2},{2,0},{1,3},{3,1},{4,6},{6,4},{5,7},{7,5},{8,10},{10,8},{9,1... | collective-permute-start | bytes 2543624 | tf_op jit(solution)/shard_map/ppermute | solution.py:49
  392.9 199.0 %reduce-scatter.5.cloned.1.call-start = ((), (), s32[]{:S(2)}) async-start(), calls=%async_computation.4 | async-start | bytes 10653696 | tf_op jit(solution)/shard_map/reduce_scatter | solution.py:214
  403.4 20.9 %collective-permute-start.15 = (bf16[368,1152]{1,0:T(8,128)(2,1)}, bf16[368,1152]{1,0:T(8,128)(2,1)S(1)}, u32[]{:S(2)}, u32[]{:S(2)}) collective-permute-start(bf16[368,1152]{1,0:T(8,128)(2,1)} %fusion.72), channel_id=1, source_target_pairs={{0,1},{1,0},{2,3},{3,2},{4,5},{5,4},{6,7},{7,6},{8,9},{9,8},{10,11... | collective-permute-start | bytes 2543624 | tf_op jit(solution)/shard_map/ppermute | solution.py:49
  430.1 4.6 collective-permute-start.17
  434.7 3.9 collective-permute-start.18
  438.5 13.6 %collective-permute-start.19 = (f32[6913]{0:T(1024)S(1)}, f32[6913]{0:T(1024)S(1)}, u32[]{:S(2)}, u32[]{:S(2)}) collective-permute-start(f32[6913]{0:T(1024)S(1)} %add.281), channel_id=1, source_target_pairs={{0,16},{4,20},{8,24},{12,28},{16,0},{20,4},{24,8},{28,12},{1,17},{... | collective-permute-start | bytes 82964 | tf_op jit(solution)/shard_map/ppermute | solution.py:98
  441.4 5.2 collective-permute-start.23
  446.7 5.4 collective-permute-start.24
  452.1 3.9 collective-permute-start.20
  (62 other events, 706.7 us)
Sparse Core Ops, SparseCore 0:
  13.7 70.5 all-gather.2
  87.1 83.4 all-gather.4
  393.0 81.8 reduce-scatter.6
  478.9 112.8 reduce-scatter.4

commit v4 on v3

--- a/solution.py
+++ b/solution.py
@@ -59,6 +59,26 @@
     if lax.axis_size("tensor") == 2:
         return partials[0] + swap(partials[1].astype(BF), "tensor").astype(F32)
     return lax.psum_scatter(partials.astype(BF), "tensor", scatter_dimension=0).astype(F32)
+
+
+def tensor_gather_parts(values):
+    if lax.axis_size("tensor") == 2:
+        return [values, swap(values, "tensor")]
+    gathered = lax.all_gather(values, "tensor", axis=0)
+    return [gathered[i] for i in range(gathered.shape[0])]
+
+
+def tensor_reduce_parts(parts):
+    if lax.axis_size("tensor") == 2:
+        return parts[0] + swap(parts[1].astype(BF), "tensor").astype(F32)
+    return lax.psum_scatter(
+        jnp.stack(parts).astype(BF), "tensor", scatter_dimension=0
+    ).astype(F32)
+
+
+def split_rows(values, count):
+    size = values.shape[0] // count
+    return [values[i * size : (i + 1) * size] for i in range(count)]
 
 
 def ctx_gather(values):
@@ -182,11 +202,17 @@
     attn_sum = tensor_reduce(attn_terms.reshape(n_t, rows, width))
     hidden = inputs + attn_sum + out_bias
     normed_two, unit_two, inverse_two = norm_forward(hidden, gain_two, shift_two)
-    normed_two_all = tensor_gather(normed_two.astype(BF)).reshape(images * half_len, width)
+    normed_two_parts = tensor_gather_parts(normed_two.astype(BF))
+    normed_two_all = jnp.concatenate(normed_two_parts)
     before = jnp.dot(normed_two_all, up_w, preferred_element_type=F32) + up_b
     active = gelu_tanh(before).astype(BF)
-    mlp_terms = jnp.einsum("rf,df->rd", active, down_wt, preferred_element_type=F32)
-    result = hidden + tensor_reduce(mlp_terms.reshape(n_t, rows, width)) + down_bias
+    before_parts = split_rows(before, n_t)
+    active_parts = split_rows(active, n_t)
+    mlp_terms = [
+        jnp.einsum("rf,df->rd", part, down_wt, preferred_element_type=F32)
+        for part in active_parts
+    ]
+    result = hidden + tensor_reduce_parts(mlp_terms) + down_bias
     layer_out = result.astype(BF).reshape(own_images, half_len, width)
 
     position = lax.axis_index("ctx") * half_len + jnp.arange(half_len)
@@ -197,23 +223,38 @@
     factor = slot_total * (half_len * lax.axis_size("ctx")) / valid_count
     grad_out = error_rows * (valid_rows[:, None] * factor)
 
-    grad_rows = tensor_gather(grad_out.astype(BF)).reshape(images * half_len, width)
-    down_grad_t = jnp.einsum("rd,rf->df", grad_rows, active, preferred_element_type=F32)
-    active_grad = jnp.einsum("rd,df->rf", grad_rows, down_wt, preferred_element_type=F32)
-    before_grad = (active_grad * gelu_slope(before)).astype(BF)
+    grad_parts = tensor_gather_parts(grad_out.astype(BF))
+    before_grad_parts = [
+        (
+            jnp.einsum("rd,df->rf", g, down_wt, preferred_element_type=F32)
+            * gelu_slope(p)
+        ).astype(BF)
+        for g, p in zip(grad_parts, before_parts)
+    ]
+    norm_two_terms = [
+        jnp.einsum("rf,df->rd", g, up_w, preferred_element_type=F32)
+        for g in before_grad_parts
+    ]
+    down_grad_t = None
+    up_grad = None
+    for g, a_part, n_part, p_grad in zip(
+        grad_parts, active_parts, normed_two_parts, before_grad_parts
+    ):
+        down_term = jnp.einsum("rd,rf->df", g, a_part, preferred_element_type=F32)
+        up_term = jnp.einsum("rd,rf->df", n_part, p_grad, preferred_element_type=F32)
+        down_grad_t = down_term if down_grad_t is None else down_grad_t + down_term
+        up_grad = up_term if up_grad is None else up_grad + up_term
+    before_grad = jnp.concatenate(before_grad_parts)
     up_bias_grad = jnp.sum(before_grad[:, :hidden_width], axis=0, dtype=F32)
-    up_grad = jnp.einsum("rd,rf->df", normed_two_all, before_grad, preferred_element_type=F32)
     mlp_grad_pack = jnp.concatenate([up_grad.astype(BF), down_grad_t.astype(BF)], axis=1)
-    norm_two_terms = jnp.einsum("rf,df->rd", before_grad, up_w, preferred_element_type=F32)
-    norm_two_grad = tensor_reduce(norm_two_terms.reshape(n_t, rows, width))
+    mlp_grads = lax.psum_scatter(
+        mlp_grad_pack, ("dp", "ctx"), scatter_dimension=0, tiled=True
+    )
+    norm_two_grad = tensor_reduce_parts(norm_two_terms)
     hidden_back, gain_two_grad, shift_two_grad = norm_backward(
         norm_two_grad, unit_two, inverse_two, gain_two
     )
     hidden_grad = grad_out + hidden_back
-    mlp_grad_pack, hidden_grad = lax.optimization_barrier((mlp_grad_pack, hidden_grad))
-    mlp_grads = lax.psum_scatter(
-        mlp_grad_pack, ("dp", "ctx"), scatter_dimension=0, tiled=True
-    )
     down_bias_grad = jnp.sum(grad_out, axis=0)
     out_bias_grad = jnp.sum(hidden_grad, axis=0)
     hidden_token_rows = tensor_gather(hidden_grad.astype(BF)).reshape(images, half_len, width)

time: 608 us -> 587 us (0.965)
  waiting for transfers between devices: 326 us -> 296 us
  matrix products: 109 us -> 124 us
  other arithmetic: 54 us -> 46.9 us
    unnamed x5, waiting for transfers between devices: 17.6 us -> 0.07 us
    dot_general x5 -> x10, matrix products: 30.2 us -> 44 us  [the longest x2 9.98 us: on_device_body(): jnp.einsum('rd,df->rf', g, down_wt, preferred_element_type=F32)]
    reduce_scatter x1, waiting for transfers between devices: 113 us -> 107 us  [on_device_body(): lax.psum_scatter(mlp_grad_pack, ('dp', 'ctx'), scatter_dimension=0, tiled...]
    unnamed x128 -> x136, local copies, waits for them, and re-layouts: 16.5 us -> 14.1 us
  transfers between devices with their start and end apart: 29 -> 29, of which waited for: 23 -> 20; matrix products, arithmetic and copies ran while one was open for 20% -> 25% of each run, Pallas kernels for 0% -> 0%
where the time goes in v4:
time: 587 us; the launch traced here: 582 us
  waiting for transfers between devices  296 us (50%)
  matrix products  124 us (21%)
  local copies, waits for them, and re-layouts  56.7 us (10%)
  other arithmetic  46.9 us (8%)
  starting transfers between devices  37.1 us (6%)
  between operations  20.9 us (4%)
    ppermute x12, waiting for transfers between devices, swap(): return lax.ppermute(values, axis, [(0, 1), (1, 0)])  123 us
    reduce_scatter x1, waiting for transfers between devices, on_device_body(): lax.psum_scatter(mlp_grad_pack, ('dp', 'ctx'), scatter_dimension=0, tiled...  107 us
    all_gather x1, waiting for transfers between devices, on_device_body(): attn_full = lax.all_gather(attn_pack, ('dp', 'ctx'), axis=1, tiled=True)  49.6 us
    ppermute x13, starting transfers between devices, tree_sum(): values = jax.tree.map(lambda v: v + lax.ppermute(v, axis, perm), values)  23.7 us
    dot_general x1, matrix products, on_device_body(): jnp.einsum('bhqe,bhke->bhqk', mixed_grad, value_all, preferred_element_ty...  17.4 us
    ppermute x13, waiting for transfers between devices, tree_sum(): values = jax.tree.map(lambda v: v + lax.ppermute(v, axis, perm), values)  16.5 us
    unnamed x136, local copies, waits for them, and re-layouts  14.1 us
    ppermute x12, starting transfers between devices, swap(): return lax.ppermute(values, axis, [(0, 1), (1, 0)])  13.3 us
  transfers between devices with their start and end apart: 29, of which 20 were waited for; matrix products, arithmetic and copies ran while one was open for 25% of the time, Pallas kernels for 0%

profile of v4, /device:TPU:0, one launch (start us, length us, event | category | flops | bytes accessed | tf_op | source)
XLA Modules:
  0.0 581.9 jit_solution(7320008070489721003)
XLA Ops:
  34.7 49.6 %all-gather.3.cloned.1.call-done = bf16[5,1152,576]{2,1,0:T(8,128)(2,1)} async-done(((bf16[5,72,576]{2,1,0:T(8,128)(2,1)}), bf16[5,1152,576]{2,1,0:T(8,128)(2,1)}) %all-gather.3.cloned.1.call-update) | async-done | bytes 6635536 | tf_op jit(solution)/shard_map/all_gather | solution.py:159
  95.2 6.9 %copy.80 = bf16[3,1152,576]{1,2,0:T(8,128)(2,1)} copy(bf16[3,1152,576]{2,1,0:T(8,128)(2,1)} %slice.156) | data formatting | bytes 7962624 | tf_op jit(solution)/shard_map/slice | solution.py:162
  102.5 7.3 %collective-permute-done.4 = bf16[368,1152]{1,0:T(8,128)(2,1)} collective-permute-done((bf16[368,1152]{1,0:T(8,128)(2,1)S(1)}, bf16[368,1152]{1,0:T(8,128)(2,1)}, u32[]{:S(2)}, u32[]{:S(2)}) %collective-permute-start.4) | collective-permute-done | bytes 847904 | tf_op jit(solution)/shard_map/ppermute | solution.py:49
  109.8 6.1 %fusion.30 = bf16[3,2,8,368,72]{3,4,1,2,0:T(8,128)(2,1)S(1)} fusion(f32[3,8,72]{2,1,0:T(8,128)S(1)} %maximum_bitcast_fusion, bf16[3,1152,8,72,1]{1,3,4,2,0:T(8,128)(2,1)} %bitcast.233, bf16[1,368,1152]{2,1,0:T(8,128)(2,1)} %bitcast.18, bf16[1,368,1152]{2,1,0:T(8,128)(2,1)S(1)} %fusion.54), kind=kOutput, calls=%fused_computation.56 | convolution fusion | flops 2936180736 | bytes 8227584 | tf_op jit(solution)/shard_map/pro,tojx->tpjrx/dot_general | solution.py:180
  132.6 6.6 %fusion.73 = bf16[2,8,368,72]{2,3,1,0:T(8,128)(2,1)S(1)} fusion(f32[2,8,368,736]{3,2,1,0:T(8,128)S(1)} %get-tuple-element.64, f32[2,8,368]{2,1,0:T(8,128)S(1)} %log_add_fusion, pred[736]{0:T(1024)(128)(4,1)S(1)} %fusion.105, bf16[2,8,368,72]{2,3,0,1:T(8,128)(2,1)} %collective-permute-done.6, bf16[2,8,368,72]{2,3,0,1:T(8,128)(2,1)S(1)} %copy-done.13), kind=kOutput, calls=%fused_computation.134 | convolution fusion | flops 645183488 | bytes 19902176 | tf_op jit(solution)/shard_map/bhqk,bhke->bhqe/dot_general | solution.py:195
  142.5 19.5 %collective-permute-done.7 = bf16[368,1152]{1,0:T(8,128)(2,1)S(1)} collective-permute-done((bf16[368,1152]{1,0:T(8,128)(2,1)S(1)}, bf16[368,1152]{1,0:T(8,128)(2,1)S(1)}, u32[]{:S(2)}, u32[]{:S(2)}) %collective-permute-start.7) | collective-permute-done | bytes 847904 | tf_op jit(solution)/shard_map/ppermute | solution.py:49
  164.7 18.7 %collective-permute-done.8 = bf16[368,1152]{1,0:T(8,128)(2,1)S(1)} collective-permute-done((bf16[368,1152]{1,0:T(8,128)(2,1)S(1)}, bf16[368,1152]{1,0:T(8,128)(2,1)S(1)}, u32[]{:S(2)}, u32[]{:S(2)}) %collective-permute-start.8) | collective-permute-done | bytes 847904 | tf_op jit(solution)/shard_map/ppermute | solution.py:49
  183.4 10.2 %fusion.9 = (bf16[736,2176]{1,0:T(8,128)(2,1)S(1)}, f32[736,2176]{1,0:T(8,128)}) fusion(f32[2176]{0:T(1024)S(1)} %pad_convert_fusion, bf16[2,1152,2176]{2,1,0:T(8,128)(2,1)} %all-gather.5.cloned.1.call-done, bf16[368,1152]{1,0:T(8,128)(2,1)S(1)} %collective-permute-done.8, bf16[368,1152]{1,0:T(8,128)(2,1)S(1)} %add_convert_fusion.1), kind=kOutput, calls=%fused_computation.20 | convolution fusion | flops 3709345792 | bytes 16327168 | tf_op jit(solution)/shard_map/dot_general | solution.py:207
  198.4 18.1 %collective-permute-done.9 = bf16[368,1152]{1,0:T(8,128)(2,1)} collective-permute-done((bf16[368,1152]{1,0:T(8,128)(2,1)}, bf16[368,1152]{1,0:T(8,128)(2,1)}, u32[]{:S(2)}, u32[]{:S(2)}) %collective-permute-start.9) | collective-permute-done | bytes 847904 | tf_op jit(solution)/shard_map/ppermute | solution.py:49
  216.5 5.8 multiply_convert_fusion.2
  223.9 17.0 %collective-permute-done.10 = bf16[368,1152]{1,0:T(8,128)(2,1)S(1)} collective-permute-done((bf16[368,1152]{1,0:T(8,128)(2,1)S(1)}, bf16[368,1152]{1,0:T(8,128)(2,1)S(1)}, u32[]{:S(2)}, u32[]{:S(2)}) %collective-permute-start.10) | collective-permute-done | bytes 847904 | tf_op jit(solution)/shard_map/ppermute | solution.py:49
  240.9 6.2 %fusion.12 = bf16[368,2176]{1,0:T(8,128)(2,1)S(1)} fusion(bf16[368,1152]{1,0:T(8,128)(2,1)S(1)} %collective-permute-done.10, bf16[2,1152,2176]{2,1,0:T(8,128)(2,1)} %all-gather.5.cloned.1.call-done, f32[736,2176]{1,0:T(8,128)S(1)} %copy-done.52), kind=kOutput, calls=%fused_computation.34 | convolution fusion | flops 1860184064 | bytes 10665984 | tf_op jit(solution)/shard_map/rd,df->rf/dot_general | solution.py:229
  254.9 12.3 %collective-permute-done.11 = bf16[368,1152]{1,0:T(8,128)(2,1)S(1)} collective-permute-done((bf16[368,1152]{1,0:T(8,128)(2,1)S(1)}, bf16[368,1152]{1,0:T(8,128)(2,1)S(1)}, u32[]{:S(2)}, u32[]{:S(2)}) %collective-permute-start.11) | collective-permute-done | bytes 847904 | tf_op jit(solution)/shard_map/ppermute | solution.py:49
  267.3 6.0 %multiply_reduce_fusion.2 = (f32[1152]{0:T(1024)}, f32[368]{0:T(512)S(1)}, f32[368]{0:T(512)S(1)}, f32[1152]{0:T(1024)}, f32[368,1152]{1,0:T(8,128)S(1)}) fusion(f32[368,1152]{1,0:T(8,128)S(1)} %get-tuple-element.41, f32[368]{0:T(512)S(1)} %add_rsqrt_fusion, f32[368]{0:T(512)S(1)} %broadcast_multiply_fusion.4, ...), kind=kOutput, calls=%fused_computation.113 | convolution fusion | flops 1849629696 | bytes 10874112 | tf_op jit(solution)/shard_map/rf,df->rd/dot_general | solution.py:235
  277.2 15.2 %collective-permute-done.12 = bf16[368,1152]{1,0:T(8,128)(2,1)S(1)} collective-permute-done((bf16[368,1152]{1,0:T(8,128)(2,1)S(1)}, bf16[368,1152]{1,0:T(8,128)(2,1)S(1)}, u32[]{:S(2)}, u32[]{:S(2)}) %collective-permute-start.12) | collective-permute-done | bytes 847904 | tf_op jit(solution)/shard_map/ppermute | solution.py:49
  294.8 5.7 fusion.96
  303.5 17.4 %multiply_reduce_fusion = (f32[2,8,368]{2,1,0:T(8,128)S(1)}, f32[2,8,368,736]{3,2,1,0:T(8,128)}) fusion(f32[2,8,368,736]{3,2,1,0:T(8,128)} %copy-done, f32[2,8,368]{2,1,0:T(8,128)S(1)} %log_add_fusion, pred[736]{0:T(1024)(128)(4,1)S(1)} %fusion.105, bf16[2,8,368,72]{2,3,0,1:T(8,128)(2,1)S(1)} %fusion.88, bf16[2,8,368,72]{2,3,0,1:T(8,128)(2,1)} %collective-permute-done.6, ...), kind=kOutput, calls=%fused_computation.1 | convolution fusion | flops 649087232 | bytes 37260000 | tf_op jit(solution)/shard_map/bhqe,bhke->bhqk/dot_general | solution.py:269
  320.9 12.9 %multiply_convert_fusion = bf16[2,8,368,736]{3,2,1,0:T(8,128)(2,1)S(1)} fusion(f32[2,8,368,736]{3,2,1,0:T(8,128)} %get-tuple-element.71, f32[2,8,368,736]{3,2,1,0:T(8,128)} %copy-done, f32[2,8,368]{2,1,0:T(8,128)S(1)} %get-tuple-element.70, f32[2,8,368]{2,1,0:T(8,128)S(1)} %log_add_fusion, pred[736]{0:T(1024)(128)(4,1)S(1)} %fusion.105), kind=kLoop, calls=%fused_computation | loop fusion | flops 26001408 | bytes 43383520 | tf_op jit(solution)/shard_map/convert_element_type | solution.py:274
  345.6 6.9 %convert_reduce_fusion.3 = (f32[8,72]{1,0:T(8,128)S(1)}, bf16[2,8,368,72]{2,3,1,0:T(8,128)(2,1)S(1)}) fusion(bf16[2,8,368,736]{3,2,1,0:T(8,128)(2,1)} %copy-done.3, bf16[2,8,368,72]{2,3,0,1:T(8,128)(2,1)} %collective-permute-done.5, bf16[2,8,368,72]{2,3,0,1:T(8,128)(2,1)} %get-tuple-element.48), kind=kOutput, calls=%fused_computation.79 | convolution fusion | flops 629120448 | bytes 11213056 | tf_op jit(solution)/shard_map/bhqk,bhke->bhqe/dot_general | solution.py:276
  355.4 6.6 %bitcast_convert_fusion = bf16[1152,3,8,72]{0,3,2,1:T(8,128)(2,1)} fusion(bf16[1,368,1152]{2,1,0:T(8,128)(2,1)} %bitcast.18, bf16[1,368,1152]{2,1,0:T(8,128)(2,1)S(1)} %copy-done.29, bf16[1,2,8,368,72]{3,4,2,1,0:T(8,128)(2,1)S(1)} %get-tuple-element.45, bf16[1,2,8,368,72]{3,4,2,1,0:T(8,128)(2,1)S(1)} %fusion.93, bf16[1,2,8,368,72]{3,4,2,1,0:T(8,128)(2,1)S(1)} %bitcast.251), kind=kOutput, calls=%fused_computation.15 | convolution fusion | flops 2943258624 | bytes 8220672 | tf_op jit(solution)/shard_map/okz,toaks->ztas/dot_general | solution.py:291
  362.0 6.9 %copy.93 = bf16[1152,1728]{1,0:T(8,128)(2,1)} copy(bf16[1152,1728]{0,1:T(8,128)(2,1)} %bitcast.235) | data formatting | bytes 7962624 | tf_op jit(solution)/shard_map/convert_element_type | solution.py:296
  398.4 6.2 %convolution_bitcast_fusion.1 = f32[2,368,1152]{2,1,0:T(8,128)S(1)} fusion(bf16[3,1152,8,72,1]{1,3,2,4,0:T(8,128)(2,1)} %bitcast.234, bf16[1,2,8,368,72]{3,4,2,1,0:T(8,128)(2,1)S(1)} %copy-done.27, bf16[1,2,8,368,72]{3,4,2,1,0:T(8,128)(2,1)S(1)} %copy-done.25, bf16[1,2,8,368,72]{3,4,2,1,0:T(8,128)(2,1)} %bitcast.252), kind=kOutput, calls=%fused_computation.38 | convolution fusion | flops 2932789248 | bytes 9916416 | tf_op jit(solution)/shard_map/toaks,tzas->okz/dot_general | solution.py:303
  413.6 14.7 %collective-permute-done.15 = bf16[368,1152]{1,0:T(8,128)(2,1)S(1)} collective-permute-done((bf16[368,1152]{1,0:T(8,128)(2,1)}, bf16[368,1152]{1,0:T(8,128)(2,1)S(1)}, u32[]{:S(2)}, u32[]{:S(2)}) %collective-permute-start.15) | collective-permute-done | bytes 847904 | tf_op jit(solution)/shard_map/ppermute | solution.py:49
  464.2 106.9 %reduce-scatter.5.cloned.1.call-done = bf16[72,4352]{1,0:T(8,128)(2,1)} async-done(((bf16[1152,4352]{1,0:T(8,128)(2,1)}), bf16[72,4352]{1,0:T(8,128)(2,1)}) %reduce-scatter.5.cloned.1.call-update) | async-done | bytes 626704 | tf_op jit(solution)/shard_map/reduce_scatter | solution.py:250
  (275 shorter events, 171.4 us)
Async XLA Ops:
  7.2 77.1 %all-gather.3.cloned.1.call-start = ((), (), s32[]{:S(2)}) async-start(), calls=%async_computation.2 | async-start | bytes 7833600 | tf_op jit(solution)/shard_map/all_gather | solution.py:159
  13.6 169.8 %all-gather.5.cloned.1.call-start = ((), (), s32[]{:S(2)}) async-start(), calls=%async_computation.3 | async-start | bytes 10653696 | tf_op jit(solution)/shard_map/all_gather | solution.py:161
  14.5 446.1 %reduce-scatter.7.cloned.1.call-start = ((), (), s32[]{:S(2)}) async-start(), calls=%async_computation.5 | async-start | bytes 5953536
  14.6 4.7 collective-permute-start
  28.6 4.9 collective-permute-start.3
  88.7 21.2 %collective-permute-start.4 = (bf16[368,1152]{1,0:T(8,128)(2,1)S(1)}, bf16[368,1152]{1,0:T(8,128)(2,1)}, u32[]{:S(2)}, u32[]{:S(2)}) collective-permute-start(bf16[368,1152]{1,0:T(8,128)(2,1)S(1)} %fusion.42), channel_id=1, source_target_pairs={{0,1},{1,0},{2,3},{3,2},{4,5},{5,4},{6,7},{7,6},{8,9},{9,8},{10,11... | collective-permute-start | bytes 2543624 | tf_op jit(solution)/shard_map/ppermute | solution.py:49
  119.2 11.3 %collective-permute-start.6 = (bf16[2,8,368,72]{2,3,0,1:T(8,128)(2,1)}, bf16[2,8,368,72]{2,3,0,1:T(8,128)(2,1)}, u32[]{:S(2)}, u32[]{:S(2)}) collective-permute-start(bf16[2,8,368,72]{2,3,0,1:T(8,128)(2,1)} %get-tuple-element.47), channel_id=1, source_target_pairs={{0,2},{2,0},{1,3},{3,1},{4,6},{6,4},{5,7},{7,5},{8,10},{10,8},{9,1... | collective-permute-start | bytes 2543624 | tf_op jit(solution)/shard_map/ppermute | solution.py:49
  140.9 21.0 %collective-permute-start.7 = (bf16[368,1152]{1,0:T(8,128)(2,1)S(1)}, bf16[368,1152]{1,0:T(8,128)(2,1)S(1)}, u32[]{:S(2)}, u32[]{:S(2)}) collective-permute-start(bf16[368,1152]{1,0:T(8,128)(2,1)S(1)} %fusion.94), channel_id=1, source_target_pairs={{0,1},{1,0},{2,3},{3,2},{4,5},{5,4},{6,7},{7,6},{8,9},{9,8},{10,11... | collective-permute-start | bytes 2543624 | tf_op jit(solution)/shard_map/ppermute | solution.py:49
  163.1 20.2 %collective-permute-start.8 = (bf16[368,1152]{1,0:T(8,128)(2,1)S(1)}, bf16[368,1152]{1,0:T(8,128)(2,1)S(1)}, u32[]{:S(2)}, u32[]{:S(2)}) collective-permute-start(bf16[368,1152]{1,0:T(8,128)(2,1)S(1)} %add_convert_fusion.1), channel_id=1, source_target_pairs={{0,1},{1,0},{2,3},{3,2},{4,5},{5,4},{6,7},{7,6},{8,9},{9,8},{10,11... | collective-permute-start | bytes 2543624 | tf_op jit(solution)/shard_map/ppermute | solution.py:49
  196.9 19.6 %collective-permute-start.9 = (bf16[368,1152]{1,0:T(8,128)(2,1)}, bf16[368,1152]{1,0:T(8,128)(2,1)}, u32[]{:S(2)}, u32[]{:S(2)}) collective-permute-start(bf16[368,1152]{1,0:T(8,128)(2,1)} %fusion.28), channel_id=1, source_target_pairs={{0,1},{1,0},{2,3},{3,2},{4,5},{5,4},{6,7},{7,6},{8,9},{9,8},{10,11... | collective-permute-start | bytes 2543624 | tf_op jit(solution)/shard_map/ppermute | solution.py:49
  222.3 18.5 %collective-permute-start.10 = (bf16[368,1152]{1,0:T(8,128)(2,1)S(1)}, bf16[368,1152]{1,0:T(8,128)(2,1)S(1)}, u32[]{:S(2)}, u32[]{:S(2)}) collective-permute-start(bf16[368,1152]{1,0:T(8,128)(2,1)S(1)} %get-tuple-element.67), channel_id=1, source_target_pairs={{0,1},{1,0},{2,3},{3,2},{4,5},{5,4},{6,7},{7,6},{8,9},{9,8},{10,11... | collective-permute-start | bytes 2543624 | tf_op jit(solution)/shard_map/ppermute | solution.py:49
  249.6 17.7 %collective-permute-start.11 = (bf16[368,1152]{1,0:T(8,128)(2,1)S(1)}, bf16[368,1152]{1,0:T(8,128)(2,1)S(1)}, u32[]{:S(2)}, u32[]{:S(2)}) collective-permute-start(bf16[368,1152]{1,0:T(8,128)(2,1)S(1)} %fusion.29), channel_id=1, source_target_pairs={{0,1},{1,0},{2,3},{3,2},{4,5},{5,4},{6,7},{7,6},{8,9},{9,8},{10,11... | collective-permute-start | bytes 2543624 | tf_op jit(solution)/shard_map/ppermute | solution.py:49
  275.6 16.8 %collective-permute-start.12 = (bf16[368,1152]{1,0:T(8,128)(2,1)S(1)}, bf16[368,1152]{1,0:T(8,128)(2,1)S(1)}, u32[]{:S(2)}, u32[]{:S(2)}) collective-permute-start(bf16[368,1152]{1,0:T(8,128)(2,1)S(1)} %convert_element_type.173), channel_id=1, source_target_pairs={{0,1},{1,0},{2,3},{3,2},{4,5},{5,4},{6,7},{7,6},{8,9},{9,8},{10,11... | collective-permute-start | bytes 2543624 | tf_op jit(solution)/shard_map/ppermute | solution.py:49
  303.5 49.1 %collective-permute-start.14 = (bf16[2,8,368,72]{2,3,1,0:T(8,128)(2,1)}, bf16[2,8,368,72]{2,3,1,0:T(8,128)(2,1)}, u32[]{:S(2)}, u32[]{:S(2)}) collective-permute-start(bf16[2,8,368,72]{2,3,1,0:T(8,128)(2,1)} %slice.271), channel_id=1, source_target_pairs={{0,2},{2,0},{1,3},{3,1},{4,6},{6,4},{5,7},{7,5},{8,10},{10,8},{9,1... | collective-permute-start | bytes 2543624 | tf_op jit(solution)/shard_map/ppermute | solution.py:49
  345.0 9.4 %collective-permute-start.13 = (bf16[2,8,368,72]{2,3,1,0:T(8,128)(2,1)S(1)}, bf16[2,8,368,72]{2,3,1,0:T(8,128)(2,1)S(1)}, u32[]{:S(2)}, u32[]{:S(2)}) collective-permute-start(bf16[2,8,368,72]{2,3,1,0:T(8,128)(2,1)S(1)} %slice.272), channel_id=1, source_target_pairs={{0,2},{2,0},{1,3},{3,1},{4,6},{6,4},{5,7},{7,5},{8,10},{10,8},{9,1... | collective-permute-start | bytes 2543624 | tf_op jit(solution)/shard_map/ppermute | solution.py:49
  374.2 196.9 %reduce-scatter.5.cloned.1.call-start = ((), (), s32[]{:S(2)}) async-start(), calls=%async_computation.4 | async-start | bytes 10653696 | tf_op jit(solution)/shard_map/reduce_scatter | solution.py:250
  407.4 20.9 %collective-permute-start.15 = (bf16[368,1152]{1,0:T(8,128)(2,1)}, bf16[368,1152]{1,0:T(8,128)(2,1)S(1)}, u32[]{:S(2)}, u32[]{:S(2)}) collective-permute-start(bf16[368,1152]{1,0:T(8,128)(2,1)} %fusion.95), channel_id=1, source_target_pairs={{0,1},{1,0},{2,3},{3,2},{4,5},{5,4},{6,7},{7,6},{8,9},{9,8},{10,11... | collective-permute-start | bytes 2543624 | tf_op jit(solution)/shard_map/ppermute | solution.py:49
  412.9 18.0 %collective-permute-start.22 = (f32[3304]{0:T(1024)S(1)}, f32[3304]{0:T(1024)S(1)}, u32[]{:S(2)}, u32[]{:S(2)}) collective-permute-start(f32[3304]{0:T(1024)S(1)} %add.320), channel_id=1, source_target_pairs={{0,4},{4,0},{8,12},{12,8},{16,20},{20,16},{24,28},{28,24},{1,5},{5... | collective-permute-start | bytes 39656 | tf_op jit(solution)/shard_map/ppermute | solution.py:118
  430.8 8.7 %collective-permute-start.16 = (f32[6913]{0:T(1024)S(1)}, f32[6913]{0:T(1024)S(1)}, u32[]{:S(2)}, u32[]{:S(2)}) collective-permute-start(f32[6913]{0:T(1024)S(1)} %constant_dynamic-update-slice_fusion.1), channel_id=1, source_target_pairs={{0,2},{2,0},{1,3},{3,1},{4,6},{6,4},{5,7},{7,5},{8,10},{10,8},{9,1... | collective-permute-start | bytes 82964 | tf_op jit(solution)/shard_map/ppermute | solution.py:118
  434.7 4.7 collective-permute-start.24
  439.5 3.9 collective-permute-start.17
  443.4 5.3 collective-permute-start.18
  448.7 5.3 collective-permute-start.19
  454.0 4.9 collective-permute-start.20
  (66 other events, 860.6 us)
Sparse Core Ops, SparseCore 0:
  13.7 70.6 all-gather.2
  87.1 83.4 all-gather.4
  374.4 80.6 reduce-scatter.6
  459.0 112.0 reduce-scatter.4

commit v5 on v4

--- a/solution.py
+++ b/solution.py
@@ -118,6 +118,32 @@
             values = jax.tree.map(lambda v: v + lax.ppermute(v, axis, perm), values)
             step *= 2
     return values
+
+
+def gather_vectors(block, count):
+    n_ctx = lax.axis_size("ctx")
+    n_dp = lax.axis_size("dp")
+    if n_ctx != 2 or n_dp & (n_dp - 1):
+        gathered = lax.all_gather(block, ("dp", "ctx"), axis=0, tiled=True)
+        return gathered, tree_sum(count, ("tensor", "dp"))
+    count = tree_sum(count, ("tensor",))
+    other = swap(block, "ctx")
+    first = lax.axis_index("ctx") == 0
+    blocks = jnp.where(first, jnp.stack([block, other]), jnp.stack([other, block]))
+    dp_index = lax.axis_index("dp")
+    step = 1
+    while step < n_dp:
+        perm = [(i, i ^ step) for i in range(n_dp)]
+        their_blocks, their_count = lax.ppermute((blocks, count), "dp", perm)
+        low = (dp_index // step) % 2 == 0
+        blocks = jnp.where(
+            low,
+            jnp.concatenate([blocks, their_blocks]),
+            jnp.concatenate([their_blocks, blocks]),
+        )
+        count = count + their_count
+        step *= 2
+    return blocks.reshape(-1, block.shape[1]), count
 
 
 def on_device_body(
@@ -148,20 +174,19 @@
     rows = own_images * half_len
     images = n_t * own_images
 
-    valid_count = tree_sum(jnp.sum(valid_len.astype(jnp.int32)), ("tensor", "dp")).astype(F32)
-    valid_count, tokens = lax.optimization_barrier((valid_count, tokens))
-
     pad_hidden = (-hidden_width) % 128
     pad_out = (-head_width) % 128
     vector_rows = jnp.stack([ln1_gain, ln1_bias, b_o, ln2_gain, ln2_bias, b_down], axis=1)
-    vector_slot = jnp.pad(vector_rows, ((0, 0), (0, head_width - vector_rows.shape[1])))
-    attn_pack = jnp.stack([w_q, w_k, w_v, w_o.T, vector_slot])
+    vectors, valid_count = gather_vectors(vector_rows, jnp.sum(valid_len.astype(jnp.int32)))
+    valid_count = valid_count.astype(F32)
+    valid_count, tokens = lax.optimization_barrier((valid_count, tokens))
+    attn_pack = jnp.stack([w_q, w_k, w_v, w_o.T])
     attn_full = lax.all_gather(attn_pack, ("dp", "ctx"), axis=1, tiled=True)
     mlp_pack = jnp.pad(jnp.stack([w_up, w_down.T]), ((0, 0), (0, 0), (0, pad_hidden)))
     mlp_full = lax.all_gather(mlp_pack, ("dp", "ctx"), axis=1, tiled=True)
     qkv_w = attn_full[:3].reshape(3, width, local_heads, HD)
     out_wt = attn_full[3]
-    vectors = attn_full[4][:, :6].astype(F32)
+    vectors = vectors.astype(F32)
     gain_one, shift_one, out_bias, gain_two, shift_two, down_bias = [
         vectors[:, i] for i in range(6)
     ]

time: 587 us -> 568 us (0.968)
  waiting for transfers between devices: 296 us -> 281 us
  local copies, waits for them, and re-layouts: 56.7 us -> 47.6 us
    all_gather x1, waiting for transfers between devices: 49.6 us -> 26.9 us  [on_device_body(): attn_full = lax.all_gather(attn_pack, ('dp', 'ctx'), axis=1, tiled=True)]
    ppermute x0 -> x6, starting transfers between devices: none -> 18.1 us  [gather_vectors(): their_blocks, their_count = lax.ppermute((blocks, count), 'dp', perm)]
    ppermute x13 -> x10, starting transfers between devices: 23.7 us -> 8.37 us  [tree_sum(): values = jax.tree.map(lambda v: v + lax.ppermute(v, axis, perm), values)]
    unnamed x136 -> x124, local copies, waits for them, and re-layouts: 14.1 us -> 9.58 us
    ppermute x13 -> x10, waiting for transfers between devices: 16.5 us -> 18.1 us  [tree_sum(): values = jax.tree.map(lambda v: v + lax.ppermute(v, axis, perm), values)]
    ppermute x12 -> x13, waiting for transfers between devices: 123 us -> 123 us  [swap(): return lax.ppermute(values, axis, [(0, 1), (1, 0)])]
    ppermute x12 -> x13, starting transfers between devices: 13.3 us -> 13.4 us  [swap(): return lax.ppermute(values, axis, [(0, 1), (1, 0)])]
  transfers between devices with their start and end apart: 29 -> 33, of which waited for: 20 -> 23; matrix products, arithmetic and copies ran while one was open for 25% -> 25% of each run, Pallas kernels for 0% -> 0%
where the time goes in v5:
time: 568 us; the launch traced here: 563 us
  waiting for transfers between devices  281 us (49%)
  matrix products  124 us (22%)
  other arithmetic  49.8 us (9%)
  local copies, waits for them, and re-layouts  47.6 us (8%)
  starting transfers between devices  40.1 us (7%)
  between operations  20.7 us (4%)
    ppermute x13, waiting for transfers between devices, swap(): return lax.ppermute(values, axis, [(0, 1), (1, 0)])  123 us
    reduce_scatter x1, waiting for transfers between devices, on_device_body(): lax.psum_scatter(mlp_grad_pack, ('dp', 'ctx'), scatter_dimension=0, tiled...  107 us
    all_gather x1, waiting for transfers between devices, on_device_body(): attn_full = lax.all_gather(attn_pack, ('dp', 'ctx'), axis=1, tiled=True)  26.9 us
    ppermute x6, starting transfers between devices, gather_vectors(): their_blocks, their_count = lax.ppermute((blocks, count), 'dp', perm)  18.1 us
    ppermute x10, waiting for transfers between devices, tree_sum(): values = jax.tree.map(lambda v: v + lax.ppermute(v, axis, perm), values)  18.1 us
    dot_general x1, matrix products, on_device_body(): jnp.einsum('bhqe,bhke->bhqk', mixed_grad, value_all, preferred_element_ty...  17.4 us
    ppermute x13, starting transfers between devices, swap(): return lax.ppermute(values, axis, [(0, 1), (1, 0)])  13.4 us
    convert_element_type x1, other arithmetic, on_device_body(): score_grad = (soft_full * (soft_grad - inner_sum)).astype(BF)  12.9 us
  transfers between devices with their start and end apart: 33, of which 23 were waited for; matrix products, arithmetic and copies ran while one was open for 25% of the time, Pallas kernels for 0%

profile of v5, /device:TPU:0, one launch (start us, length us, event | category | flops | bytes accessed | tf_op | source)
XLA Modules:
  0.0 563.5 jit_solution(13450693950332628572)
XLA Ops:
  45.9 26.9 %all-gather.3.cloned.1.call-done = bf16[4,1152,576]{2,1,0:T(8,128)(2,1)} async-done(((bf16[4,72,576]{2,1,0:T(8,128)(2,1)}), bf16[4,1152,576]{2,1,0:T(8,128)(2,1)}) %all-gather.3.cloned.1.call-update) | async-done | bytes 5308432 | tf_op jit(solution)/shard_map/all_gather | solution.py:184
  77.6 6.9 %copy.98 = bf16[3,1152,576]{1,2,0:T(8,128)(2,1)} copy(bf16[3,1152,576]{2,1,0:T(8,128)(2,1)} %slice.148) | data formatting | bytes 7962624 | tf_op jit(solution)/shard_map/slice | solution.py:187
  84.5 6.0 %fusion.30 = bf16[3,2,8,368,72]{3,4,1,2,0:T(8,128)(2,1)S(1)} fusion(f32[3,8,72]{2,1,0:T(8,128)S(1)} %maximum_bitcast_fusion, bf16[3,1152,8,72,1]{1,3,4,2,0:T(8,128)(2,1)} %bitcast.229, bf16[1,368,1152]{2,1,0:T(8,128)(2,1)} %bitcast.18, bf16[1,368,1152]{2,1,0:T(8,128)(2,1)S(1)} %fusion.54), kind=kOutput, calls=%fused_computation.56 | convolution fusion | flops 2936180736 | bytes 8227584 | tf_op jit(solution)/shard_map/pro,tojx->tpjrx/dot_general | solution.py:205
  94.9 5.5 fusion
  107.2 6.6 %fusion.73 = bf16[2,8,368,72]{2,3,1,0:T(8,128)(2,1)S(1)} fusion(f32[2,8,368,736]{3,2,1,0:T(8,128)S(1)} %get-tuple-element.62, f32[2,8,368]{2,1,0:T(8,128)S(1)} %log_add_fusion, pred[736]{0:T(1024)(128)(4,1)S(1)} %fusion.106, bf16[2,8,368,72]{2,3,0,1:T(8,128)(2,1)} %collective-permute-done.10, bf16[2,8,368,72]{2,3,0,1:T(8,128)(2,1)S(1)} %copy-done.13), kind=kOutput, calls=%fused_computation.133 | convolution fusion | flops 645183488 | bytes 19902176 | tf_op jit(solution)/shard_map/bhqk,bhke->bhqe/dot_general | solution.py:220
  117.1 19.5 %collective-permute-done.11 = bf16[368,1152]{1,0:T(8,128)(2,1)S(1)} collective-permute-done((bf16[368,1152]{1,0:T(8,128)(2,1)S(1)}, bf16[368,1152]{1,0:T(8,128)(2,1)S(1)}, u32[]{:S(2)}, u32[]{:S(2)}) %collective-permute-start.11) | collective-permute-done | bytes 847904 | tf_op jit(solution)/shard_map/ppermute | solution.py:49
  139.3 18.8 %collective-permute-done.12 = bf16[368,1152]{1,0:T(8,128)(2,1)S(1)} collective-permute-done((bf16[368,1152]{1,0:T(8,128)(2,1)S(1)}, bf16[368,1152]{1,0:T(8,128)(2,1)S(1)}, u32[]{:S(2)}, u32[]{:S(2)}) %collective-permute-start.12) | collective-permute-done | bytes 847904 | tf_op jit(solution)/shard_map/ppermute | solution.py:49
  158.9 9.9 %fusion.9 = (bf16[736,2176]{1,0:T(8,128)(2,1)S(1)}, f32[736,2176]{1,0:T(8,128)}) fusion(f32[2176]{0:T(1024)S(1)} %pad_convert_fusion, bf16[2,1152,2176]{2,1,0:T(8,128)(2,1)} %all-gather.5.cloned.1.call-done, bf16[368,1152]{1,0:T(8,128)(2,1)S(1)} %collective-permute-done.12, bf16[368,1152]{1,0:T(8,128)(2,1)S(1)} %add_convert_fusion.1), kind=kOutput, calls=%fused_computation.20 | convolution fusion | flops 3709345792 | bytes 16327168 | tf_op jit(solution)/shard_map/dot_general | solution.py:232
  173.7 19.8 %collective-permute-done.13 = bf16[368,1152]{1,0:T(8,128)(2,1)} collective-permute-done((bf16[368,1152]{1,0:T(8,128)(2,1)}, bf16[368,1152]{1,0:T(8,128)(2,1)}, u32[]{:S(2)}, u32[]{:S(2)}) %collective-permute-start.13) | collective-permute-done | bytes 847904 | tf_op jit(solution)/shard_map/ppermute | solution.py:49
  193.5 5.8 %multiply_convert_fusion.2 = (bf16[368,1152]{1,0:T(8,128)(2,1)S(1)}, f32[368,1152]{1,0:T(8,128)S(1)}) fusion(f32[368]{0:T(512)S(1)} %fusion.110, bf16[1,368,1152]{2,1,0:T(8,128)(2,1)S(1)} %copy-done.30, f32[1152]{0:T(1024)S(1)} %get-tuple-element.32, f32[368,1152]{1,0:T(8,128)S(1)} %get-tuple-element.41, bf16[368,1152]{1,0:T(8,128)(2,1)} %collective-permute-done.13, ...), kind=kOutput, calls=%fused_computation.132 | convolution fusion | flops 1848360960 | bytes 12556224 | tf_op jit(solution)/shard_map/rf,df->rd/dot_general | solution.py:237
  200.9 18.7 %collective-permute-done.14 = bf16[368,1152]{1,0:T(8,128)(2,1)S(1)} collective-permute-done((bf16[368,1152]{1,0:T(8,128)(2,1)S(1)}, bf16[368,1152]{1,0:T(8,128)(2,1)S(1)}, u32[]{:S(2)}, u32[]{:S(2)}) %collective-permute-start.14) | collective-permute-done | bytes 847904 | tf_op jit(solution)/shard_map/ppermute | solution.py:49
  219.6 6.2 %fusion.12 = bf16[368,2176]{1,0:T(8,128)(2,1)S(1)} fusion(bf16[368,1152]{1,0:T(8,128)(2,1)S(1)} %collective-permute-done.14, bf16[2,1152,2176]{2,1,0:T(8,128)(2,1)} %all-gather.5.cloned.1.call-done, f32[736,2176]{1,0:T(8,128)S(1)} %copy-done.50), kind=kOutput, calls=%fused_computation.34 | convolution fusion | flops 1860184064 | bytes 10665984 | tf_op jit(solution)/shard_map/rd,df->rf/dot_general | solution.py:254
  233.6 14.0 %collective-permute-done.15 = bf16[368,1152]{1,0:T(8,128)(2,1)S(1)} collective-permute-done((bf16[368,1152]{1,0:T(8,128)(2,1)S(1)}, bf16[368,1152]{1,0:T(8,128)(2,1)S(1)}, u32[]{:S(2)}, u32[]{:S(2)}) %collective-permute-start.15) | collective-permute-done | bytes 847904 | tf_op jit(solution)/shard_map/ppermute | solution.py:49
  247.6 6.0 %multiply_reduce_fusion.2 = (f32[1152]{0:T(1024)}, f32[368]{0:T(512)S(1)}, f32[368]{0:T(512)S(1)}, f32[1152]{0:T(1024)}, f32[368,1152]{1,0:T(8,128)S(1)}) fusion(f32[368,1152]{1,0:T(8,128)S(1)} %get-tuple-element.41, f32[368]{0:T(512)S(1)} %add_rsqrt_fusion, f32[368]{0:T(512)S(1)} %broadcast_multiply_fusion.4, ...), kind=kOutput, calls=%fused_computation.113 | convolution fusion | flops 1849629696 | bytes 10874112 | tf_op jit(solution)/shard_map/rf,df->rd/dot_general | solution.py:260
  257.6 16.9 %collective-permute-done.16 = bf16[368,1152]{1,0:T(8,128)(2,1)S(1)} collective-permute-done((bf16[368,1152]{1,0:T(8,128)(2,1)S(1)}, bf16[368,1152]{1,0:T(8,128)(2,1)S(1)}, u32[]{:S(2)}, u32[]{:S(2)}) %collective-permute-start.16) | collective-permute-done | bytes 847904 | tf_op jit(solution)/shard_map/ppermute | solution.py:49
  276.8 5.7 %fusion.96 = f32[2,8,736,72]{2,3,1,0:T(8,128)} fusion(bf16[2,8,368,72]{2,3,0,1:T(8,128)(2,1)S(1)} %fusion.88, f32[2,8,368,736]{3,2,1,0:T(8,128)S(1)} %bitcast.228, f32[2,8,368]{2,1,0:T(8,128)S(1)} %log_add_fusion, pred[736]{0:T(1024)(128)(4,1)S(1)} %fusion.106), kind=kOutput, calls=%fused_computation.151 | convolution fusion | flops 641368064 | bytes 21597920 | tf_op jit(solution)/shard_map/bhqk,bhqe->bhke/dot_general | solution.py:295
  285.5 17.4 %multiply_reduce_fusion = (f32[2,8,368]{2,1,0:T(8,128)S(1)}, f32[2,8,368,736]{3,2,1,0:T(8,128)}) fusion(f32[2,8,368,736]{3,2,1,0:T(8,128)} %copy-done, f32[2,8,368]{2,1,0:T(8,128)S(1)} %log_add_fusion, pred[736]{0:T(1024)(128)(4,1)S(1)} %fusion.106, bf16[2,8,368,72]{2,3,0,1:T(8,128)(2,1)S(1)} %fusion.88, ...), kind=kOutput, calls=%fused_computation.1 | convolution fusion | flops 649087232 | bytes 37260000 | tf_op jit(solution)/shard_map/bhqe,bhke->bhqk/dot_general | solution.py:294
  302.8 12.9 %multiply_convert_fusion = bf16[2,8,368,736]{3,2,1,0:T(8,128)(2,1)S(1)} fusion(f32[2,8,368,736]{3,2,1,0:T(8,128)} %get-tuple-element.69, f32[2,8,368,736]{3,2,1,0:T(8,128)} %copy-done, f32[2,8,368]{2,1,0:T(8,128)S(1)} %get-tuple-element.68, f32[2,8,368]{2,1,0:T(8,128)S(1)} %log_add_fusion, pred[736]{0:T(1024)(128)(4,1)S(1)} %fusion.106), kind=kLoop, calls=%fused_computation | loop fusion | flops 26001408 | bytes 43383520 | tf_op jit(solution)/shard_map/convert_element_type | solution.py:299
  327.5 6.9 %convert_reduce_fusion.3 = (f32[8,72]{1,0:T(8,128)S(1)}, bf16[2,8,368,72]{2,3,1,0:T(8,128)(2,1)S(1)}) fusion(bf16[2,8,368,736]{3,2,1,0:T(8,128)(2,1)} %copy-done.3, bf16[2,8,368,72]{2,3,0,1:T(8,128)(2,1)} %collective-permute-done.9, bf16[2,8,368,72]{2,3,0,1:T(8,128)(2,1)} %get-tuple-element.46), kind=kOutput, calls=%fused_computation.79 | convolution fusion | flops 629120448 | bytes 11213056 | tf_op jit(solution)/shard_map/bhqk,bhke->bhqe/dot_general | solution.py:301
  337.3 6.6 %bitcast_convert_fusion = bf16[1152,3,8,72]{0,3,2,1:T(8,128)(2,1)} fusion(bf16[1,368,1152]{2,1,0:T(8,128)(2,1)} %bitcast.18, bf16[1,368,1152]{2,1,0:T(8,128)(2,1)S(1)} %copy-done.29, bf16[1,2,8,368,72]{3,4,2,1,0:T(8,128)(2,1)S(1)} %get-tuple-element.43, bf16[1,2,8,368,72]{3,4,2,1,0:T(8,128)(2,1)S(1)} %fusion.93, bf16[1,2,8,368,72]{3,4,2,1,0:T(8,128)(2,1)S(1)} %bitcast.253), kind=kOutput, calls=%fused_computation.15 | convolution fusion | flops 2943258624 | bytes 8220672 | tf_op jit(solution)/shard_map/okz,toaks->ztas/dot_general | solution.py:316
  343.9 6.8 %copy.115 = bf16[1152,1728]{1,0:T(8,128)(2,1)} copy(bf16[1152,1728]{0,1:T(8,128)(2,1)} %bitcast.231) | data formatting | bytes 7962624 | tf_op jit(solution)/shard_map/convert_element_type | solution.py:321
  380.3 6.7 %convolution_bitcast_fusion.1 = f32[2,368,1152]{2,1,0:T(8,128)S(1)} fusion(bf16[3,1152,8,72,1]{1,3,2,4,0:T(8,128)(2,1)} %bitcast.230, bf16[1,2,8,368,72]{3,4,2,1,0:T(8,128)(2,1)S(1)} %copy-done.27, bf16[1,2,8,368,72]{3,4,2,1,0:T(8,128)(2,1)S(1)} %copy-done.25, bf16[1,2,8,368,72]{3,4,2,1,0:T(8,128)(2,1)} %bitcast.254), kind=kOutput, calls=%fused_computation.38 | convolution fusion | flops 2932789248 | bytes 9916416 | tf_op jit(solution)/shard_map/toaks,tzas->okz/dot_general | solution.py:328
  395.4 14.9 %collective-permute-done.19 = bf16[368,1152]{1,0:T(8,128)(2,1)S(1)} collective-permute-done((bf16[368,1152]{1,0:T(8,128)(2,1)}, bf16[368,1152]{1,0:T(8,128)(2,1)S(1)}, u32[]{:S(2)}, u32[]{:S(2)}) %collective-permute-start.19) | collective-permute-done | bytes 847904 | tf_op jit(solution)/shard_map/ppermute | solution.py:49
  445.7 106.9 %reduce-scatter.5.cloned.1.call-done = bf16[72,4352]{1,0:T(8,128)(2,1)} async-done(((bf16[1152,4352]{1,0:T(8,128)(2,1)}), bf16[72,4352]{1,0:T(8,128)(2,1)}) %reduce-scatter.5.cloned.1.call-update) | async-done | bytes 626704 | tf_op jit(solution)/shard_map/reduce_scatter | solution.py:275
  (277 shorter events, 170.4 us)
Async XLA Ops:
  7.2 65.6 %all-gather.3.cloned.1.call-start = ((), (), s32[]{:S(2)}) async-start(), calls=%async_computation.2 | async-start | bytes 6266880 | tf_op jit(solution)/shard_map/all_gather | solution.py:184
  9.2 149.7 %all-gather.5.cloned.1.call-start = ((), (), s32[]{:S(2)}) async-start(), calls=%async_computation.3 | async-start | bytes 10653696 | tf_op jit(solution)/shard_map/all_gather | solution.py:186
  11.2 431.0 %reduce-scatter.7.cloned.1.call-start = ((), (), s32[]{:S(2)}) async-start(), calls=%async_computation.5 | async-start | bytes 5953536
  11.2 4.7 collective-permute-start
  15.1 15.5 %collective-permute-start.4 = (bf16[72,6]{0,1:T(8,128)(2,1)S(1)}, bf16[72,6]{0,1:T(8,128)(2,1)S(1)}, u32[]{:S(2)}, u32[]{:S(2)}) collective-permute-start(bf16[72,6]{0,1:T(8,128)(2,1)S(1)} %stack.111), channel_id=1, source_target_pairs={{0,2},{2,0},{1,3},{3,1},{4,6},{6,4},{5,7},{7,5},{8,10},{10,8},{9,1... | collective-permute-start | bytes 2600 | tf_op jit(solution)/shard_map/ppermute | solution.py:49
  38.0 4.7 collective-permute-start.7
  43.3 41.2 %collective-permute-start.8 = (bf16[368,1152]{1,0:T(8,128)(2,1)S(1)}, bf16[368,1152]{1,0:T(8,128)(2,1)}, u32[]{:S(2)}, u32[]{:S(2)}) collective-permute-start(bf16[368,1152]{1,0:T(8,128)(2,1)S(1)} %fusion.42), channel_id=1, source_target_pairs={{0,1},{1,0},{2,3},{3,2},{4,5},{5,4},{6,7},{7,6},{8,9},{9,8},{10,11... | collective-permute-start | bytes 2543624 | tf_op jit(solution)/shard_map/ppermute | solution.py:49
  94.2 11.0 %collective-permute-start.10 = (bf16[2,8,368,72]{2,3,0,1:T(8,128)(2,1)}, bf16[2,8,368,72]{2,3,0,1:T(8,128)(2,1)}, u32[]{:S(2)}, u32[]{:S(2)}) collective-permute-start(bf16[2,8,368,72]{2,3,0,1:T(8,128)(2,1)} %get-tuple-element.45), channel_id=1, source_target_pairs={{0,2},{2,0},{1,3},{3,1},{4,6},{6,4},{5,7},{7,5},{8,10},{10,8},{9,1... | collective-permute-start | bytes 2543624 | tf_op jit(solution)/shard_map/ppermute | solution.py:49
  115.5 21.1 %collective-permute-start.11 = (bf16[368,1152]{1,0:T(8,128)(2,1)S(1)}, bf16[368,1152]{1,0:T(8,128)(2,1)S(1)}, u32[]{:S(2)}, u32[]{:S(2)}) collective-permute-start(bf16[368,1152]{1,0:T(8,128)(2,1)S(1)} %fusion.94), channel_id=1, source_target_pairs={{0,1},{1,0},{2,3},{3,2},{4,5},{5,4},{6,7},{7,6},{8,9},{9,8},{10,11... | collective-permute-start | bytes 2543624 | tf_op jit(solution)/shard_map/ppermute | solution.py:49
  137.8 20.3 %collective-permute-start.12 = (bf16[368,1152]{1,0:T(8,128)(2,1)S(1)}, bf16[368,1152]{1,0:T(8,128)(2,1)S(1)}, u32[]{:S(2)}, u32[]{:S(2)}) collective-permute-start(bf16[368,1152]{1,0:T(8,128)(2,1)S(1)} %add_convert_fusion.1), channel_id=1, source_target_pairs={{0,1},{1,0},{2,3},{3,2},{4,5},{5,4},{6,7},{7,6},{8,9},{9,8},{10,11... | collective-permute-start | bytes 2543624 | tf_op jit(solution)/shard_map/ppermute | solution.py:49
  172.2 21.3 %collective-permute-start.13 = (bf16[368,1152]{1,0:T(8,128)(2,1)}, bf16[368,1152]{1,0:T(8,128)(2,1)}, u32[]{:S(2)}, u32[]{:S(2)}) collective-permute-start(bf16[368,1152]{1,0:T(8,128)(2,1)} %fusion.28), channel_id=1, source_target_pairs={{0,1},{1,0},{2,3},{3,2},{4,5},{5,4},{6,7},{7,6},{8,9},{9,8},{10,11... | collective-permute-start | bytes 2543624 | tf_op jit(solution)/shard_map/ppermute | solution.py:49
  199.3 20.2 %collective-permute-start.14 = (bf16[368,1152]{1,0:T(8,128)(2,1)S(1)}, bf16[368,1152]{1,0:T(8,128)(2,1)S(1)}, u32[]{:S(2)}, u32[]{:S(2)}) collective-permute-start(bf16[368,1152]{1,0:T(8,128)(2,1)S(1)} %get-tuple-element.65), channel_id=1, source_target_pairs={{0,1},{1,0},{2,3},{3,2},{4,5},{5,4},{6,7},{7,6},{8,9},{9,8},{10,11... | collective-permute-start | bytes 2543624 | tf_op jit(solution)/shard_map/ppermute | solution.py:49
  228.3 19.4 %collective-permute-start.15 = (bf16[368,1152]{1,0:T(8,128)(2,1)S(1)}, bf16[368,1152]{1,0:T(8,128)(2,1)S(1)}, u32[]{:S(2)}, u32[]{:S(2)}) collective-permute-start(bf16[368,1152]{1,0:T(8,128)(2,1)S(1)} %fusion.29), channel_id=1, source_target_pairs={{0,1},{1,0},{2,3},{3,2},{4,5},{5,4},{6,7},{7,6},{8,9},{9,8},{10,11... | collective-permute-start | bytes 2543624 | tf_op jit(solution)/shard_map/ppermute | solution.py:49
  256.0 18.5 %collective-permute-start.16 = (bf16[368,1152]{1,0:T(8,128)(2,1)S(1)}, bf16[368,1152]{1,0:T(8,128)(2,1)S(1)}, u32[]{:S(2)}, u32[]{:S(2)}) collective-permute-start(bf16[368,1152]{1,0:T(8,128)(2,1)S(1)} %convert_element_type.175), channel_id=1, source_target_pairs={{0,1},{1,0},{2,3},{3,2},{4,5},{5,4},{6,7},{7,6},{8,9},{9,8},{10,11... | collective-permute-start | bytes 2543624 | tf_op jit(solution)/shard_map/ppermute | solution.py:49
  285.5 49.0 %collective-permute-start.18 = (bf16[2,8,368,72]{2,3,1,0:T(8,128)(2,1)}, bf16[2,8,368,72]{2,3,1,0:T(8,128)(2,1)}, u32[]{:S(2)}, u32[]{:S(2)}) collective-permute-start(bf16[2,8,368,72]{2,3,1,0:T(8,128)(2,1)} %slice.259), channel_id=1, source_target_pairs={{0,2},{2,0},{1,3},{3,1},{4,6},{6,4},{5,7},{7,5},{8,10},{10,8},{9,1... | collective-permute-start | bytes 2543624 | tf_op jit(solution)/shard_map/ppermute | solution.py:49
  327.0 9.4 %collective-permute-start.17 = (bf16[2,8,368,72]{2,3,1,0:T(8,128)(2,1)S(1)}, bf16[2,8,368,72]{2,3,1,0:T(8,128)(2,1)S(1)}, u32[]{:S(2)}, u32[]{:S(2)}) collective-permute-start(bf16[2,8,368,72]{2,3,1,0:T(8,128)(2,1)S(1)} %slice.260), channel_id=1, source_target_pairs={{0,2},{2,0},{1,3},{3,1},{4,6},{6,4},{5,7},{7,5},{8,10},{10,8},{9,1... | collective-permute-start | bytes 2543624 | tf_op jit(solution)/shard_map/ppermute | solution.py:49
  356.1 196.5 %reduce-scatter.5.cloned.1.call-start = ((), (), s32[]{:S(2)}) async-start(), calls=%async_computation.4 | async-start | bytes 10653696 | tf_op jit(solution)/shard_map/reduce_scatter | solution.py:275
  389.7 20.6 %collective-permute-start.19 = (bf16[368,1152]{1,0:T(8,128)(2,1)}, bf16[368,1152]{1,0:T(8,128)(2,1)S(1)}, u32[]{:S(2)}, u32[]{:S(2)}) collective-permute-start(bf16[368,1152]{1,0:T(8,128)(2,1)} %fusion.95), channel_id=1, source_target_pairs={{0,1},{1,0},{2,3},{3,2},{4,5},{5,4},{6,7},{7,6},{8,9},{9,8},{10,11... | collective-permute-start | bytes 2543624 | tf_op jit(solution)/shard_map/ppermute | solution.py:49
  394.9 18.0 %collective-permute-start.26 = (f32[3304]{0:T(1024)S(1)}, f32[3304]{0:T(1024)S(1)}, u32[]{:S(2)}, u32[]{:S(2)}) collective-permute-start(f32[3304]{0:T(1024)S(1)} %add.334), channel_id=1, source_target_pairs={{0,4},{4,0},{8,12},{12,8},{16,20},{20,16},{24,28},{28,24},{1,5},{5... | collective-permute-start | bytes 39656 | tf_op jit(solution)/shard_map/ppermute | solution.py:118
  412.8 9.0 %collective-permute-start.20 = (f32[6913]{0:T(1024)S(1)}, f32[6913]{0:T(1024)S(1)}, u32[]{:S(2)}, u32[]{:S(2)}) collective-permute-start(f32[6913]{0:T(1024)S(1)} %constant_dynamic-update-slice_fusion), channel_id=1, source_target_pairs={{0,2},{2,0},{1,3},{3,1},{4,6},{6,4},{5,7},{7,5},{8,10},{10,8},{9,1... | collective-permute-start | bytes 82964 | tf_op jit(solution)/shard_map/ppermute | solution.py:118
  416.7 5.1 collective-permute-start.28
  425.8 5.1 collective-permute-start.22
  430.9 4.8 collective-permute-start.23
  435.7 4.6 collective-permute-start.24
  (69 other events, 940.0 us)
Sparse Core Ops, SparseCore 0:
  10.8 61.9 all-gather.2
  75.6 83.2 all-gather.4
  356.2 79.5 reduce-scatter.6
  439.8 112.7 reduce-scatter.4

commit v6 on v5

--- a/solution.py
+++ b/solution.py
@@ -74,11 +74,6 @@
     return lax.psum_scatter(
         jnp.stack(parts).astype(BF), "tensor", scatter_dimension=0
     ).astype(F32)
-
-
-def split_rows(values, count):
-    size = values.shape[0] // count
-    return [values[i * size : (i + 1) * size] for i in range(count)]
 
 
 def ctx_gather(values):
@@ -144,6 +139,35 @@
         count = count + their_count
         step *= 2
     return blocks.reshape(-1, block.shape[1]), count
+
+
+def halving_reduce_scatter(values):
+    n_ctx = lax.axis_size("ctx")
+    n_dp = lax.axis_size("dp")
+    if n_ctx != 2 or n_dp & (n_dp - 1):
+        return lax.psum_scatter(
+            values.astype(BF), ("dp", "ctx"), scatter_dimension=0, tiled=True
+        ).astype(F32)
+    total, cols = values.shape
+    piece = total // (n_dp * n_ctx)
+    acc = values.reshape(n_dp, 2, piece, cols)
+    me = lax.axis_index("ctx")
+    keep = lax.dynamic_index_in_dim(acc, me, axis=1, keepdims=False)
+    send = lax.dynamic_index_in_dim(acc, 1 - me, axis=1, keepdims=False).astype(BF)
+    acc = keep + swap(send, "ctx").astype(F32)
+    dp_index = lax.axis_index("dp")
+    groups = n_dp
+    step = 1
+    while step < n_dp:
+        acc = acc.reshape(groups // 2, 2, piece, cols)
+        bit = (dp_index // step) % 2
+        keep = lax.dynamic_index_in_dim(acc, bit, axis=1, keepdims=False)
+        send = lax.dynamic_index_in_dim(acc, 1 - bit, axis=1, keepdims=False).astype(BF)
+        perm = [(i, i ^ step) for i in range(n_dp)]
+        acc = keep + lax.ppermute(send, "dp", perm).astype(F32)
+        groups //= 2
+        step *= 2
+    return acc.reshape(piece, cols)
 
 
 def on_device_body(
@@ -228,11 +252,10 @@
     hidden = inputs + attn_sum + out_bias
     normed_two, unit_two, inverse_two = norm_forward(hidden, gain_two, shift_two)
     normed_two_parts = tensor_gather_parts(normed_two.astype(BF))
-    normed_two_all = jnp.concatenate(normed_two_parts)
-    before = jnp.dot(normed_two_all, up_w, preferred_element_type=F32) + up_b
-    active = gelu_tanh(before).astype(BF)
-    before_parts = split_rows(before, n_t)
-    active_parts = split_rows(active, n_t)
+    before_parts = [
+        jnp.dot(part, up_w, preferred_element_type=F32) + up_b for part in normed_two_parts
+    ]
+    active_parts = [gelu_tanh(part).astype(BF) for part in before_parts]
     mlp_terms = [
         jnp.einsum("rf,df->rd", part, down_wt, preferred_element_type=F32)
         for part in active_parts
@@ -316,14 +339,8 @@
     qkv_weight_grad = jnp.einsum(
         "okz,toaks->ztas", normed_every_row, qkv_grads, preferred_element_type=F32
     ).reshape(width, 3 * head_width)
-    attn_grads = lax.psum_scatter(
-        jnp.concatenate(
-            [jnp.pad(out_grad_t.astype(BF), ((0, 0), (0, pad_out))), qkv_weight_grad.astype(BF)],
-            axis=1,
-        ),
-        ("dp", "ctx"),
-        scatter_dimension=0,
-        tiled=True,
+    attn_grads = halving_reduce_scatter(
+        jnp.concatenate([jnp.pad(out_grad_t, ((0, 0), (0, pad_out))), qkv_weight_grad], axis=1)
     )
     norm_one_terms = jnp.einsum(
         "toaks,tzas->okz", qkv_grads, qkv_w, preferred_element_type=F32
@@ -356,7 +373,6 @@
     query_bias_sum = head_sums[:head_width]
     value_bias_sum = head_sums[head_width : 2 * head_width]
     up_bias_sum = head_sums[2 * head_width :]
-    attn_grads = attn_grads.astype(F32)
     mlp_grads = mlp_grads.astype(F32)
     out_cols = head_width + pad_out
     attn_grads = [

time: 568 us -> 534 us (0.940)
  waiting for transfers between devices: 281 us -> 177 us
  local copies, waits for them, and re-layouts: 47.6 us -> 92.6 us
  matrix products: 124 us -> 136 us
  other arithmetic: 49.8 us -> 56.9 us
  starting transfers between devices: 40.1 us -> 46.3 us
    reduce_scatter x1, waiting for transfers between devices: 107 us -> 0.01 us  [on_device_body(): lax.psum_scatter(mlp_grad_pack, ('dp', 'ctx'), scatter_dimension=0, tiled...]
    concatenate x0 -> x2, local copies, waits for them, and re-layouts: none -> 48.2 us  [on_device_body(): jnp.concatenate([jnp.pad(out_grad_t, ((0, 0), (0, pad_out))), qkv_weight_...]
    ppermute x13 -> x14, waiting for transfers between devices: 123 us -> 82.3 us  [swap(): return lax.ppermute(values, axis, [(0, 1), (1, 0)])]
    ppermute x10, waiting for transfers between devices: 18.1 us -> 50 us  [tree_sum(): values = jax.tree.map(lambda v: v + lax.ppermute(v, axis, perm), values)]
    ppermute x0 -> x3, waiting for transfers between devices: none -> 10.9 us  [halving_reduce_scatter(): acc = keep + lax.ppermute(send, 'dp', perm).astype(F32)]
    convert_element_type x2 -> x3, local copies, waits for them, and re-layouts: 8.92 us -> 2.27 us  [halving_reduce_scatter(): lax.dynamic_index_in_dim(acc, 1 - bit, axis=1, keepdims=False).astype(BF)]
    add x0 -> x3, other arithmetic: none -> 5.99 us  [the longest x2 3.6 us: halving_reduce_scatter(): acc = keep + lax.ppermute(send, 'dp', perm).astype(F32)]
    unnamed x124 -> x128, local copies, waits for them, and re-layouts: 9.58 us -> 12.2 us
  transfers between devices with their start and end apart: 33 -> 36, of which waited for: 23 -> 23; matrix products, arithmetic and copies ran while one was open for 25% -> 43% of each run, Pallas kernels for 0% -> 0%
where the time goes in v6:
time: 534 us; the launch traced here: 529 us
  waiting for transfers between devices  177 us (33%)
  matrix products  136 us (25%)
  local copies, waits for them, and re-layouts  92.6 us (17%)
  other arithmetic  56.9 us (11%)
  starting transfers between devices  46.3 us (9%)
  between operations  20.4 us (4%)
    ppermute x14, waiting for transfers between devices, swap(): return lax.ppermute(values, axis, [(0, 1), (1, 0)])  82.3 us
    ppermute x10, waiting for transfers between devices, tree_sum(): values = jax.tree.map(lambda v: v + lax.ppermute(v, axis, perm), values)  50 us
    concatenate x2, local copies, waits for them, and re-layouts, on_device_body(): jnp.concatenate([jnp.pad(out_grad_t, ((0, 0), (0, pad_out))), qkv_weight_...  48.2 us
    all_gather x1, waiting for transfers between devices, on_device_body(): attn_full = lax.all_gather(attn_pack, ('dp', 'ctx'), axis=1, tiled=True)  26.6 us
    ppermute x6, starting transfers between devices, gather_vectors(): their_blocks, their_count = lax.ppermute((blocks, count), 'dp', perm)  17.8 us
    dot_general x1, matrix products, on_device_body(): jnp.einsum('bhqe,bhke->bhqk', mixed_grad, value_all, preferred_element_ty...  17.7 us
    ppermute x14, starting transfers between devices, swap(): return lax.ppermute(values, axis, [(0, 1), (1, 0)])  13.3 us
    convert_element_type x1, other arithmetic, on_device_body(): score_grad = (soft_full * (soft_grad - inner_sum)).astype(BF)  13.3 us
  transfers between devices with their start and end apart: 36, of which 23 were waited for; matrix products, arithmetic and copies ran while one was open for 43% of the time, Pallas kernels for 0%

profile of v6, /device:TPU:0, one launch (start us, length us, event | category | flops | bytes accessed | tf_op | source)
XLA Modules:
  0.0 529.5 jit_solution(7750568382308529565)
XLA Ops:
  46.2 26.6 %all-gather.3.cloned.1.call-done = bf16[4,1152,576]{2,1,0:T(8,128)(2,1)} async-done(((bf16[4,72,576]{2,1,0:T(8,128)(2,1)}), bf16[4,1152,576]{2,1,0:T(8,128)(2,1)}) %all-gather.3.cloned.1.call-update) | async-done | bytes 5308432 | tf_op jit(solution)/shard_map/all_gather | solution.py:208
  77.6 7.0 %copy.83 = bf16[3,1152,576]{1,2,0:T(8,128)(2,1)} copy(bf16[3,1152,576]{2,1,0:T(8,128)(2,1)} %slice.132) | data formatting | bytes 7962624 | tf_op jit(solution)/shard_map/slice | solution.py:211
  84.6 6.0 %fusion.28 = bf16[3,2,8,368,72]{3,4,1,2,0:T(8,128)(2,1)S(1)} fusion(f32[3,8,72]{2,1,0:T(8,128)S(1)} %maximum_bitcast_fusion, bf16[3,1152,8,72,1]{1,3,4,2,0:T(8,128)(2,1)} %bitcast.259, bf16[1,368,1152]{2,1,0:T(8,128)(2,1)} %bitcast.18, bf16[1,368,1152]{2,1,0:T(8,128)(2,1)S(1)} %fusion.52), kind=kOutput, calls=%fused_computation.60 | convolution fusion | flops 2936180736 | bytes 8227584 | tf_op jit(solution)/shard_map/pro,tojx->tpjrx/dot_general | solution.py:229
  107.2 6.2 %fusion.69 = bf16[2,8,368,72]{2,3,1,0:T(8,128)(2,1)S(1)} fusion(f32[2,8,368,736]{3,2,1,0:T(8,128)S(1)} %get-tuple-element.63, f32[2,8,368]{2,1,0:T(8,128)S(1)} %log_add_fusion, pred[736]{0:T(1024)(128)(4,1)S(1)} %fusion.97, bf16[2,8,368,72]{2,3,0,1:T(8,128)(2,1)} %collective-permute-done.10, bf16[2,8,368,72]{2,3,0,1:T(8,128)(2,1)S(1)} %copy-done.20), kind=kOutput, calls=%fused_computation.135 | convolution fusion | flops 645183488 | bytes 19902176 | tf_op jit(solution)/shard_map/bhqk,bhke->bhqe/dot_general | solution.py:244
  116.8 19.5 %collective-permute-done.11 = bf16[368,1152]{1,0:T(8,128)(2,1)S(1)} collective-permute-done((bf16[368,1152]{1,0:T(8,128)(2,1)S(1)}, bf16[368,1152]{1,0:T(8,128)(2,1)S(1)}, u32[]{:S(2)}, u32[]{:S(2)}) %collective-permute-start.11) | collective-permute-done | bytes 847904 | tf_op jit(solution)/shard_map/ppermute | solution.py:49
  139.0 18.8 %collective-permute-done.12 = bf16[368,1152]{1,0:T(8,128)(2,1)S(1)} collective-permute-done((bf16[368,1152]{1,0:T(8,128)(2,1)S(1)}, bf16[368,1152]{1,0:T(8,128)(2,1)S(1)}, u32[]{:S(2)}, u32[]{:S(2)}) %collective-permute-start.12) | collective-permute-done | bytes 847904 | tf_op jit(solution)/shard_map/ppermute | solution.py:49
  174.6 14.7 %collective-permute-done.13 = bf16[368,1152]{1,0:T(8,128)(2,1)S(1)} collective-permute-done((bf16[368,1152]{1,0:T(8,128)(2,1)}, bf16[368,1152]{1,0:T(8,128)(2,1)S(1)}, u32[]{:S(2)}, u32[]{:S(2)}) %collective-permute-start.13) | collective-permute-done | bytes 847904 | tf_op jit(solution)/shard_map/ppermute | solution.py:49
  189.3 6.5 %multiply_convert_fusion.4 = (bf16[368,1152]{1,0:T(8,128)(2,1)S(1)}, f32[368,1152]{1,0:T(8,128)}) fusion(f32[368]{0:T(512)S(1)} %fusion.101, bf16[1,368,1152]{2,1,0:T(8,128)(2,1)S(1)} %copy-done.36, f32[1152]{0:T(1024)S(1)} %get-tuple-element.32, f32[368,1152]{1,0:T(8,128)S(1)} %get-tuple-element.41, bf16[368,1152]{1,0:T(8,128)(2,1)S(1)} %collective-permute-done.13, ...), kind=kOutput, calls=%fused_computation.134 | convolution fusion | flops 1855567872 | bytes 14157760 | tf_op jit(solution)/shard_map/rf,df->rd/dot_general | solution.py:260
  207.4 8.5 %collective-permute-done.14 = bf16[368,1152]{1,0:T(8,128)(2,1)S(1)} collective-permute-done((bf16[368,1152]{1,0:T(8,128)(2,1)S(1)}, bf16[368,1152]{1,0:T(8,128)(2,1)S(1)}, u32[]{:S(2)}, u32[]{:S(2)}) %collective-permute-start.14) | collective-permute-done | bytes 847904 | tf_op jit(solution)/shard_map/ppermute | solution.py:49
  215.9 6.0 %fusion.10 = bf16[368,2176]{1,0:T(8,128)(2,1)S(1)} fusion(bf16[368,1152]{1,0:T(8,128)(2,1)S(1)} %collective-permute-done.14, bf16[2,1152,2176]{2,1,0:T(8,128)(2,1)} %all-gather.5.cloned.1.call-done, f32[368,2176]{1,0:T(8,128)S(1)} %copy-done.23), kind=kOutput, calls=%fused_computation.35 | convolution fusion | flops 1860184064 | bytes 10665984 | tf_op jit(solution)/shard_map/rd,df->rf/dot_general | solution.py:277
  222.0 6.3 %fusion.27 = bf16[368,1152]{1,0:T(8,128)(2,1)} fusion(bf16[368,2176]{1,0:T(8,128)(2,1)S(1)} %fusion.10, bf16[2,1152,2176]{2,1,0:T(8,128)(2,1)} %all-gather.5.cloned.1.call-done), kind=kOutput, calls=%fused_computation.59 | convolution fusion | flops 1845393408 | bytes 7462912 | tf_op jit(solution)/shard_map/rf,df->rd/dot_general | solution.py:283
  240.3 7.7 %collective-permute-done.15 = bf16[368,1152]{1,0:T(8,128)(2,1)} collective-permute-done((bf16[368,1152]{1,0:T(8,128)(2,1)}, bf16[368,1152]{1,0:T(8,128)(2,1)}, u32[]{:S(2)}, u32[]{:S(2)}) %collective-permute-start.15) | collective-permute-done | bytes 847904 | tf_op jit(solution)/shard_map/ppermute | solution.py:49
  265.2 12.6 %collective-permute-done.16 = bf16[368,1152]{1,0:T(8,128)(2,1)} collective-permute-done((bf16[368,1152]{1,0:T(8,128)(2,1)}, bf16[368,1152]{1,0:T(8,128)(2,1)}, u32[]{:S(2)}, u32[]{:S(2)}) %collective-permute-start.16) | collective-permute-done | bytes 847904 | tf_op jit(solution)/shard_map/ppermute | solution.py:49
  280.5 9.2 %fusion.86 = f32[2,8,736,72]{2,3,1,0:T(8,128)S(1)} fusion(bf16[2,8,368,72]{2,3,0,1:T(8,128)(2,1)S(1)} %fusion.78, f32[2,8,368,736]{3,2,1,0:T(8,128)} %copy-done, f32[2,8,368]{2,1,0:T(8,128)S(1)} %log_add_fusion, pred[736]{0:T(1024)(128)(4,1)S(1)} %fusion.97), kind=kOutput, calls=%fused_computation.151 | convolution fusion | flops 641368064 | bytes 21597920 | tf_op jit(solution)/shard_map/bhqk,bhqe->bhke/dot_general | solution.py:318
  292.9 17.7 %multiply_reduce_fusion = (f32[2,8,368]{2,1,0:T(8,128)S(1)}, f32[2,8,368,736]{3,2,1,0:T(8,128)}) fusion(f32[2,8,368,736]{3,2,1,0:T(8,128)} %copy-done, f32[2,8,368]{2,1,0:T(8,128)S(1)} %log_add_fusion, pred[736]{0:T(1024)(128)(4,1)S(1)} %fusion.97, bf16[2,8,368,72]{2,3,0,1:T(8,128)(2,1)S(1)} %fusion.78, bf16[2,8,368,72]{2,3,0,1:T(8,128)(2,1)} %collective-permute-done.10, ...), kind=kOutput, calls=%fused_computation.1 | convolution fusion | flops 649087232 | bytes 37260000 | tf_op jit(solution)/shard_map/bhqe,bhke->bhqk/dot_general | solution.py:317
  310.6 13.3 %multiply_convert_fusion = bf16[2,8,368,736]{3,2,1,0:T(8,128)(2,1)S(1)} fusion(f32[2,8,368,736]{3,2,1,0:T(8,128)} %get-tuple-element.68, f32[2,8,368,736]{3,2,1,0:T(8,128)} %copy-done, f32[2,8,368]{2,1,0:T(8,128)S(1)} %get-tuple-element.67, f32[2,8,368]{2,1,0:T(8,128)S(1)} %log_add_fusion, pred[736]{0:T(1024)(128)(4,1)S(1)} %fusion.97), kind=kLoop, calls=%fused_computation | loop fusion | flops 26001408 | bytes 43383520 | tf_op jit(solution)/shard_map/convert_element_type | solution.py:322
  338.0 7.8 %convert_reduce_fusion.3 = (f32[8,72]{1,0:T(8,128)S(1)}, bf16[2,8,368,72]{2,3,1,0:T(8,128)(2,1)}) fusion(bf16[2,8,368,736]{3,2,1,0:T(8,128)(2,1)} %copy-done.3, bf16[2,8,368,72]{2,3,0,1:T(8,128)(2,1)} %collective-permute-done.9, bf16[2,8,368,72]{2,3,0,1:T(8,128)(2,1)} %get-tuple-element.46), kind=kOutput, calls=%fused_computation.83 | convolution fusion | flops 629120448 | bytes 11213056 | tf_op jit(solution)/shard_map/bhqk,bhke->bhqe/dot_general | solution.py:324
  350.2 7.1 %convolution_bitcast_fusion = f32[1152,3,8,72]{0,3,2,1:T(8,128)} fusion(bf16[1,368,1152]{2,1,0:T(8,128)(2,1)} %bitcast.18, bf16[1,368,1152]{2,1,0:T(8,128)(2,1)S(1)} %copy-done.35, bf16[1,2,8,368,72]{3,4,2,1,0:T(8,128)(2,1)S(1)} %get-tuple-element.43, bf16[1,2,8,368,72]{3,4,2,1,0:T(8,128)(2,1)S(1)} %fusion.83, bf16[1,2,8,368,72]{3,4,2,1,0:T(8,128)(2,1)S(1)} %bitcast.281), kind=kOutput, calls=%fused_computation.17 | convolution fusion | flops 2941267968 | bytes 12201984 | tf_op jit(solution)/shard_map/okz,toaks->ztas/dot_general | solution.py:339
  357.4 29.3 %reshape.232 = f32[8,2,72,1728]{2,1,0,3:T(2,128)} reshape(f32[1152,3,8,72]{0,3,2,1:T(8,128)} %convolution_bitcast_fusion) | data formatting | bytes 15925248 | tf_op jit(solution)/shard_map/concatenate | solution.py:343
  386.6 18.9 %copy.110 = f32[8,2,72,1728]{3,2,1,0:T(8,128)} copy(f32[8,2,72,1728]{2,1,0,3:T(2,128)} %reshape.232) | data formatting | bytes 15925248 | tf_op jit(solution)/shard_map/concatenate | solution.py:343
  409.5 6.8 %convolution_bitcast_fusion.2 = f32[2,368,1152]{2,1,0:T(8,128)S(1)} fusion(bf16[3,1152,8,72,1]{1,3,2,4,0:T(8,128)(2,1)} %bitcast.260, bf16[1,2,8,368,72]{3,4,2,1,0:T(8,128)(2,1)} %copy-done.33, bf16[1,2,8,368,72]{3,4,2,1,0:T(8,128)(2,1)} %copy-done.32, bf16[1,2,8,368,72]{3,4,2,1,0:T(8,128)(2,1)} %bitcast.280), kind=kOutput, calls=%fused_computation.37 | convolution fusion | flops 2932789248 | bytes 9916416 | tf_op jit(solution)/shard_map/toaks,tzas->okz/dot_general | solution.py:345
  429.7 29.3 %collective-permute-done.30 = f32[3304]{0:T(1024)S(1)} collective-permute-done((f32[3304]{0:T(1024)S(1)}, f32[3304]{0:T(1024)S(1)}, u32[]{:S(2)}, u32[]{:S(2)}) %collective-permute-start.30) | collective-permute-done | bytes 13248 | tf_op jit(solution)/shard_map/ppermute | solution.py:113
  478.2 12.9 %collective-permute-done.22 = f32[6913]{0:T(1024)S(1)} collective-permute-done((f32[6913]{0:T(1024)S(1)}, f32[6913]{0:T(1024)S(1)}, u32[]{:S(2)}, u32[]{:S(2)}) %collective-permute-start.22) | collective-permute-done | bytes 27684 | tf_op jit(solution)/shard_map/ppermute | solution.py:113
  505.7 10.9 %collective-permute-done.28 = bf16[1,72,2368]{2,1,0:T(8,128)(2,1)S(1)} collective-permute-done((bf16[1,72,2368]{2,1,0:T(8,128)(2,1)S(1)}, bf16[1,72,2368]{2,1,0:T(8,128)(2,1)S(1)}, u32[]{:S(2)}, u32[]{:S(2)}) %collective-permute-start.28) | collective-permute-done | bytes 341024 | tf_op jit(solution)/shard_map/ppermute | solution.py:167
  (294 shorter events, 199.5 us)
Async XLA Ops:
  7.2 65.6 %all-gather.3.cloned.1.call-start = ((), (), s32[]{:S(2)}) async-start(), calls=%async_computation.1 | async-start | bytes 6266880 | tf_op jit(solution)/shard_map/all_gather | solution.py:208
  9.2 149.7 %all-gather.5.cloned.1.call-start = ((), (), s32[]{:S(2)}) async-start(), calls=%async_computation.2 | async-start | bytes 10653696 | tf_op jit(solution)/shard_map/all_gather | solution.py:210
  11.2 507.5 %reduce-scatter.2.cloned.1.call-start = ((), (), s32[]{:S(2)}) async-start(), calls=%async_computation.3 | async-start | bytes 10653696 | tf_op jit(solution)/shard_map/reduce_scatter | solution.py:298
  15.1 15.9 %collective-permute-start.4 = (bf16[72,6]{0,1:T(8,128)(2,1)S(1)}, bf16[72,6]{0,1:T(8,128)(2,1)S(1)}, u32[]{:S(2)}, u32[]{:S(2)}) collective-permute-start(bf16[72,6]{0,1:T(8,128)(2,1)S(1)} %stack.111), channel_id=1, source_target_pairs={{0,2},{2,0},{1,3},{3,1},{4,6},{6,4},{5,7},{7,5},{8,10},{10,8},{9,1... | collective-permute-start | bytes 2600 | tf_op jit(solution)/shard_map/ppermute | solution.py:49
  43.7 40.9 %collective-permute-start.8 = (bf16[368,1152]{1,0:T(8,128)(2,1)S(1)}, bf16[368,1152]{1,0:T(8,128)(2,1)}, u32[]{:S(2)}, u32[]{:S(2)}) collective-permute-start(bf16[368,1152]{1,0:T(8,128)(2,1)S(1)} %fusion.40), channel_id=1, source_target_pairs={{0,1},{1,0},{2,3},{3,2},{4,5},{5,4},{6,7},{7,6},{8,9},{9,8},{10,11... | collective-permute-start | bytes 2543624 | tf_op jit(solution)/shard_map/ppermute | solution.py:49
  94.3 11.0 %collective-permute-start.10 = (bf16[2,8,368,72]{2,3,0,1:T(8,128)(2,1)}, bf16[2,8,368,72]{2,3,0,1:T(8,128)(2,1)}, u32[]{:S(2)}, u32[]{:S(2)}) collective-permute-start(bf16[2,8,368,72]{2,3,0,1:T(8,128)(2,1)} %get-tuple-element.45), channel_id=1, source_target_pairs={{0,2},{2,0},{1,3},{3,1},{4,6},{6,4},{5,7},{7,5},{8,10},{10,8},{9,1... | collective-permute-start | bytes 2543624 | tf_op jit(solution)/shard_map/ppermute | solution.py:49
  115.2 21.1 %collective-permute-start.11 = (bf16[368,1152]{1,0:T(8,128)(2,1)S(1)}, bf16[368,1152]{1,0:T(8,128)(2,1)S(1)}, u32[]{:S(2)}, u32[]{:S(2)}) collective-permute-start(bf16[368,1152]{1,0:T(8,128)(2,1)S(1)} %fusion.84), channel_id=1, source_target_pairs={{0,1},{1,0},{2,3},{3,2},{4,5},{5,4},{6,7},{7,6},{8,9},{9,8},{10,11... | collective-permute-start | bytes 2543624 | tf_op jit(solution)/shard_map/ppermute | solution.py:49
  137.5 20.3 %collective-permute-start.12 = (bf16[368,1152]{1,0:T(8,128)(2,1)S(1)}, bf16[368,1152]{1,0:T(8,128)(2,1)S(1)}, u32[]{:S(2)}, u32[]{:S(2)}) collective-permute-start(bf16[368,1152]{1,0:T(8,128)(2,1)S(1)} %add_convert_fusion.1), channel_id=1, source_target_pairs={{0,1},{1,0},{2,3},{3,2},{4,5},{5,4},{6,7},{7,6},{8,9},{9,8},{10,11... | collective-permute-start | bytes 2543624 | tf_op jit(solution)/shard_map/ppermute | solution.py:49
  168.1 21.2 %collective-permute-start.13 = (bf16[368,1152]{1,0:T(8,128)(2,1)}, bf16[368,1152]{1,0:T(8,128)(2,1)S(1)}, u32[]{:S(2)}, u32[]{:S(2)}) collective-permute-start(bf16[368,1152]{1,0:T(8,128)(2,1)} %fusion.26), channel_id=1, source_target_pairs={{0,1},{1,0},{2,3},{3,2},{4,5},{5,4},{6,7},{7,6},{8,9},{9,8},{10,11... | collective-permute-start | bytes 2543624 | tf_op jit(solution)/shard_map/ppermute | solution.py:49
  195.8 20.2 %collective-permute-start.14 = (bf16[368,1152]{1,0:T(8,128)(2,1)S(1)}, bf16[368,1152]{1,0:T(8,128)(2,1)S(1)}, u32[]{:S(2)}, u32[]{:S(2)}) collective-permute-start(bf16[368,1152]{1,0:T(8,128)(2,1)S(1)} %get-tuple-element.64), channel_id=1, source_target_pairs={{0,1},{1,0},{2,3},{3,2},{4,5},{5,4},{6,7},{7,6},{8,9},{9,8},{10,11... | collective-permute-start | bytes 2543624 | tf_op jit(solution)/shard_map/ppermute | solution.py:49
  228.3 19.6 %collective-permute-start.15 = (bf16[368,1152]{1,0:T(8,128)(2,1)}, bf16[368,1152]{1,0:T(8,128)(2,1)}, u32[]{:S(2)}, u32[]{:S(2)}) collective-permute-start(bf16[368,1152]{1,0:T(8,128)(2,1)} %fusion.27), channel_id=1, source_target_pairs={{0,1},{1,0},{2,3},{3,2},{4,5},{5,4},{6,7},{7,6},{8,9},{9,8},{10,11... | collective-permute-start | bytes 2543624 | tf_op jit(solution)/shard_map/ppermute | solution.py:49
  259.1 18.8 %collective-permute-start.16 = (bf16[368,1152]{1,0:T(8,128)(2,1)}, bf16[368,1152]{1,0:T(8,128)(2,1)}, u32[]{:S(2)}, u32[]{:S(2)}) collective-permute-start(bf16[368,1152]{1,0:T(8,128)(2,1)} %convert_element_type.199), channel_id=1, source_target_pairs={{0,1},{1,0},{2,3},{3,2},{4,5},{5,4},{6,7},{7,6},{8,9},{9,8},{10,11... | collective-permute-start | bytes 2543624 | tf_op jit(solution)/shard_map/ppermute | solution.py:49
  292.9 52.9 %collective-permute-start.18 = (bf16[2,8,368,72]{2,3,1,0:T(8,128)(2,1)}, bf16[2,8,368,72]{2,3,1,0:T(8,128)(2,1)}, u32[]{:S(2)}, u32[]{:S(2)}) collective-permute-start(bf16[2,8,368,72]{2,3,1,0:T(8,128)(2,1)} %slice.228), channel_id=1, source_target_pairs={{0,2},{2,0},{1,3},{3,1},{4,6},{6,4},{5,7},{7,5},{8,10},{10,8},{9,1... | collective-permute-start | bytes 2543624 | tf_op jit(solution)/shard_map/ppermute | solution.py:49
  337.6 9.9 %collective-permute-start.17 = (bf16[2,8,368,72]{2,3,1,0:T(8,128)(2,1)}, bf16[2,8,368,72]{2,3,1,0:T(8,128)(2,1)}, u32[]{:S(2)}, u32[]{:S(2)}) collective-permute-start(bf16[2,8,368,72]{2,3,1,0:T(8,128)(2,1)} %slice.229), channel_id=1, source_target_pairs={{0,2},{2,0},{1,3},{3,1},{4,6},{6,4},{5,7},{7,5},{8,10},{10,8},{9,1... | collective-permute-start | bytes 2543624 | tf_op jit(solution)/shard_map/ppermute | solution.py:49
  409.5 9.5 %collective-permute-start.25 = (bf16[8,72,2368]{2,1,0:T(8,128)(2,1)}, bf16[8,72,2368]{2,1,0:T(8,128)(2,1)}, u32[]{:S(2)}, u32[]{:S(2)}) collective-permute-start(bf16[8,72,2368]{2,1,0:T(8,128)(2,1)} %fusion.25), channel_id=1, source_target_pairs={{0,2},{2,0},{1,3},{3,1},{4,6},{6,4},{5,7},{7,5},{8,10},{10,8},{9,1... | collective-permute-start | bytes 8183816 | tf_op jit(solution)/shard_map/ppermute | solution.py:49
  417.4 47.4 %collective-permute-start.19 = (bf16[368,1152]{1,0:T(8,128)(2,1)}, bf16[368,1152]{1,0:T(8,128)(2,1)}, u32[]{:S(2)}, u32[]{:S(2)}) collective-permute-start(bf16[368,1152]{1,0:T(8,128)(2,1)} %fusion.85), channel_id=1, source_target_pairs={{0,1},{1,0},{2,3},{3,2},{4,5},{5,4},{6,7},{7,6},{8,9},{9,8},{10,11... | collective-permute-start | bytes 2543624 | tf_op jit(solution)/shard_map/ppermute | solution.py:49
  425.6 42.0 %collective-permute-start.26 = (bf16[4,72,2368]{2,1,0:T(8,128)(2,1)}, bf16[4,72,2368]{2,1,0:T(8,128)(2,1)S(1)}, u32[]{:S(2)}, u32[]{:S(2)}) collective-permute-start(bf16[4,72,2368]{2,1,0:T(8,128)(2,1)} %fusion.75), channel_id=1, source_target_pairs={{0,4},{4,0},{8,12},{12,8},{16,20},{20,16},{24,28},{28,24},{1,5},{5... | collective-permute-start | bytes 4091912 | tf_op jit(solution)/shard_map/ppermute | solution.py:167
  428.9 30.0 %collective-permute-start.30 = (f32[3304]{0:T(1024)S(1)}, f32[3304]{0:T(1024)S(1)}, u32[]{:S(2)}, u32[]{:S(2)}) collective-permute-start(f32[3304]{0:T(1024)S(1)} %add.390), channel_id=1, source_target_pairs={{0,4},{4,0},{8,12},{12,8},{16,20},{20,16},{24,28},{28,24},{1,5},{5... | collective-permute-start | bytes 39656 | tf_op jit(solution)/shard_map/ppermute | solution.py:113
  462.7 10.9 %collective-permute-start.32 = (f32[3304]{0:T(1024)S(1)}, f32[3304]{0:T(1024)S(1)}, u32[]{:S(2)}, u32[]{:S(2)}) collective-permute-start(f32[3304]{0:T(1024)S(1)} %add.392), channel_id=1, source_target_pairs={{0,16},{4,20},{8,24},{12,28},{16,0},{20,4},{24,8},{28,12},{1,17},{... | collective-permute-start | bytes 39656 | tf_op jit(solution)/shard_map/ppermute | solution.py:113
  467.5 6.0 %collective-permute-start.20 = (f32[6913]{0:T(1024)S(1)}, f32[6913]{0:T(1024)S(1)}, u32[]{:S(2)}, u32[]{:S(2)}) collective-permute-start(f32[6913]{0:T(1024)S(1)} %constant_dynamic-update-slice_fusion), channel_id=1, source_target_pairs={{0,2},{2,0},{1,3},{3,1},{4,6},{6,4},{5,7},{7,5},{8,10},{10,8},{9,1... | collective-permute-start | bytes 82964 | tf_op jit(solution)/shard_map/ppermute | solution.py:113
  472.2 24.9 %collective-permute-start.27 = (bf16[2,72,2368]{2,1,0:T(8,128)(2,1)}, bf16[2,72,2368]{2,1,0:T(8,128)(2,1)S(1)}, u32[]{:S(2)}, u32[]{:S(2)}) collective-permute-start(bf16[2,72,2368]{2,1,0:T(8,128)(2,1)} %fusion.91), channel_id=1, source_target_pairs={{0,8},{4,12},{8,0},{12,4},{16,24},{20,28},{24,16},{28,20},{1,9},{5... | collective-permute-start | bytes 2045960 | tf_op jit(solution)/shard_map/ppermute | solution.py:167
  477.5 13.6 %collective-permute-start.22 = (f32[6913]{0:T(1024)S(1)}, f32[6913]{0:T(1024)S(1)}, u32[]{:S(2)}, u32[]{:S(2)}) collective-permute-start(f32[6913]{0:T(1024)S(1)} %add.370), channel_id=1, source_target_pairs={{0,8},{4,12},{8,0},{12,4},{16,24},{20,28},{24,16},{28,20},{1,9},{5... | collective-permute-start | bytes 82964 | tf_op jit(solution)/shard_map/ppermute | solution.py:113
  495.9 7.9 %collective-permute-start.24 = (f32[6913]{0:T(1024)S(1)}, f32[6913]{0:T(1024)S(1)}, u32[]{:S(2)}, u32[]{:S(2)}) collective-permute-start(f32[6913]{0:T(1024)S(1)} %add.372), channel_id=1, source_target_pairs={{0,1},{1,0},{2,3},{3,2},{4,5},{5,4},{6,7},{7,6},{8,9},{9,8},{10,11... | collective-permute-start | bytes 82964 | tf_op jit(solution)/shard_map/ppermute | solution.py:113
  499.8 16.8 %collective-permute-start.28 = (bf16[1,72,2368]{2,1,0:T(8,128)(2,1)S(1)}, bf16[1,72,2368]{2,1,0:T(8,128)(2,1)S(1)}, u32[]{:S(2)}, u32[]{:S(2)}) collective-permute-start(bf16[1,72,2368]{2,1,0:T(8,128)(2,1)S(1)} %dynamic-slice_convert_fusion.1), channel_id=1, source_target_pairs={{0,16},{4,20},{8,24},{12,28},{16,0},{20,4},{24,8},{28,12},{1,17},{... | collective-permute-start | bytes 1022984 | tf_op jit(solution)/shard_map/ppermute | solution.py:167
  (74 other events, 1105.3 us)
Sparse Core Ops, SparseCore 0:
  10.8 61.9 all-gather.2
  75.6 83.2 all-gather.4
  265.2 111.6 reduce-scatter.1

commit v7 on v5

--- a/solution.py
+++ b/solution.py
@@ -70,15 +70,11 @@
 
 def tensor_reduce_parts(parts):
     if lax.axis_size("tensor") == 2:
-        return parts[0] + swap(parts[1].astype(BF), "tensor").astype(F32)
+        other = swap(parts[1].astype(BF), "tensor")
+        return lax.optimization_barrier(parts[0]) + other.astype(F32)
     return lax.psum_scatter(
         jnp.stack(parts).astype(BF), "tensor", scatter_dimension=0
     ).astype(F32)
-
-
-def split_rows(values, count):
-    size = values.shape[0] // count
-    return [values[i * size : (i + 1) * size] for i in range(count)]
 
 
 def ctx_gather(values):
@@ -228,11 +224,10 @@
     hidden = inputs + attn_sum + out_bias
     normed_two, unit_two, inverse_two = norm_forward(hidden, gain_two, shift_two)
     normed_two_parts = tensor_gather_parts(normed_two.astype(BF))
-    normed_two_all = jnp.concatenate(normed_two_parts)
-    before = jnp.dot(normed_two_all, up_w, preferred_element_type=F32) + up_b
-    active = gelu_tanh(before).astype(BF)
-    before_parts = split_rows(before, n_t)
-    active_parts = split_rows(active, n_t)
+    before_parts = [
+        jnp.dot(part, up_w, preferred_element_type=F32) + up_b for part in normed_two_parts
+    ]
+    active_parts = [gelu_tanh(part).astype(BF) for part in before_parts]
     mlp_terms = [
         jnp.einsum("rf,df->rd", part, down_wt, preferred_element_type=F32)
         for part in active_parts

time: 568 us -> 553 us (0.974)
  matrix products: 124 us -> 114 us
  waiting for transfers between devices: 281 us -> 271 us
    ppermute x13, waiting for transfers between devices: 123 us -> 110 us  [swap(): return lax.ppermute(values, axis, [(0, 1), (1, 0)])]
  transfers between devices with their start and end apart: 33 -> 33, of which waited for: 23 -> 22; matrix products, arithmetic and copies ran while one was open for 25% -> 27% of each run, Pallas kernels for 0% -> 0%
where the time goes in v7:
time: 553 us; the launch traced here: 543 us
  waiting for transfers between devices  271 us (49%)
  matrix products  114 us (21%)
  other arithmetic  53.2 us (10%)
  local copies, waits for them, and re-layouts  47.5 us (9%)
  starting transfers between devices  36.3 us (7%)
  between operations  21 us (4%)
    ppermute x13, waiting for transfers between devices, swap(): return lax.ppermute(values, axis, [(0, 1), (1, 0)])  110 us
    reduce_scatter x1, waiting for transfers between devices, on_device_body(): lax.psum_scatter(mlp_grad_pack, ('dp', 'ctx'), scatter_dimension=0, tiled...  107 us
    all_gather x1, waiting for transfers between devices, on_device_body(): attn_full = lax.all_gather(attn_pack, ('dp', 'ctx'), axis=1, tiled=True)  26.6 us
    ppermute x10, waiting for transfers between devices, tree_sum(): values = jax.tree.map(lambda v: v + lax.ppermute(v, axis, perm), values)  21.6 us
    ppermute x6, starting transfers between devices, gather_vectors(): their_blocks, their_count = lax.ppermute((blocks, count), 'dp', perm)  17.8 us
    dot_general x1, matrix products, on_device_body(): jnp.einsum('bhqe,bhke->bhqk', mixed_grad, value_all, preferred_element_ty...  14.8 us
    ppermute x13, starting transfers between devices, swap(): return lax.ppermute(values, axis, [(0, 1), (1, 0)])  13.5 us
    convert_element_type x1, other arithmetic, on_device_body(): score_grad = (soft_full * (soft_grad - inner_sum)).astype(BF)  12.9 us
  transfers between devices with their start and end apart: 33, of which 22 were waited for; matrix products, arithmetic and copies ran while one was open for 27% of the time, Pallas kernels for 0%

profile of v7, /device:TPU:0, one launch (start us, length us, event | category | flops | bytes accessed | tf_op | source)
XLA Modules:
  0.0 543.1 jit_solution(8730449405602277406)
XLA Ops:
  46.2 26.6 %all-gather.3.cloned.1.call-done = bf16[4,1152,576]{2,1,0:T(8,128)(2,1)} async-done(((bf16[4,72,576]{2,1,0:T(8,128)(2,1)}), bf16[4,1152,576]{2,1,0:T(8,128)(2,1)}) %all-gather.3.cloned.1.call-update) | async-done | bytes 5308432 | tf_op jit(solution)/shard_map/all_gather | solution.py:180
  77.6 6.6 %copy.98 = bf16[3,1152,576]{1,2,0:T(8,128)(2,1)} copy(bf16[3,1152,576]{2,1,0:T(8,128)(2,1)} %slice.132) | data formatting | bytes 7962624 | tf_op jit(solution)/shard_map/slice | solution.py:183
  85.1 5.8 %fusion.25 = bf16[3,2,8,368,72]{3,4,1,2,0:T(8,128)(2,1)S(1)} fusion(f32[3,8,72]{2,1,0:T(8,128)S(1)} %maximum_bitcast_fusion, bf16[3,1152,8,72,1]{1,3,4,2,0:T(8,128)(2,1)} %bitcast.224, bf16[1,368,1152]{2,1,0:T(8,128)(2,1)S(1)} %bitcast.244, bf16[1,368,1152]{2,1,0:T(8,128)(2,1)S(1)} %fusion.49), kind=kOutput, calls=%fused_computation.53 | convolution fusion | flops 2936180736 | bytes 8227584 | tf_op jit(solution)/shard_map/pro,tojx->tpjrx/dot_general | solution.py:201
  95.2 5.5 %fusion = (f32[2,8,368]{2,1,0:T(8,128)S(1)}, f32[2,8,368,736]{3,2,1,0:T(8,128)S(1)}) fusion(pred[736]{0:T(1024)(128)(4,1)S(1)} %fusion.91, bf16[2,8,368,72]{2,3,0,1:T(8,128)(2,1)S(1)} %get-tuple-element.45, bf16[2,8,368,72]{2,3,0,1:T(8,128)(2,1)} %collective-permute-done.9, bf16[2,8,368,72]{2,3,0,1:T(8,128)(2,1)} %get-tuple-element.47), kind=kOutput, calls=%fused_computation.7 | convolution fusion | flops 640420096 | bytes 19902176 | tf_op jit(solution)/shard_map/bhqe,bhke->bhqk/dot_general | solution.py:210
  107.5 6.3 %fusion.65 = bf16[2,8,368,72]{2,3,1,0:T(8,128)(2,1)} fusion(f32[2,8,368,736]{3,2,1,0:T(8,128)S(1)} %get-tuple-element.61, f32[2,8,368]{2,1,0:T(8,128)S(1)} %log_add_fusion, pred[736]{0:T(1024)(128)(4,1)S(1)} %fusion.91, bf16[2,8,368,72]{2,3,0,1:T(8,128)(2,1)S(1)} %collective-permute-done.10, bf16[2,8,368,72]{2,3,0,1:T(8,128)(2,1)S(1)} %copy-done.17), kind=kOutput, calls=%fused_computation.127 | convolution fusion | flops 645183488 | bytes 19902176 | tf_op jit(solution)/shard_map/bhqk,bhke->bhqe/dot_general | solution.py:216
  118.3 19.5 %collective-permute-done.11 = bf16[368,1152]{1,0:T(8,128)(2,1)S(1)} collective-permute-done((bf16[368,1152]{1,0:T(8,128)(2,1)S(1)}, bf16[368,1152]{1,0:T(8,128)(2,1)S(1)}, u32[]{:S(2)}, u32[]{:S(2)}) %collective-permute-start.11) | collective-permute-done | bytes 847904 | tf_op jit(solution)/shard_map/ppermute | solution.py:49
  140.6 18.8 %collective-permute-done.12 = bf16[368,1152]{1,0:T(8,128)(2,1)} collective-permute-done((bf16[368,1152]{1,0:T(8,128)(2,1)S(1)}, bf16[368,1152]{1,0:T(8,128)(2,1)}, u32[]{:S(2)}, u32[]{:S(2)}) %collective-permute-start.12) | collective-permute-done | bytes 847904 | tf_op jit(solution)/shard_map/ppermute | solution.py:49
  159.4 5.2 convolution_add_fusion.2
  174.8 13.6 %collective-permute-done.13 = bf16[368,1152]{1,0:T(8,128)(2,1)S(1)} collective-permute-done((bf16[368,1152]{1,0:T(8,128)(2,1)S(1)}, bf16[368,1152]{1,0:T(8,128)(2,1)S(1)}, u32[]{:S(2)}, u32[]{:S(2)}) %collective-permute-start.13) | collective-permute-done | bytes 847904 | tf_op jit(solution)/shard_map/ppermute | solution.py:49
  192.0 18.1 %collective-permute-done.14 = bf16[368,1152]{1,0:T(8,128)(2,1)S(1)} collective-permute-done((bf16[368,1152]{1,0:T(8,128)(2,1)S(1)}, bf16[368,1152]{1,0:T(8,128)(2,1)S(1)}, u32[]{:S(2)}, u32[]{:S(2)}) %collective-permute-start.14) | collective-permute-done | bytes 847904 | tf_op jit(solution)/shard_map/ppermute | solution.py:49
  221.7 5.4 %fusion.9 = f32[368,1152]{1,0:T(8,128)S(1)} fusion(bf16[368,2176]{1,0:T(8,128)(2,1)S(1)} %fusion.6, bf16[2,1152,2176]{2,1,0:T(8,128)(2,1)} %all-gather.5.cloned.1.call-done), kind=kOutput, calls=%fused_computation.34 | convolution fusion | flops 1844969472 | bytes 8310784 | tf_op jit(solution)/shard_map/rf,df->rd/dot_general | solution.py:255
  227.1 8.0 %collective-permute-done.15 = bf16[368,1152]{1,0:T(8,128)(2,1)S(1)} collective-permute-done((bf16[368,1152]{1,0:T(8,128)(2,1)S(1)}, bf16[368,1152]{1,0:T(8,128)(2,1)S(1)}, u32[]{:S(2)}, u32[]{:S(2)}) %collective-permute-start.15) | collective-permute-done | bytes 847904 | tf_op jit(solution)/shard_map/ppermute | solution.py:49
  240.8 16.3 %collective-permute-done.16 = bf16[368,1152]{1,0:T(8,128)(2,1)S(1)} collective-permute-done((bf16[368,1152]{1,0:T(8,128)(2,1)S(1)}, bf16[368,1152]{1,0:T(8,128)(2,1)S(1)}, u32[]{:S(2)}, u32[]{:S(2)}) %collective-permute-start.16) | collective-permute-done | bytes 847904 | tf_op jit(solution)/shard_map/ppermute | solution.py:49
  260.4 7.0 %fusion.81 = f32[2,8,736,72]{2,3,1,0:T(8,128)} fusion(bf16[2,8,368,72]{2,3,0,1:T(8,128)(2,1)} %fusion.73, f32[2,8,368,736]{3,2,1,0:T(8,128)S(1)} %bitcast.223, f32[2,8,368]{2,1,0:T(8,128)S(1)} %log_add_fusion, pred[736]{0:T(1024)(128)(4,1)S(1)} %fusion.91), kind=kOutput, calls=%fused_computation.140 | convolution fusion | flops 641368064 | bytes 21597920 | tf_op jit(solution)/shard_map/bhqk,bhqe->bhke/dot_general | solution.py:290
  270.3 14.8 %multiply_reduce_fusion = (f32[2,8,368]{2,1,0:T(8,128)S(1)}, f32[2,8,368,736]{3,2,1,0:T(8,128)}) fusion(f32[2,8,368,736]{3,2,1,0:T(8,128)} %copy-done, f32[2,8,368]{2,1,0:T(8,128)S(1)} %log_add_fusion, pred[736]{0:T(1024)(128)(4,1)S(1)} %fusion.91, bf16[2,8,368,72]{2,3,0,1:T(8,128)(2,1)S(1)} %copy-done.35, bf16[2,8,368,72]{2,3,0,1:T(8,128)(2,1)S(1)} %copy-done.34, ...), kind=kOutput, calls=%fused_computation.1 | convolution fusion | flops 649087232 | bytes 37260000 | tf_op jit(solution)/shard_map/bhqe,bhke->bhqk/dot_general | solution.py:289
  285.2 12.9 %multiply_convert_fusion = bf16[2,8,368,736]{3,2,1,0:T(8,128)(2,1)S(1)} fusion(f32[2,8,368,736]{3,2,1,0:T(8,128)} %get-tuple-element.63, f32[2,8,368,736]{3,2,1,0:T(8,128)} %copy-done, f32[2,8,368]{2,1,0:T(8,128)S(1)} %get-tuple-element.62, f32[2,8,368]{2,1,0:T(8,128)S(1)} %log_add_fusion, pred[736]{0:T(1024)(128)(4,1)S(1)} %fusion.91), kind=kLoop, calls=%fused_computation | loop fusion | flops 26001408 | bytes 43383520 | tf_op jit(solution)/shard_map/convert_element_type | solution.py:294
  309.0 7.8 %convert_reduce_fusion.3 = (f32[8,72]{1,0:T(8,128)S(1)}, bf16[2,8,368,72]{2,3,1,0:T(8,128)(2,1)}) fusion(bf16[2,8,368,736]{3,2,1,0:T(8,128)(2,1)} %copy-done.3, bf16[2,8,368,72]{2,3,0,1:T(8,128)(2,1)} %collective-permute-done.9, bf16[2,8,368,72]{2,3,0,1:T(8,128)(2,1)} %get-tuple-element.47), kind=kOutput, calls=%fused_computation.76 | convolution fusion | flops 629120448 | bytes 11213056 | tf_op jit(solution)/shard_map/bhqk,bhke->bhqe/dot_general | solution.py:296
  318.7 5.2 bitcast_convert_fusion
  323.9 6.6 %copy.115 = bf16[1152,1728]{1,0:T(8,128)(2,1)} copy(bf16[1152,1728]{0,1:T(8,128)(2,1)} %bitcast.226) | data formatting | bytes 7962624 | tf_op jit(solution)/shard_map/convert_element_type | solution.py:316
  330.5 5.3 fusion.5
  348.0 5.4 fusion.2
  359.9 6.6 %convolution_bitcast_fusion.1 = f32[2,368,1152]{2,1,0:T(8,128)S(1)} fusion(bf16[3,1152,8,72,1]{1,3,2,4,0:T(8,128)(2,1)} %bitcast.225, bf16[1,2,8,368,72]{3,4,2,1,0:T(8,128)(2,1)S(1)} %copy-done.32, bf16[1,2,8,368,72]{3,4,2,1,0:T(8,128)(2,1)S(1)} %copy-done.30, bf16[1,2,8,368,72]{3,4,2,1,0:T(8,128)(2,1)S(1)} %bitcast.249), kind=kOutput, calls=%fused_computation.31 | convolution fusion | flops 2932789248 | bytes 9916416 | tf_op jit(solution)/shard_map/toaks,tzas->okz/dot_general | solution.py:323
  374.8 15.0 %collective-permute-done.19 = bf16[368,1152]{1,0:T(8,128)(2,1)S(1)} collective-permute-done((bf16[368,1152]{1,0:T(8,128)(2,1)}, bf16[368,1152]{1,0:T(8,128)(2,1)S(1)}, u32[]{:S(2)}, u32[]{:S(2)}) %collective-permute-start.19) | collective-permute-done | bytes 847904 | tf_op jit(solution)/shard_map/ppermute | solution.py:49
  425.1 106.9 %reduce-scatter.5.cloned.1.call-done = bf16[72,4352]{1,0:T(8,128)(2,1)} async-done(((bf16[1152,4352]{1,0:T(8,128)(2,1)}), bf16[72,4352]{1,0:T(8,128)(2,1)}) %reduce-scatter.5.cloned.1.call-update) | async-done | bytes 626704 | tf_op jit(solution)/shard_map/reduce_scatter | solution.py:270
  (292 shorter events, 172.9 us)
Async XLA Ops:
  7.2 65.6 %all-gather.3.cloned.1.call-start = ((), (), s32[]{:S(2)}) async-start(), calls=%async_computation.2 | async-start | bytes 6266880 | tf_op jit(solution)/shard_map/all_gather | solution.py:180
  9.2 150.3 %all-gather.5.cloned.1.call-start = ((), (), s32[]{:S(2)}) async-start(), calls=%async_computation.3 | async-start | bytes 10653696 | tf_op jit(solution)/shard_map/all_gather | solution.py:182
  11.2 410.4 %reduce-scatter.7.cloned.1.call-start = ((), (), s32[]{:S(2)}) async-start(), calls=%async_computation.5 | async-start | bytes 5953536
  11.2 4.9 collective-permute-start
  15.1 15.9 %collective-permute-start.4 = (bf16[72,6]{0,1:T(8,128)(2,1)S(1)}, bf16[72,6]{0,1:T(8,128)(2,1)S(1)}, u32[]{:S(2)}, u32[]{:S(2)}) collective-permute-start(bf16[72,6]{0,1:T(8,128)(2,1)S(1)} %stack.111), channel_id=1, source_target_pairs={{0,2},{2,0},{1,3},{3,1},{4,6},{6,4},{5,7},{7,5},{8,10},{10,8},{9,1... | collective-permute-start | bytes 2600 | tf_op jit(solution)/shard_map/ppermute | solution.py:49
  25.3 4.9 collective-permute-start.3
  38.4 4.7 collective-permute-start.7
  43.7 40.5 %collective-permute-start.8 = (bf16[368,1152]{1,0:T(8,128)(2,1)S(1)}, bf16[368,1152]{1,0:T(8,128)(2,1)S(1)}, u32[]{:S(2)}, u32[]{:S(2)}) collective-permute-start(bf16[368,1152]{1,0:T(8,128)(2,1)S(1)} %fusion.37), channel_id=1, source_target_pairs={{0,1},{1,0},{2,3},{3,2},{4,5},{5,4},{6,7},{7,6},{8,9},{9,8},{10,11... | collective-permute-start | bytes 2543624 | tf_op jit(solution)/shard_map/ppermute | solution.py:49
  94.5 11.0 %collective-permute-start.10 = (bf16[2,8,368,72]{2,3,0,1:T(8,128)(2,1)}, bf16[2,8,368,72]{2,3,0,1:T(8,128)(2,1)S(1)}, u32[]{:S(2)}, u32[]{:S(2)}) collective-permute-start(bf16[2,8,368,72]{2,3,0,1:T(8,128)(2,1)} %get-tuple-element.46), channel_id=1, source_target_pairs={{0,2},{2,0},{1,3},{3,1},{4,6},{6,4},{5,7},{7,5},{8,10},{10,8},{9,1... | collective-permute-start | bytes 2543624 | tf_op jit(solution)/shard_map/ppermute | solution.py:49
  116.8 21.1 %collective-permute-start.11 = (bf16[368,1152]{1,0:T(8,128)(2,1)S(1)}, bf16[368,1152]{1,0:T(8,128)(2,1)S(1)}, u32[]{:S(2)}, u32[]{:S(2)}) collective-permute-start(bf16[368,1152]{1,0:T(8,128)(2,1)S(1)} %fusion.79), channel_id=1, source_target_pairs={{0,1},{1,0},{2,3},{3,2},{4,5},{5,4},{6,7},{7,6},{8,9},{9,8},{10,11... | collective-permute-start | bytes 2543624 | tf_op jit(solution)/shard_map/ppermute | solution.py:49
  139.0 20.4 %collective-permute-start.12 = (bf16[368,1152]{1,0:T(8,128)(2,1)S(1)}, bf16[368,1152]{1,0:T(8,128)(2,1)}, u32[]{:S(2)}, u32[]{:S(2)}) collective-permute-start(bf16[368,1152]{1,0:T(8,128)(2,1)S(1)} %add_convert_fusion.1), channel_id=1, source_target_pairs={{0,1},{1,0},{2,3},{3,2},{4,5},{5,4},{6,7},{7,6},{8,9},{9,8},{10,11... | collective-permute-start | bytes 2543624 | tf_op jit(solution)/shard_map/ppermute | solution.py:49
  168.0 20.5 %collective-permute-start.13 = (bf16[368,1152]{1,0:T(8,128)(2,1)S(1)}, bf16[368,1152]{1,0:T(8,128)(2,1)S(1)}, u32[]{:S(2)}, u32[]{:S(2)}) collective-permute-start(bf16[368,1152]{1,0:T(8,128)(2,1)S(1)} %fusion.23), channel_id=1, source_target_pairs={{0,1},{1,0},{2,3},{3,2},{4,5},{5,4},{6,7},{7,6},{8,9},{9,8},{10,11... | collective-permute-start | bytes 2543624 | tf_op jit(solution)/shard_map/ppermute | solution.py:49
  190.5 19.7 %collective-permute-start.14 = (bf16[368,1152]{1,0:T(8,128)(2,1)S(1)}, bf16[368,1152]{1,0:T(8,128)(2,1)S(1)}, u32[]{:S(2)}, u32[]{:S(2)}) collective-permute-start(bf16[368,1152]{1,0:T(8,128)(2,1)S(1)} %multiply_convert_fusion.4), channel_id=1, source_target_pairs={{0,1},{1,0},{2,3},{3,2},{4,5},{5,4},{6,7},{7,6},{8,9},{9,8},{10,11... | collective-permute-start | bytes 2543624 | tf_op jit(solution)/shard_map/ppermute | solution.py:49
  216.3 18.8 %collective-permute-start.15 = (bf16[368,1152]{1,0:T(8,128)(2,1)S(1)}, bf16[368,1152]{1,0:T(8,128)(2,1)S(1)}, u32[]{:S(2)}, u32[]{:S(2)}) collective-permute-start(bf16[368,1152]{1,0:T(8,128)(2,1)S(1)} %fusion.24), channel_id=1, source_target_pairs={{0,1},{1,0},{2,3},{3,2},{4,5},{5,4},{6,7},{7,6},{8,9},{9,8},{10,11... | collective-permute-start | bytes 2543624 | tf_op jit(solution)/shard_map/ppermute | solution.py:49
  239.1 17.9 %collective-permute-start.16 = (bf16[368,1152]{1,0:T(8,128)(2,1)S(1)}, bf16[368,1152]{1,0:T(8,128)(2,1)S(1)}, u32[]{:S(2)}, u32[]{:S(2)}) collective-permute-start(bf16[368,1152]{1,0:T(8,128)(2,1)S(1)} %convert_element_type.179), channel_id=1, source_target_pairs={{0,1},{1,0},{2,3},{3,2},{4,5},{5,4},{6,7},{7,6},{8,9},{9,8},{10,11... | collective-permute-start | bytes 2543624 | tf_op jit(solution)/shard_map/ppermute | solution.py:49
  270.3 46.4 %collective-permute-start.18 = (bf16[2,8,368,72]{2,3,1,0:T(8,128)(2,1)}, bf16[2,8,368,72]{2,3,1,0:T(8,128)(2,1)}, u32[]{:S(2)}, u32[]{:S(2)}) collective-permute-start(bf16[2,8,368,72]{2,3,1,0:T(8,128)(2,1)} %slice.226), channel_id=1, source_target_pairs={{0,2},{2,0},{1,3},{3,1},{4,6},{6,4},{5,7},{7,5},{8,10},{10,8},{9,1... | collective-permute-start | bytes 2543624 | tf_op jit(solution)/shard_map/ppermute | solution.py:49
  308.4 10.0 %collective-permute-start.17 = (bf16[2,8,368,72]{2,3,1,0:T(8,128)(2,1)S(1)}, bf16[2,8,368,72]{2,3,1,0:T(8,128)(2,1)S(1)}, u32[]{:S(2)}, u32[]{:S(2)}) collective-permute-start(bf16[2,8,368,72]{2,3,1,0:T(8,128)(2,1)S(1)} %slice.227), channel_id=1, source_target_pairs={{0,2},{2,0},{1,3},{3,1},{4,6},{6,4},{5,7},{7,5},{8,10},{10,8},{9,1... | collective-permute-start | bytes 2543624 | tf_op jit(solution)/shard_map/ppermute | solution.py:49
  335.9 196.1 %reduce-scatter.5.cloned.1.call-start = ((), (), s32[]{:S(2)}) async-start(), calls=%async_computation.4 | async-start | bytes 10653696 | tf_op jit(solution)/shard_map/reduce_scatter | solution.py:270
  369.2 20.6 %collective-permute-start.19 = (bf16[368,1152]{1,0:T(8,128)(2,1)}, bf16[368,1152]{1,0:T(8,128)(2,1)S(1)}, u32[]{:S(2)}, u32[]{:S(2)}) collective-permute-start(bf16[368,1152]{1,0:T(8,128)(2,1)} %fusion.80), channel_id=1, source_target_pairs={{0,1},{1,0},{2,3},{3,2},{4,5},{5,4},{6,7},{7,6},{8,9},{9,8},{10,11... | collective-permute-start | bytes 2543624 | tf_op jit(solution)/shard_map/ppermute | solution.py:49
  374.7 17.7 %collective-permute-start.26 = (f32[3304]{0:T(1024)S(1)}, f32[3304]{0:T(1024)S(1)}, u32[]{:S(2)}, u32[]{:S(2)}) collective-permute-start(f32[3304]{0:T(1024)S(1)} %add.333), channel_id=1, source_target_pairs={{0,4},{4,0},{8,12},{12,8},{16,20},{20,16},{24,28},{28,24},{1,5},{5... | collective-permute-start | bytes 39656 | tf_op jit(solution)/shard_map/ppermute | solution.py:114
  392.3 9.1 %collective-permute-start.20 = (f32[6913]{0:T(1024)S(1)}, f32[6913]{0:T(1024)S(1)}, u32[]{:S(2)}, u32[]{:S(2)}) collective-permute-start(f32[6913]{0:T(1024)S(1)} %constant_dynamic-update-slice_fusion), channel_id=1, source_target_pairs={{0,2},{2,0},{1,3},{3,1},{4,6},{6,4},{5,7},{7,5},{8,10},{10,8},{9,1... | collective-permute-start | bytes 82964 | tf_op jit(solution)/shard_map/ppermute | solution.py:114
  396.2 5.2 collective-permute-start.28
  405.4 5.2 collective-permute-start.22
  410.6 4.8 collective-permute-start.23
  (75 other events, 1040.1 us)
Sparse Core Ops, SparseCore 0:
  10.8 61.9 all-gather.2
  75.6 83.2 all-gather.4
  336.0 78.2 reduce-scatter.6
  418.3 113.6 reduce-scatter.4

commit v8 on v7

--- a/solution.py
+++ b/solution.py
@@ -277,29 +277,44 @@
     hidden_grad = grad_out + hidden_back
     down_bias_grad = jnp.sum(grad_out, axis=0)
     out_bias_grad = jnp.sum(hidden_grad, axis=0)
-    hidden_token_rows = tensor_gather(hidden_grad.astype(BF)).reshape(images, half_len, width)
-    out_grad_t = jnp.einsum(
-        "lcd,lscm->dsm", hidden_token_rows, mixed_per_head, preferred_element_type=F32
-    ).reshape(width, head_width)
-    mixed_grad = jnp.einsum(
-        "lcd,dsm->lscm", hidden_token_rows, out_per_head, preferred_element_type=F32
-    ).astype(BF)
-
-    soft_full = jnp.exp(scores - log_totals)
-    soft_grad = jnp.einsum("bhqe,bhke->bhqk", mixed_grad, value_all, preferred_element_type=F32)
-    value_grads = jnp.einsum(
-        "bhqk,bhqe->bhke", soft_full.astype(BF), mixed_grad, preferred_element_type=F32
-    )
-    inner_sum = jnp.sum(soft_full * soft_grad, axis=-1, keepdims=True)
-    score_grad = (soft_full * (soft_grad - inner_sum)).astype(BF)
-    query_grads = (
-        jnp.einsum("bhqk,bhke->bhqe", score_grad, key_all, preferred_element_type=F32)
-        * score_scale
-    )
-    key_grads = (
-        jnp.einsum("bhqk,bhqe->bhke", score_grad, queries, preferred_element_type=F32)
-        * score_scale
-    )
+    hidden_token_parts = tensor_gather_parts(hidden_grad.astype(BF))
+    out_grad_t = None
+    query_parts, key_parts, value_parts = [], [], []
+    for i, token_grad in enumerate(hidden_token_parts):
+        sl = slice(i * own_images, (i + 1) * own_images)
+        token_grad = token_grad.reshape(own_images, half_len, width)
+        mixed_i = mixed_per_head[sl]
+        out_term = jnp.einsum(
+            "lcd,lscm->dsm", token_grad, mixed_i, preferred_element_type=F32
+        ).reshape(width, head_width)
+        out_grad_t = out_term if out_grad_t is None else out_grad_t + out_term
+        mixed_grad = jnp.einsum(
+            "lcd,dsm->lscm", token_grad, out_per_head, preferred_element_type=F32
+        ).astype(BF)
+        value_i = value_all[sl]
+        key_i = key_all[sl]
+        soft_full = jnp.exp(scores[sl] - log_totals[sl])
+        soft_grad = jnp.einsum("bhqe,bhke->bhqk", mixed_grad, value_i, preferred_element_type=F32)
+        value_parts.append(
+            jnp.einsum(
+                "bhqk,bhqe->bhke", soft_full.astype(BF), mixed_grad, preferred_element_type=F32
+            )
+        )
+        inner_sum = jnp.sum(soft_full * soft_grad, axis=-1, keepdims=True)
+        score_grad = (soft_full * (soft_grad - inner_sum)).astype(BF)
+        query_parts.append(
+            jnp.einsum("bhqk,bhke->bhqe", score_grad, key_i, preferred_element_type=F32)
+            * score_scale
+        )
+        key_parts.append(
+            jnp.einsum(
+                "bhqk,bhqe->bhke", score_grad, queries[sl], preferred_element_type=F32
+            )
+            * score_scale
+        )
+    query_grads = jnp.concatenate(query_parts)
+    key_grads = jnp.concatenate(key_parts)
+    value_grads = jnp.concatenate(value_parts)
     key_reduced_precision = ctx_reduce(key_grads, half_len).astype(BF)
     value_reduced_precision = ctx_reduce(value_grads, half_len).astype(BF)
     query_reduced_precision = query_grads.astype(BF)

time: 553 us -> 537 us (0.971)
  waiting for transfers between devices: 271 us -> 261 us
    convert_element_type x2 -> x1, other arithmetic: 13 us -> 0.09 us  [on_device_body(): hidden_token_parts = tensor_gather_parts(hidden_grad.astype(BF))]
    another operation x1 -> x3, other arithmetic: 0.09 us -> 12.5 us  [tensor_gather(): return jnp.stack([values, swap(values, 'tensor')])]
    ppermute x13, waiting for transfers between devices: 110 us -> 102 us  [swap(): return lax.ppermute(values, axis, [(0, 1), (1, 0)])]
    unnamed x136 -> x141, local copies, waits for them, and re-layouts: 11.2 us -> 14 us
    dot_general x5 -> x10, matrix products: 30.3 us -> 32.6 us  [the longest x2 12.1 us: on_device_body(): jnp.einsum('bhqe,bhke->bhqk', mixed_grad, value_i, preferred_element_type...]
  transfers between devices with their start and end apart: 33 -> 33, of which waited for: 22 -> 22; matrix products, arithmetic and copies ran while one was open for 27% -> 29% of each run, Pallas kernels for 0% -> 0%
where the time goes in v8:
time: 537 us; the launch traced here: 532 us
  waiting for transfers between devices  261 us (49%)
  matrix products  115 us (21%)
  other arithmetic  53.3 us (10%)
  local copies, waits for them, and re-layouts  45.7 us (9%)
  starting transfers between devices  37.3 us (7%)
  between operations  20.8 us (4%)
    reduce_scatter x1, waiting for transfers between devices, on_device_body(): lax.psum_scatter(mlp_grad_pack, ('dp', 'ctx'), scatter_dimension=0, tiled...  105 us
    ppermute x13, waiting for transfers between devices, swap(): return lax.ppermute(values, axis, [(0, 1), (1, 0)])  102 us
    all_gather x1, waiting for transfers between devices, on_device_body(): attn_full = lax.all_gather(attn_pack, ('dp', 'ctx'), axis=1, tiled=True)  26.5 us
    ppermute x10, waiting for transfers between devices, tree_sum(): values = jax.tree.map(lambda v: v + lax.ppermute(v, axis, perm), values)  21.2 us
    ppermute x6, starting transfers between devices, gather_vectors(): their_blocks, their_count = lax.ppermute((blocks, count), 'dp', perm)  18.1 us
    unnamed x141, local copies, waits for them, and re-layouts  14 us
    ppermute x13, starting transfers between devices, swap(): return lax.ppermute(values, axis, [(0, 1), (1, 0)])  13 us
    another operation x3, other arithmetic  12.5 us
  transfers between devices with their start and end apart: 33, of which 22 were waited for; matrix products, arithmetic and copies ran while one was open for 29% of the time, Pallas kernels for 0%

profile of v8, /device:TPU:0, one launch (start us, length us, event | category | flops | bytes accessed | tf_op | source)
XLA Modules:
  0.0 532.3 jit_solution(825849445055306711)
XLA Ops:
  46.5 26.5 %all-gather.3.cloned.1.call-done = bf16[4,1152,576]{2,1,0:T(8,128)(2,1)} async-done(((bf16[4,72,576]{2,1,0:T(8,128)(2,1)}), bf16[4,1152,576]{2,1,0:T(8,128)(2,1)}) %all-gather.3.cloned.1.call-update) | async-done | bytes 5308432 | tf_op jit(solution)/shard_map/all_gather | solution.py:180
  77.8 6.9 %copy.74 = bf16[3,1152,576]{1,2,0:T(8,128)(2,1)} copy(bf16[3,1152,576]{2,1,0:T(8,128)(2,1)} %slice.186) | data formatting | bytes 7962624 | tf_op jit(solution)/shard_map/slice | solution.py:183
  85.7 5.8 %fusion.43 = bf16[3,2,8,368,72]{3,4,1,2,0:T(8,128)(2,1)S(1)} fusion(f32[3,8,72]{2,1,0:T(8,128)S(1)} %maximum_bitcast_fusion, bf16[3,1152,8,72,1]{1,3,4,2,0:T(8,128)(2,1)} %bitcast.304, bf16[1,368,1152]{2,1,0:T(8,128)(2,1)S(1)} %bitcast.334, bf16[1,368,1152]{2,1,0:T(8,128)(2,1)S(1)} %fusion.75), kind=kOutput, calls=%fused_computation.77 | convolution fusion | flops 2936180736 | bytes 8227584 | tf_op jit(solution)/shard_map/pro,tojx->tpjrx/dot_general | solution.py:201
  97.2 5.6 %fusion.141 = (f32[2,8,368]{2,1,0:T(8,128)S(1)}, f32[2,8,368,736]{3,2,1,0:T(8,128)S(1)}) fusion(bf16[2,8,368,72]{2,3,0,1:T(8,128)(2,1)} %get-tuple-element.49, pred[736]{0:T(1024)(128)(4,1)S(1)} %fusion.118, bf16[2,8,368,72]{2,3,0,1:T(8,128)(2,1)} %collective-permute-done.9, bf16[2,8,368,72]{2,3,0,1:T(8,128)(2,1)} %get-tuple-element.51), kind=kOutput, calls=%fused_computation.251 | convolution fusion | flops 640420096 | bytes 19902176 | tf_op jit(solution)/shard_map/bhqe,bhke->bhqk/dot_general | solution.py:210
  109.0 4.9 fusion.86
  119.0 19.5 %collective-permute-done.11 = bf16[368,1152]{1,0:T(8,128)(2,1)S(1)} collective-permute-done((bf16[368,1152]{1,0:T(8,128)(2,1)S(1)}, bf16[368,1152]{1,0:T(8,128)(2,1)S(1)}, u32[]{:S(2)}, u32[]{:S(2)}) %collective-permute-start.11) | collective-permute-done | bytes 847904 | tf_op jit(solution)/shard_map/ppermute | solution.py:49
  141.3 18.8 %collective-permute-done.12 = bf16[368,1152]{1,0:T(8,128)(2,1)} collective-permute-done((bf16[368,1152]{1,0:T(8,128)(2,1)S(1)}, bf16[368,1152]{1,0:T(8,128)(2,1)}, u32[]{:S(2)}, u32[]{:S(2)}) %collective-permute-start.12) | collective-permute-done | bytes 847904 | tf_op jit(solution)/shard_map/ppermute | solution.py:49
  160.1 5.2 convolution_add_fusion.2
  175.4 13.3 %collective-permute-done.13 = bf16[368,1152]{1,0:T(8,128)(2,1)S(1)} collective-permute-done((bf16[368,1152]{1,0:T(8,128)(2,1)S(1)}, bf16[368,1152]{1,0:T(8,128)(2,1)S(1)}, u32[]{:S(2)}, u32[]{:S(2)}) %collective-permute-start.13) | collective-permute-done | bytes 847904 | tf_op jit(solution)/shard_map/ppermute | solution.py:49
  192.9 16.9 %collective-permute-done.14 = bf16[368,1152]{1,0:T(8,128)(2,1)S(1)} collective-permute-done((bf16[368,1152]{1,0:T(8,128)(2,1)S(1)}, bf16[368,1152]{1,0:T(8,128)(2,1)S(1)}, u32[]{:S(2)}, u32[]{:S(2)}) %collective-permute-start.14) | collective-permute-done | bytes 847904 | tf_op jit(solution)/shard_map/ppermute | solution.py:49
  221.3 5.4 %fusion.27 = f32[368,1152]{1,0:T(8,128)S(1)} fusion(bf16[368,2176]{1,0:T(8,128)(2,1)S(1)} %fusion.24, bf16[2,1152,2176]{2,1,0:T(8,128)(2,1)} %all-gather.5.cloned.1.call-done), kind=kOutput, calls=%fused_computation.58 | convolution fusion | flops 1844969472 | bytes 8310784 | tf_op jit(solution)/shard_map/rf,df->rd/dot_general | solution.py:255
  226.8 7.7 %collective-permute-done.15 = bf16[368,1152]{1,0:T(8,128)(2,1)S(1)} collective-permute-done((bf16[368,1152]{1,0:T(8,128)(2,1)S(1)}, bf16[368,1152]{1,0:T(8,128)(2,1)S(1)}, u32[]{:S(2)}, u32[]{:S(2)}) %collective-permute-start.15) | collective-permute-done | bytes 847904 | tf_op jit(solution)/shard_map/ppermute | solution.py:49
  245.2 10.4 %collective-permute-done.16 = bf16[368,1152]{1,0:T(8,128)(2,1)} collective-permute-done((bf16[368,1152]{1,0:T(8,128)(2,1)S(1)}, bf16[368,1152]{1,0:T(8,128)(2,1)}, u32[]{:S(2)}, u32[]{:S(2)}) %collective-permute-start.16) | collective-permute-done | bytes 847904 | tf_op jit(solution)/shard_map/ppermute | solution.py:49
  265.1 10.6 %fusion.9 = (f32[8,368]{1,0:T(8,128)S(1)}, f32[8,368]{1,0:T(8,128)S(1)}, f32[8,368,736]{2,1,0:T(8,128)}) fusion(f32[2,8,368,736]{3,2,1,0:T(8,128)} %copy-done, f32[8,368]{1,0:T(8,128)S(1)} %get-tuple-element.64, f32[8,368,736]{2,1,0:T(8,128)S(1)} %fusion.102, f32[8,368]{1,0:T(8,128)S(1)} %get-tuple-element.65, bf16[8,368,72]{1,2,0:T(8,128)(2,1)S(1)} %fusion.93, ...), kind=kOutput, calls=%fused_computation.22 | convolution fusion | flops 326707456 | bytes 36835328 | tf_op jit(solution)/shard_map/bhqe,bhke->bhqk/dot_general | solution.py:297
  275.8 9.9 %fusion.20 = (bf16[8,368,736]{2,1,0:T(8,128)(2,1)S(1)}, bf16[8,368,736]{2,1,0:T(8,128)(2,1)S(1)}) fusion(f32[8,368,736]{2,1,0:T(8,128)} %get-tuple-element.70, f32[2,8,368,736]{3,2,1,0:T(8,128)} %copy-done, f32[8,368]{1,0:T(8,128)S(1)} %get-tuple-element.22, f32[8,368]{1,0:T(8,128)S(1)} %get-tuple-element.64, f32[8,368,736]{2,1,0:T(8,128)S(1)} %fusion.102, ...), kind=kLoop, calls=%fused_computation.42 | loop fusion | flops 17334272 | bytes 43382784 | tf_op jit(solution)/shard_map/reshape.9
  308.8 5.2 bitcast_convert_fusion
  314.0 6.6 %copy.85 = bf16[1152,1728]{1,0:T(8,128)(2,1)} copy(bf16[1152,1728]{0,1:T(8,128)(2,1)} %bitcast.306) | data formatting | bytes 7962624 | tf_op jit(solution)/shard_map/convert_element_type | solution.py:331
  320.6 5.3 fusion.13
  333.5 5.1 fusion
  338.7 5.4 %fusion.1 = bf16[1152,2176]{1,0:T(8,128)(2,1)S(1)} fusion(f32[1152,2176]{1,0:T(8,128)S(1)} %fusion.132, bf16[368,1152]{1,0:T(8,128)(2,1)S(1)} %copy-done.34, f32[368,2176]{1,0:T(8,128)} %copy-done.28), kind=kOutput, calls=%fused_computation.6 | convolution fusion | flops 1857189888 | bytes 19091456 | tf_op jit(solution)/shard_map/rd,rf->df/dot_general | solution.py:263
  350.1 7.1 %convolution_bitcast_fusion.1 = f32[2,368,1152]{2,1,0:T(8,128)S(1)} fusion(bf16[3,1152,8,72,1]{1,3,2,4,0:T(8,128)(2,1)} %bitcast.305, bf16[1,2,8,368,72]{3,4,2,1,0:T(8,128)(2,1)S(1)} %bitcast.313, bf16[1,2,8,368,72]{3,4,2,1,0:T(8,128)(2,1)} %copy-done.38, bf16[1,1,8,368,72]{3,4,2,1,0:T(8,128)(2,1)} %bitcast.318, bf16[1,1,8,368,72]{3,4,2,1,0:T(8,128)(2,1)S(1)} %bitcast.315), kind=kOutput, calls=%fused_computation.51 | convolution fusion | flops 2934061056 | bytes 9916416 | tf_op jit(solution)/shard_map/toaks,tzas->okz/dot_general | solution.py:338
  366.1 15.2 %collective-permute-done.19 = bf16[368,1152]{1,0:T(8,128)(2,1)S(1)} collective-permute-done((bf16[368,1152]{1,0:T(8,128)(2,1)}, bf16[368,1152]{1,0:T(8,128)(2,1)S(1)}, u32[]{:S(2)}, u32[]{:S(2)}) %collective-permute-start.19) | collective-permute-done | bytes 847904 | tf_op jit(solution)/shard_map/ppermute | solution.py:49
  387.7 5.8 %collective-permute-done.28 = f32[3304]{0:T(1024)S(1)} collective-permute-done((f32[3304]{0:T(1024)S(1)}, f32[3304]{0:T(1024)S(1)}, u32[]{:S(2)}, u32[]{:S(2)}) %collective-permute-start.28) | collective-permute-done | bytes 13248 | tf_op jit(solution)/shard_map/ppermute | solution.py:114
  416.6 104.8 %reduce-scatter.5.cloned.1.call-done = bf16[72,4352]{1,0:T(8,128)(2,1)} async-done(((bf16[1152,4352]{1,0:T(8,128)(2,1)}), bf16[72,4352]{1,0:T(8,128)(2,1)}) %reduce-scatter.5.cloned.1.call-update) | async-done | bytes 626704 | tf_op jit(solution)/shard_map/reduce_scatter | solution.py:270
  (304 shorter events, 183.4 us)
Async XLA Ops:
  7.2 65.9 %all-gather.3.cloned.1.call-start = ((), (), s32[]{:S(2)}) async-start(), calls=%async_computation.2 | async-start | bytes 6266880 | tf_op jit(solution)/shard_map/all_gather | solution.py:180
  9.2 150.9 %all-gather.5.cloned.1.call-start = ((), (), s32[]{:S(2)}) async-start(), calls=%async_computation.3 | async-start | bytes 10653696 | tf_op jit(solution)/shard_map/all_gather | solution.py:182
  11.2 401.8 %reduce-scatter.7.cloned.1.call-start = ((), (), s32[]{:S(2)}) async-start(), calls=%async_computation.5 | async-start | bytes 5953536
  11.2 4.9 collective-permute-start
  15.1 16.1 %collective-permute-start.4 = (bf16[72,6]{0,1:T(8,128)(2,1)S(1)}, bf16[72,6]{0,1:T(8,128)(2,1)S(1)}, u32[]{:S(2)}, u32[]{:S(2)}) collective-permute-start(bf16[72,6]{0,1:T(8,128)(2,1)S(1)} %stack.100), channel_id=1, source_target_pairs={{0,2},{2,0},{1,3},{3,1},{4,6},{6,4},{5,7},{7,5},{8,10},{10,8},{9,1... | collective-permute-start | bytes 2600 | tf_op jit(solution)/shard_map/ppermute | solution.py:49
  25.6 4.8 collective-permute-start.3
  38.6 4.7 collective-permute-start.7
  43.9 40.9 %collective-permute-start.8 = (bf16[368,1152]{1,0:T(8,128)(2,1)S(1)}, bf16[368,1152]{1,0:T(8,128)(2,1)S(1)}, u32[]{:S(2)}, u32[]{:S(2)}) collective-permute-start(bf16[368,1152]{1,0:T(8,128)(2,1)S(1)} %fusion.63), channel_id=1, source_target_pairs={{0,1},{1,0},{2,3},{3,2},{4,5},{5,4},{6,7},{7,6},{8,9},{9,8},{10,11... | collective-permute-start | bytes 2543624 | tf_op jit(solution)/shard_map/ppermute | solution.py:49
  96.5 10.4 %collective-permute-start.10 = (bf16[2,8,368,72]{2,3,0,1:T(8,128)(2,1)S(1)}, bf16[2,8,368,72]{2,3,0,1:T(8,128)(2,1)S(1)}, u32[]{:S(2)}, u32[]{:S(2)}) collective-permute-start(bf16[2,8,368,72]{2,3,0,1:T(8,128)(2,1)S(1)} %get-tuple-element.50), channel_id=1, source_target_pairs={{0,2},{2,0},{1,3},{3,1},{4,6},{6,4},{5,7},{7,5},{8,10},{10,8},{9,1... | collective-permute-start | bytes 2543624 | tf_op jit(solution)/shard_map/ppermute | solution.py:49
  117.4 21.1 %collective-permute-start.11 = (bf16[368,1152]{1,0:T(8,128)(2,1)S(1)}, bf16[368,1152]{1,0:T(8,128)(2,1)S(1)}, u32[]{:S(2)}, u32[]{:S(2)}) collective-permute-start(bf16[368,1152]{1,0:T(8,128)(2,1)S(1)} %fusion.111), channel_id=1, source_target_pairs={{0,1},{1,0},{2,3},{3,2},{4,5},{5,4},{6,7},{7,6},{8,9},{9,8},{10,11... | collective-permute-start | bytes 2543624 | tf_op jit(solution)/shard_map/ppermute | solution.py:49
  139.7 20.4 %collective-permute-start.12 = (bf16[368,1152]{1,0:T(8,128)(2,1)S(1)}, bf16[368,1152]{1,0:T(8,128)(2,1)}, u32[]{:S(2)}, u32[]{:S(2)}) collective-permute-start(bf16[368,1152]{1,0:T(8,128)(2,1)S(1)} %add_convert_fusion.1), channel_id=1, source_target_pairs={{0,1},{1,0},{2,3},{3,2},{4,5},{5,4},{6,7},{7,6},{8,9},{9,8},{10,11... | collective-permute-start | bytes 2543624 | tf_op jit(solution)/shard_map/ppermute | solution.py:49
  168.6 20.1 %collective-permute-start.13 = (bf16[368,1152]{1,0:T(8,128)(2,1)S(1)}, bf16[368,1152]{1,0:T(8,128)(2,1)S(1)}, u32[]{:S(2)}, u32[]{:S(2)}) collective-permute-start(bf16[368,1152]{1,0:T(8,128)(2,1)S(1)} %fusion.41), channel_id=1, source_target_pairs={{0,1},{1,0},{2,3},{3,2},{4,5},{5,4},{6,7},{7,6},{8,9},{9,8},{10,11... | collective-permute-start | bytes 2543624 | tf_op jit(solution)/shard_map/ppermute | solution.py:49
  190.5 19.3 %collective-permute-start.14 = (bf16[368,1152]{1,0:T(8,128)(2,1)S(1)}, bf16[368,1152]{1,0:T(8,128)(2,1)S(1)}, u32[]{:S(2)}, u32[]{:S(2)}) collective-permute-start(bf16[368,1152]{1,0:T(8,128)(2,1)S(1)} %multiply_convert_fusion.2), channel_id=1, source_target_pairs={{0,1},{1,0},{2,3},{3,2},{4,5},{5,4},{6,7},{7,6},{8,9},{9,8},{10,11... | collective-permute-start | bytes 2543624 | tf_op jit(solution)/shard_map/ppermute | solution.py:49
  216.0 18.4 %collective-permute-start.15 = (bf16[368,1152]{1,0:T(8,128)(2,1)S(1)}, bf16[368,1152]{1,0:T(8,128)(2,1)S(1)}, u32[]{:S(2)}, u32[]{:S(2)}) collective-permute-start(bf16[368,1152]{1,0:T(8,128)(2,1)S(1)} %fusion.42), channel_id=1, source_target_pairs={{0,1},{1,0},{2,3},{3,2},{4,5},{5,4},{6,7},{7,6},{8,9},{9,8},{10,11... | collective-permute-start | bytes 2543624 | tf_op jit(solution)/shard_map/ppermute | solution.py:49
  237.9 17.7 %collective-permute-start.16 = (bf16[368,1152]{1,0:T(8,128)(2,1)S(1)}, bf16[368,1152]{1,0:T(8,128)(2,1)}, u32[]{:S(2)}, u32[]{:S(2)}) collective-permute-start(bf16[368,1152]{1,0:T(8,128)(2,1)S(1)} %convert_element_type.201), channel_id=1, source_target_pairs={{0,1},{1,0},{2,3},{3,2},{4,5},{5,4},{6,7},{7,6},{8,9},{9,8},{10,11... | collective-permute-start | bytes 2543624 | tf_op jit(solution)/shard_map/ppermute | solution.py:49
  262.7 41.7 %collective-permute-start.18 = (bf16[2,8,368,72]{2,3,1,0:T(8,128)(2,1)}, bf16[2,8,368,72]{2,3,1,0:T(8,128)(2,1)}, u32[]{:S(2)}, u32[]{:S(2)}) collective-permute-start(bf16[2,8,368,72]{2,3,1,0:T(8,128)(2,1)} %fusion.58), channel_id=1, source_target_pairs={{0,2},{2,0},{1,3},{3,1},{4,6},{6,4},{5,7},{7,5},{8,10},{10,8},{9,1... | collective-permute-start | bytes 2543624 | tf_op jit(solution)/shard_map/ppermute | solution.py:49
  291.1 15.6 %collective-permute-start.17 = (bf16[2,8,368,72]{2,3,1,0:T(8,128)(2,1)}, bf16[2,8,368,72]{2,3,1,0:T(8,128)(2,1)}, u32[]{:S(2)}, u32[]{:S(2)}) collective-permute-start(bf16[2,8,368,72]{2,3,1,0:T(8,128)(2,1)} %fusion.59), channel_id=1, source_target_pairs={{0,2},{2,0},{1,3},{3,1},{4,6},{6,4},{5,7},{7,5},{8,10},{10,8},{9,1... | collective-permute-start | bytes 2543624 | tf_op jit(solution)/shard_map/ppermute | solution.py:49
  326.0 195.4 %reduce-scatter.5.cloned.1.call-start = ((), (), s32[]{:S(2)}) async-start(), calls=%async_computation.4 | async-start | bytes 10653696 | tf_op jit(solution)/shard_map/reduce_scatter | solution.py:270
  360.0 21.3 %collective-permute-start.19 = (bf16[368,1152]{1,0:T(8,128)(2,1)}, bf16[368,1152]{1,0:T(8,128)(2,1)S(1)}, u32[]{:S(2)}, u32[]{:S(2)}) collective-permute-start(bf16[368,1152]{1,0:T(8,128)(2,1)} %fusion.112), channel_id=1, source_target_pairs={{0,1},{1,0},{2,3},{3,2},{4,5},{5,4},{6,7},{7,6},{8,9},{9,8},{10,11... | collective-permute-start | bytes 2543624 | tf_op jit(solution)/shard_map/ppermute | solution.py:49
  365.3 18.6 %collective-permute-start.26 = (f32[3304]{0:T(1024)S(1)}, f32[3304]{0:T(1024)S(1)}, u32[]{:S(2)}, u32[]{:S(2)}) collective-permute-start(f32[3304]{0:T(1024)S(1)} %add.342), channel_id=1, source_target_pairs={{0,4},{4,0},{8,12},{12,8},{16,20},{20,16},{24,28},{28,24},{1,5},{5... | collective-permute-start | bytes 39656 | tf_op jit(solution)/shard_map/ppermute | solution.py:114
  383.8 9.7 %collective-permute-start.20 = (f32[6913]{0:T(1024)S(1)}, f32[6913]{0:T(1024)S(1)}, u32[]{:S(2)}, u32[]{:S(2)}) collective-permute-start(f32[6913]{0:T(1024)S(1)} %constant_dynamic-update-slice_fusion), channel_id=1, source_target_pairs={{0,2},{2,0},{1,3},{3,1},{4,6},{6,4},{5,7},{7,5},{8,10},{10,8},{9,1... | collective-permute-start | bytes 82964 | tf_op jit(solution)/shard_map/ppermute | solution.py:114
  387.7 5.8 %collective-permute-start.28 = (f32[3304]{0:T(1024)S(1)}, f32[3304]{0:T(1024)S(1)}, u32[]{:S(2)}, u32[]{:S(2)}) collective-permute-start(f32[3304]{0:T(1024)S(1)} %add.344), channel_id=1, source_target_pairs={{0,16},{4,20},{8,24},{12,28},{16,0},{20,4},{24,8},{28,12},{1,17},{... | collective-permute-start | bytes 39656 | tf_op jit(solution)/shard_map/ppermute | solution.py:114
  401.6 5.0 collective-permute-start.23
  406.6 4.6 collective-permute-start.24
  (77 other events, 849.9 us)
Sparse Core Ops, SparseCore 0:
  10.8 62.2 all-gather.2
  75.8 83.2 all-gather.4
  326.1 78.5 reduce-scatter.6
  408.7 112.6 reduce-scatter.4

commit v9 on v8

--- a/solution.py
+++ b/solution.py
@@ -228,6 +228,11 @@
         jnp.dot(part, up_w, preferred_element_type=F32) + up_b for part in normed_two_parts
     ]
     active_parts = [gelu_tanh(part).astype(BF) for part in before_parts]
+    slope_parts = [gelu_slope(part) for part in before_parts]
+    if len(slope_parts) == 2:
+        slope_parts[0], slope_parts[1], active_parts[0] = lax.optimization_barrier(
+            (slope_parts[0], slope_parts[1], active_parts[0])
+        )
     mlp_terms = [
         jnp.einsum("rf,df->rd", part, down_wt, preferred_element_type=F32)
         for part in active_parts
@@ -247,9 +252,9 @@
     before_grad_parts = [
         (
             jnp.einsum("rd,df->rf", g, down_wt, preferred_element_type=F32)
-            * gelu_slope(p)
+            * p
         ).astype(BF)
-        for g, p in zip(grad_parts, before_parts)
+        for g, p in zip(grad_parts, slope_parts)
     ]
     norm_two_terms = [
         jnp.einsum("rf,df->rd", g, up_w, preferred_element_type=F32)

time: 537 us -> 545 us (1.015)
  matrix products: 115 us -> 124 us
    dot_general x1, matrix products: 4.94 us -> 16.2 us  [on_device_body(): jnp.einsum('bhqk,bhke->bhqe', soft_weights, value_all, preferred_element_...]
  transfers between devices with their start and end apart: 33 -> 33, of which waited for: 22 -> 22; matrix products, arithmetic and copies ran while one was open for 29% -> 30% of each run, Pallas kernels for 0% -> 0%
where the time goes in v9:
time: 545 us; the launch traced here: 541 us
  waiting for transfers between devices  256 us (47%)
  matrix products  124 us (23%)
  other arithmetic  53.4 us (10%)
  local copies, waits for them, and re-layouts  45.4 us (8%)
  starting transfers between devices  41.3 us (8%)
  between operations  20.6 us (4%)
    reduce_scatter x1, waiting for transfers between devices, on_device_body(): lax.psum_scatter(mlp_grad_pack, ('dp', 'ctx'), scatter_dimension=0, tiled...  107 us
    ppermute x13, waiting for transfers between devices, swap(): return lax.ppermute(values, axis, [(0, 1), (1, 0)])  100 us
    all_gather x1, waiting for transfers between devices, on_device_body(): attn_full = lax.all_gather(attn_pack, ('dp', 'ctx'), axis=1, tiled=True)  26.7 us
    ppermute x6, starting transfers between devices, gather_vectors(): their_blocks, their_count = lax.ppermute((blocks, count), 'dp', perm)  17.9 us
    dot_general x1, matrix products, on_device_body(): jnp.einsum('bhqk,bhke->bhqe', soft_weights, value_all, preferred_element_...  16.2 us
    ppermute x10, waiting for transfers between devices, tree_sum(): values = jax.tree.map(lambda v: v + lax.ppermute(v, axis, perm), values)  15.9 us
    unnamed x141, local copies, waits for them, and re-layouts  13.9 us
    ppermute x13, starting transfers between devices, swap(): return lax.ppermute(values, axis, [(0, 1), (1, 0)])  12.8 us
  transfers between devices with their start and end apart: 33, of which 22 were waited for; matrix products, arithmetic and copies ran while one was open for 30% of the time, Pallas kernels for 0%

profile of v9, /device:TPU:0, one launch (start us, length us, event | category | flops | bytes accessed | tf_op | source)
XLA Modules:
  0.0 540.8 jit_solution(5583302599122215924)
XLA Ops:
  46.3 26.7 %all-gather.3.cloned.1.call-done = bf16[4,1152,576]{2,1,0:T(8,128)(2,1)} async-done(((bf16[4,72,576]{2,1,0:T(8,128)(2,1)}), bf16[4,1152,576]{2,1,0:T(8,128)(2,1)}) %all-gather.3.cloned.1.call-update) | async-done | bytes 5308432 | tf_op jit(solution)/shard_map/all_gather | solution.py:180
  77.8 7.0 %copy.74 = bf16[3,1152,576]{1,2,0:T(8,128)(2,1)} copy(bf16[3,1152,576]{2,1,0:T(8,128)(2,1)} %slice.186) | data formatting | bytes 7962624 | tf_op jit(solution)/shard_map/slice | solution.py:183
  85.6 5.8 %fusion.43 = bf16[3,2,8,368,72]{3,4,1,2,0:T(8,128)(2,1)S(1)} fusion(f32[3,8,72]{2,1,0:T(8,128)S(1)} %maximum_bitcast_fusion, bf16[3,1152,8,72,1]{1,3,4,2,0:T(8,128)(2,1)} %bitcast.310, bf16[1,368,1152]{2,1,0:T(8,128)(2,1)S(1)} %bitcast.340, bf16[1,368,1152]{2,1,0:T(8,128)(2,1)S(1)} %fusion.75), kind=kOutput, calls=%fused_computation.77 | convolution fusion | flops 2936180736 | bytes 8227584 | tf_op jit(solution)/shard_map/pro,tojx->tpjrx/dot_general | solution.py:201
  97.3 5.6 %fusion.140 = (f32[2,8,368]{2,1,0:T(8,128)S(1)}, f32[2,8,368,736]{3,2,1,0:T(8,128)S(1)}) fusion(bf16[2,8,368,72]{2,3,0,1:T(8,128)(2,1)} %get-tuple-element.57, pred[736]{0:T(1024)(128)(4,1)S(1)} %fusion.118, bf16[2,8,368,72]{2,3,0,1:T(8,128)(2,1)} %collective-permute-done.9, bf16[2,8,368,72]{2,3,0,1:T(8,128)(2,1)} %get-tuple-element.59), kind=kOutput, calls=%fused_computation.250 | convolution fusion | flops 640420096 | bytes 19902176 | tf_op jit(solution)/shard_map/bhqe,bhke->bhqk/dot_general | solution.py:210
  109.1 16.2 %fusion.86 = bf16[2,8,368,72]{2,3,1,0:T(8,128)(2,1)S(1)} fusion(f32[2,8,368,736]{3,2,1,0:T(8,128)S(1)} %get-tuple-element.77, f32[2,8,368]{2,1,0:T(8,128)S(1)} %log_add_fusion, bf16[2,8,368,72]{2,3,0,1:T(8,128)(2,1)S(1)} %collective-permute-done.10, bf16[2,8,368,72]{2,3,0,1:T(8,128)(2,1)S(1)} %get-tuple-element.58), kind=kOutput, calls=%fused_computation.155 | convolution fusion | flops 636516352 | bytes 19901440 | tf_op jit(solution)/shard_map/bhqk,bhke->bhqe/dot_general | solution.py:216
  130.3 19.5 %collective-permute-done.11 = bf16[368,1152]{1,0:T(8,128)(2,1)S(1)} collective-permute-done((bf16[368,1152]{1,0:T(8,128)(2,1)S(1)}, bf16[368,1152]{1,0:T(8,128)(2,1)S(1)}, u32[]{:S(2)}, u32[]{:S(2)}) %collective-permute-start.11) | collective-permute-done | bytes 847904 | tf_op jit(solution)/shard_map/ppermute | solution.py:49
  152.6 18.8 %collective-permute-done.12 = bf16[368,1152]{1,0:T(8,128)(2,1)} collective-permute-done((bf16[368,1152]{1,0:T(8,128)(2,1)S(1)}, bf16[368,1152]{1,0:T(8,128)(2,1)}, u32[]{:S(2)}, u32[]{:S(2)}) %collective-permute-start.12) | collective-permute-done | bytes 847904 | tf_op jit(solution)/shard_map/ppermute | solution.py:49
  171.4 6.1 %fusion.39 = (f32[368,2176]{1,0:T(8,128)S(1)}, f32[368,2176]{1,0:T(8,128)S(1)}) fusion(f32[2176]{0:T(1024)S(1)} %pad_convert_fusion, bf16[368,1152]{1,0:T(8,128)(2,1)} %collective-permute-done.12, bf16[2,1152,2176]{2,1,0:T(8,128)(2,1)} %all-gather.5.cloned.1.call-done), kind=kOutput, calls=%fused_computation.70 | convolution fusion | flops 1859383296 | bytes 12276224 | tf_op jit(solution)/shard_map/dot_general | solution.py:228
  188.0 12.0 %collective-permute-done.13 = bf16[368,1152]{1,0:T(8,128)(2,1)S(1)} collective-permute-done((bf16[368,1152]{1,0:T(8,128)(2,1)S(1)}, bf16[368,1152]{1,0:T(8,128)(2,1)S(1)}, u32[]{:S(2)}, u32[]{:S(2)}) %collective-permute-start.13) | collective-permute-done | bytes 847904 | tf_op jit(solution)/shard_map/ppermute | solution.py:49
  204.0 16.2 %collective-permute-done.14 = bf16[368,1152]{1,0:T(8,128)(2,1)S(1)} collective-permute-done((bf16[368,1152]{1,0:T(8,128)(2,1)S(1)}, bf16[368,1152]{1,0:T(8,128)(2,1)S(1)}, u32[]{:S(2)}, u32[]{:S(2)}) %collective-permute-start.14) | collective-permute-done | bytes 847904 | tf_op jit(solution)/shard_map/ppermute | solution.py:49
  229.5 5.4 %fusion.27 = f32[368,1152]{1,0:T(8,128)S(1)} fusion(bf16[368,2176]{1,0:T(8,128)(2,1)S(1)} %fusion.24, bf16[2,1152,2176]{2,1,0:T(8,128)(2,1)} %all-gather.5.cloned.1.call-done), kind=kOutput, calls=%fused_computation.58 | convolution fusion | flops 1844969472 | bytes 8310784 | tf_op jit(solution)/shard_map/rf,df->rd/dot_general | solution.py:260
  234.9 7.9 %collective-permute-done.15 = bf16[368,1152]{1,0:T(8,128)(2,1)S(1)} collective-permute-done((bf16[368,1152]{1,0:T(8,128)(2,1)S(1)}, bf16[368,1152]{1,0:T(8,128)(2,1)S(1)}, u32[]{:S(2)}, u32[]{:S(2)}) %collective-permute-start.15) | collective-permute-done | bytes 847904 | tf_op jit(solution)/shard_map/ppermute | solution.py:49
  253.6 9.7 %collective-permute-done.16 = bf16[368,1152]{1,0:T(8,128)(2,1)} collective-permute-done((bf16[368,1152]{1,0:T(8,128)(2,1)S(1)}, bf16[368,1152]{1,0:T(8,128)(2,1)}, u32[]{:S(2)}, u32[]{:S(2)}) %collective-permute-start.16) | collective-permute-done | bytes 847904 | tf_op jit(solution)/shard_map/ppermute | solution.py:49
  272.7 10.6 %fusion.9 = (f32[8,368]{1,0:T(8,128)S(1)}, f32[8,368]{1,0:T(8,128)S(1)}, f32[8,368,736]{2,1,0:T(8,128)}) fusion(f32[2,8,368,736]{3,2,1,0:T(8,128)} %copy-done, f32[8,368]{1,0:T(8,128)S(1)} %get-tuple-element.72, f32[8,368,736]{2,1,0:T(8,128)S(1)} %fusion.102, f32[8,368]{1,0:T(8,128)S(1)} %get-tuple-element.73, bf16[8,368,72]{1,2,0:T(8,128)(2,1)S(1)} %fusion.93, ...), kind=kOutput, calls=%fused_computation.22 | convolution fusion | flops 326707456 | bytes 36835328 | tf_op jit(solution)/shard_map/bhqe,bhke->bhqk/dot_general | solution.py:302
  283.3 10.1 %fusion.20 = (bf16[8,368,736]{2,1,0:T(8,128)(2,1)S(1)}, bf16[8,368,736]{2,1,0:T(8,128)(2,1)S(1)}) fusion(f32[8,368,736]{2,1,0:T(8,128)} %get-tuple-element.80, f32[2,8,368,736]{3,2,1,0:T(8,128)} %copy-done, f32[8,368]{1,0:T(8,128)S(1)} %get-tuple-element.28, f32[8,368]{1,0:T(8,128)S(1)} %get-tuple-element.72, f32[8,368,736]{2,1,0:T(8,128)S(1)} %fusion.102, ...), kind=kLoop, calls=%fused_computation.42 | loop fusion | flops 17334272 | bytes 43382784 | tf_op jit(solution)/shard_map/reshape.9
  316.5 5.2 bitcast_convert_fusion
  321.7 6.6 %copy.85 = bf16[1152,1728]{1,0:T(8,128)(2,1)} copy(bf16[1152,1728]{0,1:T(8,128)(2,1)} %bitcast.312) | data formatting | bytes 7962624 | tf_op jit(solution)/shard_map/convert_element_type | solution.py:336
  328.2 5.3 fusion.13
  341.1 5.1 fusion
  346.2 5.5 %fusion.1 = bf16[1152,2176]{1,0:T(8,128)(2,1)S(1)} fusion(f32[1152,2176]{1,0:T(8,128)S(1)} %fusion.142, bf16[368,1152]{1,0:T(8,128)(2,1)S(1)} %copy-done.34, f32[368,2176]{1,0:T(8,128)} %copy-done.26), kind=kOutput, calls=%fused_computation.6 | convolution fusion | flops 1857189888 | bytes 19091456 | tf_op jit(solution)/shard_map/rd,rf->df/dot_general | solution.py:268
  351.7 4.8 pad_maximum_fusion
  357.7 6.7 %convolution_bitcast_fusion.1 = f32[2,368,1152]{2,1,0:T(8,128)S(1)} fusion(bf16[3,1152,8,72,1]{1,3,2,4,0:T(8,128)(2,1)} %bitcast.311, bf16[1,2,8,368,72]{3,4,2,1,0:T(8,128)(2,1)S(1)} %bitcast.319, bf16[1,2,8,368,72]{3,4,2,1,0:T(8,128)(2,1)} %copy-done.38, bf16[1,1,8,368,72]{3,4,2,1,0:T(8,128)(2,1)} %bitcast.324, bf16[1,1,8,368,72]{3,4,2,1,0:T(8,128)(2,1)S(1)} %bitcast.321), kind=kOutput, calls=%fused_computation.51 | convolution fusion | flops 2934061056 | bytes 9916416 | tf_op jit(solution)/shard_map/toaks,tzas->okz/dot_general | solution.py:343
  372.9 15.6 %collective-permute-done.19 = bf16[368,1152]{1,0:T(8,128)(2,1)S(1)} collective-permute-done((bf16[368,1152]{1,0:T(8,128)(2,1)}, bf16[368,1152]{1,0:T(8,128)(2,1)S(1)}, u32[]{:S(2)}, u32[]{:S(2)}) %collective-permute-start.19) | collective-permute-done | bytes 847904 | tf_op jit(solution)/shard_map/ppermute | solution.py:49
  423.1 106.9 %reduce-scatter.5.cloned.1.call-done = bf16[72,4352]{1,0:T(8,128)(2,1)} async-done(((bf16[1152,4352]{1,0:T(8,128)(2,1)}), bf16[72,4352]{1,0:T(8,128)(2,1)}) %reduce-scatter.5.cloned.1.call-update) | async-done | bytes 626704 | tf_op jit(solution)/shard_map/reduce_scatter | solution.py:275
  (304 shorter events, 181.0 us)
Async XLA Ops:
  7.2 65.8 %all-gather.3.cloned.1.call-start = ((), (), s32[]{:S(2)}) async-start(), calls=%async_computation.2 | async-start | bytes 6266880 | tf_op jit(solution)/shard_map/all_gather | solution.py:180
  9.2 162.3 %all-gather.5.cloned.1.call-start = ((), (), s32[]{:S(2)}) async-start(), calls=%async_computation.3 | async-start | bytes 10653696 | tf_op jit(solution)/shard_map/all_gather | solution.py:182
  11.2 408.3 %reduce-scatter.7.cloned.1.call-start = ((), (), s32[]{:S(2)}) async-start(), calls=%async_computation.5 | async-start | bytes 5953536
  11.2 4.9 collective-permute-start
  15.1 15.9 %collective-permute-start.4 = (bf16[72,6]{0,1:T(8,128)(2,1)S(1)}, bf16[72,6]{0,1:T(8,128)(2,1)S(1)}, u32[]{:S(2)}, u32[]{:S(2)}) collective-permute-start(bf16[72,6]{0,1:T(8,128)(2,1)S(1)} %stack.100), channel_id=1, source_target_pairs={{0,2},{2,0},{1,3},{3,1},{4,6},{6,4},{5,7},{7,5},{8,10},{10,8},{9,1... | collective-permute-start | bytes 2600 | tf_op jit(solution)/shard_map/ppermute | solution.py:49
  25.4 4.8 collective-permute-start.3
  38.5 4.7 collective-permute-start.7
  43.7 41.0 %collective-permute-start.8 = (bf16[368,1152]{1,0:T(8,128)(2,1)S(1)}, bf16[368,1152]{1,0:T(8,128)(2,1)S(1)}, u32[]{:S(2)}, u32[]{:S(2)}) collective-permute-start(bf16[368,1152]{1,0:T(8,128)(2,1)S(1)} %fusion.63), channel_id=1, source_target_pairs={{0,1},{1,0},{2,3},{3,2},{4,5},{5,4},{6,7},{7,6},{8,9},{9,8},{10,11... | collective-permute-start | bytes 2543624 | tf_op jit(solution)/shard_map/ppermute | solution.py:49
  96.6 10.4 %collective-permute-start.10 = (bf16[2,8,368,72]{2,3,0,1:T(8,128)(2,1)S(1)}, bf16[2,8,368,72]{2,3,0,1:T(8,128)(2,1)S(1)}, u32[]{:S(2)}, u32[]{:S(2)}) collective-permute-start(bf16[2,8,368,72]{2,3,0,1:T(8,128)(2,1)S(1)} %get-tuple-element.58), channel_id=1, source_target_pairs={{0,2},{2,0},{1,3},{3,1},{4,6},{6,4},{5,7},{7,5},{8,10},{10,8},{9,1... | collective-permute-start | bytes 2543624 | tf_op jit(solution)/shard_map/ppermute | solution.py:49
  128.8 21.1 %collective-permute-start.11 = (bf16[368,1152]{1,0:T(8,128)(2,1)S(1)}, bf16[368,1152]{1,0:T(8,128)(2,1)S(1)}, u32[]{:S(2)}, u32[]{:S(2)}) collective-permute-start(bf16[368,1152]{1,0:T(8,128)(2,1)S(1)} %fusion.111), channel_id=1, source_target_pairs={{0,1},{1,0},{2,3},{3,2},{4,5},{5,4},{6,7},{7,6},{8,9},{9,8},{10,11... | collective-permute-start | bytes 2543624 | tf_op jit(solution)/shard_map/ppermute | solution.py:49
  151.0 20.4 %collective-permute-start.12 = (bf16[368,1152]{1,0:T(8,128)(2,1)S(1)}, bf16[368,1152]{1,0:T(8,128)(2,1)}, u32[]{:S(2)}, u32[]{:S(2)}) collective-permute-start(bf16[368,1152]{1,0:T(8,128)(2,1)S(1)} %add_convert_fusion.1), channel_id=1, source_target_pairs={{0,1},{1,0},{2,3},{3,2},{4,5},{5,4},{6,7},{7,6},{8,9},{9,8},{10,11... | collective-permute-start | bytes 2543624 | tf_op jit(solution)/shard_map/ppermute | solution.py:49
  180.5 19.5 %collective-permute-start.13 = (bf16[368,1152]{1,0:T(8,128)(2,1)S(1)}, bf16[368,1152]{1,0:T(8,128)(2,1)S(1)}, u32[]{:S(2)}, u32[]{:S(2)}) collective-permute-start(bf16[368,1152]{1,0:T(8,128)(2,1)S(1)} %fusion.41), channel_id=1, source_target_pairs={{0,1},{1,0},{2,3},{3,2},{4,5},{5,4},{6,7},{7,6},{8,9},{9,8},{10,11... | collective-permute-start | bytes 2543624 | tf_op jit(solution)/shard_map/ppermute | solution.py:49
  201.6 18.6 %collective-permute-start.14 = (bf16[368,1152]{1,0:T(8,128)(2,1)S(1)}, bf16[368,1152]{1,0:T(8,128)(2,1)S(1)}, u32[]{:S(2)}, u32[]{:S(2)}) collective-permute-start(bf16[368,1152]{1,0:T(8,128)(2,1)S(1)} %multiply_convert_fusion.2), channel_id=1, source_target_pairs={{0,1},{1,0},{2,3},{3,2},{4,5},{5,4},{6,7},{7,6},{8,9},{9,8},{10,11... | collective-permute-start | bytes 2543624 | tf_op jit(solution)/shard_map/ppermute | solution.py:49
  225.1 17.8 %collective-permute-start.15 = (bf16[368,1152]{1,0:T(8,128)(2,1)S(1)}, bf16[368,1152]{1,0:T(8,128)(2,1)S(1)}, u32[]{:S(2)}, u32[]{:S(2)}) collective-permute-start(bf16[368,1152]{1,0:T(8,128)(2,1)S(1)} %fusion.42), channel_id=1, source_target_pairs={{0,1},{1,0},{2,3},{3,2},{4,5},{5,4},{6,7},{7,6},{8,9},{9,8},{10,11... | collective-permute-start | bytes 2543624 | tf_op jit(solution)/shard_map/ppermute | solution.py:49
  246.4 17.0 %collective-permute-start.16 = (bf16[368,1152]{1,0:T(8,128)(2,1)S(1)}, bf16[368,1152]{1,0:T(8,128)(2,1)}, u32[]{:S(2)}, u32[]{:S(2)}) collective-permute-start(bf16[368,1152]{1,0:T(8,128)(2,1)S(1)} %convert_element_type.201), channel_id=1, source_target_pairs={{0,1},{1,0},{2,3},{3,2},{4,5},{5,4},{6,7},{7,6},{8,9},{9,8},{10,11... | collective-permute-start | bytes 2543624 | tf_op jit(solution)/shard_map/ppermute | solution.py:49
  270.3 41.8 %collective-permute-start.18 = (bf16[2,8,368,72]{2,3,1,0:T(8,128)(2,1)}, bf16[2,8,368,72]{2,3,1,0:T(8,128)(2,1)}, u32[]{:S(2)}, u32[]{:S(2)}) collective-permute-start(bf16[2,8,368,72]{2,3,1,0:T(8,128)(2,1)} %fusion.58), channel_id=1, source_target_pairs={{0,2},{2,0},{1,3},{3,1},{4,6},{6,4},{5,7},{7,5},{8,10},{10,8},{9,1... | collective-permute-start | bytes 2543624 | tf_op jit(solution)/shard_map/ppermute | solution.py:49
  298.8 15.5 %collective-permute-start.17 = (bf16[2,8,368,72]{2,3,1,0:T(8,128)(2,1)}, bf16[2,8,368,72]{2,3,1,0:T(8,128)(2,1)}, u32[]{:S(2)}, u32[]{:S(2)}) collective-permute-start(bf16[2,8,368,72]{2,3,1,0:T(8,128)(2,1)} %fusion.59), channel_id=1, source_target_pairs={{0,2},{2,0},{1,3},{3,1},{4,6},{6,4},{5,7},{7,5},{8,10},{10,8},{9,1... | collective-permute-start | bytes 2543624 | tf_op jit(solution)/shard_map/ppermute | solution.py:49
  333.6 196.4 %reduce-scatter.5.cloned.1.call-start = ((), (), s32[]{:S(2)}) async-start(), calls=%async_computation.4 | async-start | bytes 10653696 | tf_op jit(solution)/shard_map/reduce_scatter | solution.py:275
  367.2 21.3 %collective-permute-start.19 = (bf16[368,1152]{1,0:T(8,128)(2,1)}, bf16[368,1152]{1,0:T(8,128)(2,1)S(1)}, u32[]{:S(2)}, u32[]{:S(2)}) collective-permute-start(bf16[368,1152]{1,0:T(8,128)(2,1)} %fusion.112), channel_id=1, source_target_pairs={{0,1},{1,0},{2,3},{3,2},{4,5},{5,4},{6,7},{7,6},{8,9},{9,8},{10,11... | collective-permute-start | bytes 2543624 | tf_op jit(solution)/shard_map/ppermute | solution.py:49
  372.3 18.8 %collective-permute-start.26 = (f32[3304]{0:T(1024)S(1)}, f32[3304]{0:T(1024)S(1)}, u32[]{:S(2)}, u32[]{:S(2)}) collective-permute-start(f32[3304]{0:T(1024)S(1)} %add.342), channel_id=1, source_target_pairs={{0,4},{4,0},{8,12},{12,8},{16,20},{20,16},{24,28},{28,24},{1,5},{5... | collective-permute-start | bytes 39656 | tf_op jit(solution)/shard_map/ppermute | solution.py:114
  391.0 8.8 %collective-permute-start.20 = (f32[6913]{0:T(1024)S(1)}, f32[6913]{0:T(1024)S(1)}, u32[]{:S(2)}, u32[]{:S(2)}) collective-permute-start(f32[6913]{0:T(1024)S(1)} %constant_dynamic-update-slice_fusion), channel_id=1, source_target_pairs={{0,2},{2,0},{1,3},{3,1},{4,6},{6,4},{5,7},{7,5},{8,10},{10,8},{9,1... | collective-permute-start | bytes 82964 | tf_op jit(solution)/shard_map/ppermute | solution.py:114
  394.9 4.9 collective-permute-start.28
  403.8 4.9 collective-permute-start.22
  408.7 4.8 collective-permute-start.23
  (77 other events, 773.1 us)
Sparse Core Ops, SparseCore 0:
  10.8 62.1 all-gather.2
  75.8 83.2 all-gather.4
  333.7 79.7 reduce-scatter.6
  417.4 112.4 reduce-scatter.4

commit v10 on v8

--- a/solution.py
+++ b/solution.py
@@ -243,29 +243,50 @@
     factor = slot_total * (half_len * lax.axis_size("ctx")) / valid_count
     grad_out = error_rows * (valid_rows[:, None] * factor)
 
-    grad_parts = tensor_gather_parts(grad_out.astype(BF))
-    before_grad_parts = [
+    grad_rows = grad_out.astype(BF)
+    cut = (rows // 2) // 16 * 16
+    if n_t == 2 and rows % 16 == 0 and cut > 0:
+        chunks = [(grad_rows, active_parts[0], before_parts[0], normed_two_parts[0])]
+        owners = [0]
+        for lo, hi in ((0, cut), (cut, rows)):
+            chunks.append(
+                (
+                    swap(grad_rows[lo:hi], "tensor"),
+                    active_parts[1][lo:hi],
+                    before_parts[1][lo:hi],
+                    normed_two_parts[1][lo:hi],
+                )
+            )
+            owners.append(1)
+    else:
+        grad_parts = tensor_gather_parts(grad_rows)
+        chunks = list(zip(grad_parts, active_parts, before_parts, normed_two_parts))
+        owners = list(range(len(chunks)))
+    before_grad_chunks = [
         (
             jnp.einsum("rd,df->rf", g, down_wt, preferred_element_type=F32)
             * gelu_slope(p)
         ).astype(BF)
-        for g, p in zip(grad_parts, before_parts)
+        for g, _, p, _ in chunks
+    ]
+    term_chunks = [
+        jnp.einsum("rf,df->rd", g, up_w, preferred_element_type=F32)
+        for g in before_grad_chunks
     ]
     norm_two_terms = [
-        jnp.einsum("rf,df->rd", g, up_w, preferred_element_type=F32)
-        for g in before_grad_parts
+        jnp.concatenate([t for t, o in zip(term_chunks, owners) if o == k])
+        for k in range(n_t)
     ]
     down_grad_t = None
     up_grad = None
-    for g, a_part, n_part, p_grad in zip(
-        grad_parts, active_parts, normed_two_parts, before_grad_parts
-    ):
+    up_bias_grad = None
+    for (g, a_part, _, n_part), p_grad in zip(chunks, before_grad_chunks):
         down_term = jnp.einsum("rd,rf->df", g, a_part, preferred_element_type=F32)
         up_term = jnp.einsum("rd,rf->df", n_part, p_grad, preferred_element_type=F32)
+        bias_term = jnp.sum(p_grad[:, :hidden_width], axis=0, dtype=F32)
         down_grad_t = down_term if down_grad_t is None else down_grad_t + down_term
         up_grad = up_term if up_grad is None else up_grad + up_term
-    before_grad = jnp.concatenate(before_grad_parts)
-    up_bias_grad = jnp.sum(before_grad[:, :hidden_width], axis=0, dtype=F32)
+        up_bias_grad = bias_term if up_bias_grad is None else up_bias_grad + bias_term
     mlp_grad_pack = jnp.concatenate([up_grad.astype(BF), down_grad_t.astype(BF)], axis=1)
     mlp_grads = lax.psum_scatter(
         mlp_grad_pack, ("dp", "ctx"), scatter_dimension=0, tiled=True

time: 537 us -> 534 us (level)
  waiting for transfers between devices: 261 us -> 221 us
  matrix products: 115 us -> 138 us
  starting transfers between devices: 37.3 us -> 47.9 us
    reduce_scatter x1, waiting for transfers between devices: 105 us -> 82.2 us  [on_device_body(): lax.psum_scatter(mlp_grad_pack, ('dp', 'ctx'), scatter_dimension=0, tiled...]
    dot_general x2 -> x3, matrix products: 8.4 us -> 22.3 us  [on_device_body(): down_term = jnp.einsum('rd,rf->df', g, a_part, preferred_element_type=F32)]
    dot_general x2 -> x3, matrix products: 8.05 us -> 18.2 us  [on_device_body(): jnp.einsum('rd,rf->df', n_part, p_grad, preferred_element_type=F32)]
    ppermute x10, waiting for transfers between devices: 21.2 us -> 12.2 us  [tree_sum(): values = jax.tree.map(lambda v: v + lax.ppermute(v, axis, perm), values)]
    ppermute x10, starting transfers between devices: 5.64 us -> 14.1 us  [tree_sum(): values = jax.tree.map(lambda v: v + lax.ppermute(v, axis, perm), values)]
    ppermute x13 -> x14, waiting for transfers between devices: 102 us -> 94 us  [swap(): return lax.ppermute(values, axis, [(0, 1), (1, 0)])]
    ppermute x13 -> x14, starting transfers between devices: 13 us -> 15.3 us  [swap(): return lax.ppermute(values, axis, [(0, 1), (1, 0)])]
    unnamed x141 -> x169, local copies, waits for them, and re-layouts: 14 us -> 12.3 us
  transfers between devices with their start and end apart: 33 -> 34, of which waited for: 22 -> 22; matrix products, arithmetic and copies ran while one was open for 29% -> 35% of each run, Pallas kernels for 0% -> 0%
where the time goes in v10:
time: 534 us; the launch traced here: 529 us
  waiting for transfers between devices  221 us (41%)
  matrix products  138 us (26%)
  other arithmetic  54 us (10%)
  starting transfers between devices  47.9 us (9%)
  local copies, waits for them, and re-layouts  47.2 us (9%)
  between operations  21.5 us (4%)
    ppermute x14, waiting for transfers between devices, swap(): return lax.ppermute(values, axis, [(0, 1), (1, 0)])  94 us
    reduce_scatter x1, waiting for transfers between devices, on_device_body(): lax.psum_scatter(mlp_grad_pack, ('dp', 'ctx'), scatter_dimension=0, tiled...  82.2 us
    all_gather x1, waiting for transfers between devices, on_device_body(): attn_full = lax.all_gather(attn_pack, ('dp', 'ctx'), axis=1, tiled=True)  26.7 us
    dot_general x3, matrix products, on_device_body(): down_term = jnp.einsum('rd,rf->df', g, a_part, preferred_element_type=F32)  22.3 us
    dot_general x3, matrix products, on_device_body(): jnp.einsum('rd,rf->df', n_part, p_grad, preferred_element_type=F32)  18.2 us
    ppermute x6, starting transfers between devices, gather_vectors(): their_blocks, their_count = lax.ppermute((blocks, count), 'dp', perm)  18.1 us
    ppermute x14, starting transfers between devices, swap(): return lax.ppermute(values, axis, [(0, 1), (1, 0)])  15.3 us
    ppermute x10, starting transfers between devices, tree_sum(): values = jax.tree.map(lambda v: v + lax.ppermute(v, axis, perm), values)  14.1 us
  transfers between devices with their start and end apart: 34, of which 22 were waited for; matrix products, arithmetic and copies ran while one was open for 35% of the time, Pallas kernels for 0%

profile of v10, /device:TPU:0, one launch (start us, length us, event | category | flops | bytes accessed | tf_op | source)
XLA Modules:
  0.0 529.2 jit_solution(9196430323223045579)
XLA Ops:
  46.4 26.7 %all-gather.3.cloned.1.call-done = bf16[4,1152,576]{2,1,0:T(8,128)(2,1)} async-done(((bf16[4,72,576]{2,1,0:T(8,128)(2,1)}), bf16[4,1152,576]{2,1,0:T(8,128)(2,1)}) %all-gather.3.cloned.1.call-update) | async-done | bytes 5308432 | tf_op jit(solution)/shard_map/all_gather | solution.py:180
  77.9 7.2 %copy.74 = bf16[3,1152,576]{1,2,0:T(8,128)(2,1)} copy(bf16[3,1152,576]{2,1,0:T(8,128)(2,1)} %slice.226) | data formatting | bytes 7962624 | tf_op jit(solution)/shard_map/slice | solution.py:183
  86.0 5.8 %fusion.40 = bf16[3,2,8,368,72]{3,4,1,2,0:T(8,128)(2,1)S(1)} fusion(f32[3,8,72]{2,1,0:T(8,128)S(1)} %maximum_bitcast_fusion, bf16[3,1152,8,72,1]{1,3,4,2,0:T(8,128)(2,1)} %bitcast.312, bf16[1,368,1152]{2,1,0:T(8,128)(2,1)S(1)} %bitcast.342, bf16[1,368,1152]{2,1,0:T(8,128)(2,1)S(1)} %fusion.78), kind=kOutput, calls=%fused_computation.73 | convolution fusion | flops 2936180736 | bytes 8227584 | tf_op jit(solution)/shard_map/pro,tojx->tpjrx/dot_general | solution.py:201
  99.7 5.6 %fusion.160 = (f32[2,8,368]{2,1,0:T(8,128)S(1)}, f32[2,8,368,736]{3,2,1,0:T(8,128)S(1)}) fusion(bf16[2,8,368,72]{2,3,0,1:T(8,128)(2,1)} %get-tuple-element.49, pred[736]{0:T(1024)(128)(4,1)S(1)} %fusion.137, bf16[2,8,368,72]{2,3,0,1:T(8,128)(2,1)} %collective-permute-done.9, bf16[2,8,368,72]{2,3,0,1:T(8,128)(2,1)} %get-tuple-element.51), kind=kOutput, calls=%fused_computation.277 | convolution fusion | flops 640420096 | bytes 19902176 | tf_op jit(solution)/shard_map/bhqe,bhke->bhqk/dot_general | solution.py:210
  121.1 19.7 %collective-permute-done.11 = bf16[368,1152]{1,0:T(8,128)(2,1)S(1)} collective-permute-done((bf16[368,1152]{1,0:T(8,128)(2,1)S(1)}, bf16[368,1152]{1,0:T(8,128)(2,1)S(1)}, u32[]{:S(2)}, u32[]{:S(2)}) %collective-permute-start.11) | collective-permute-done | bytes 847904 | tf_op jit(solution)/shard_map/ppermute | solution.py:49
  143.5 18.9 %collective-permute-done.12 = bf16[368,1152]{1,0:T(8,128)(2,1)} collective-permute-done((bf16[368,1152]{1,0:T(8,128)(2,1)S(1)}, bf16[368,1152]{1,0:T(8,128)(2,1)}, u32[]{:S(2)}, u32[]{:S(2)}) %collective-permute-start.12) | collective-permute-done | bytes 847904 | tf_op jit(solution)/shard_map/ppermute | solution.py:49
  177.2 12.5 %collective-permute-done.13 = bf16[368,1152]{1,0:T(8,128)(2,1)S(1)} collective-permute-done((bf16[368,1152]{1,0:T(8,128)(2,1)S(1)}, bf16[368,1152]{1,0:T(8,128)(2,1)S(1)}, u32[]{:S(2)}, u32[]{:S(2)}) %collective-permute-start.13) | collective-permute-done | bytes 847904 | tf_op jit(solution)/shard_map/ppermute | solution.py:49
  195.1 8.6 %collective-permute-done.14 = bf16[176,1152]{1,0:T(8,128)(2,1)S(1)} collective-permute-done((bf16[176,1152]{1,0:T(8,128)(2,1)S(1)}, bf16[176,1152]{1,0:T(8,128)(2,1)S(1)}, u32[]{:S(2)}, u32[]{:S(2)}) %collective-permute-start.14) | collective-permute-done | bytes 405536 | tf_op jit(solution)/shard_map/ppermute | solution.py:49
  219.1 5.4 %fusion.43 = f32[368,1152]{1,0:T(8,128)S(1)} fusion(bf16[368,2176]{1,0:T(8,128)(2,1)S(1)} %fusion.26, bf16[2,1152,2176]{2,1,0:T(8,128)(2,1)} %all-gather.5.cloned.1.call-done), kind=kOutput, calls=%fused_computation.77 | convolution fusion | flops 1844969472 | bytes 8310784 | tf_op jit(solution)/shard_map/rf,df->rd/dot_general | solution.py:273
  224.6 6.7 %collective-permute-done.16 = bf16[368,1152]{1,0:T(8,128)(2,1)S(1)} collective-permute-done((bf16[368,1152]{1,0:T(8,128)(2,1)S(1)}, bf16[368,1152]{1,0:T(8,128)(2,1)S(1)}, u32[]{:S(2)}, u32[]{:S(2)}) %collective-permute-start.16) | collective-permute-done | bytes 847904 | tf_op jit(solution)/shard_map/ppermute | solution.py:49
  242.5 9.3 %collective-permute-done.17 = bf16[368,1152]{1,0:T(8,128)(2,1)} collective-permute-done((bf16[368,1152]{1,0:T(8,128)(2,1)S(1)}, bf16[368,1152]{1,0:T(8,128)(2,1)}, u32[]{:S(2)}, u32[]{:S(2)}) %collective-permute-start.17) | collective-permute-done | bytes 847904 | tf_op jit(solution)/shard_map/ppermute | solution.py:49
  261.1 10.7 %fusion.11 = (f32[8,368]{1,0:T(8,128)S(1)}, f32[8,368]{1,0:T(8,128)S(1)}, f32[8,368,736]{2,1,0:T(8,128)}) fusion(f32[2,8,368,736]{3,2,1,0:T(8,128)} %copy-done, f32[8,368]{1,0:T(8,128)S(1)} %get-tuple-element.64, f32[8,368,736]{2,1,0:T(8,128)S(1)} %fusion.115, f32[8,368]{1,0:T(8,128)S(1)} %get-tuple-element.65, bf16[8,368,72]{1,2,0:T(8,128)(2,1)S(1)} %fusion.106, ...), kind=kOutput, calls=%fused_computation.24 | convolution fusion | flops 326707456 | bytes 36835328 | tf_op jit(solution)/shard_map/bhqe,bhke->bhqk/dot_general | solution.py:318
  271.8 9.9 %fusion.22 = (bf16[8,368,736]{2,1,0:T(8,128)(2,1)S(1)}, bf16[8,368,736]{2,1,0:T(8,128)(2,1)S(1)}) fusion(f32[8,368,736]{2,1,0:T(8,128)} %get-tuple-element.72, f32[2,8,368,736]{3,2,1,0:T(8,128)} %copy-done, f32[8,368]{1,0:T(8,128)S(1)} %get-tuple-element.22, f32[8,368]{1,0:T(8,128)S(1)} %get-tuple-element.64, f32[8,368,736]{2,1,0:T(8,128)S(1)} %fusion.115, ...), kind=kLoop, calls=%fused_computation.41 | loop fusion | flops 17334272 | bytes 43382784 | tf_op jit(solution)/shard_map/reshape.9
  310.0 6.6 %copy.85 = bf16[1152,1728]{1,0:T(8,128)(2,1)} copy(bf16[1152,1728]{0,1:T(8,128)(2,1)} %bitcast.314) | data formatting | bytes 7962624 | tf_op jit(solution)/shard_map/convert_element_type | solution.py:352
  316.5 5.3 %fusion.15 = bf16[1152,2368]{1,0:T(8,128)(2,1)} fusion(bf16[1152,576]{1,0:T(8,128)(2,1)S(1)} %copy-done.18, bf16[1152,1728]{1,0:T(8,128)(2,1)} %copy.85), kind=kLoop, calls=%fused_computation.29 | loop fusion | flops 16367616 | bytes 10764288 | tf_op jit(solution)/shard_map/concatenate | solution.py:351
  326.4 7.2 %fusion.151 = f32[1152,2176]{1,0:T(8,128)} fusion(bf16[368,1152]{1,0:T(8,128)(2,1)S(1)} %copy-done.14, f32[368,2176]{1,0:T(8,128)S(1)} %copy-done.29), kind=kOutput, calls=%fused_computation.270 | convolution fusion | flops 1852176384 | bytes 14077952 | tf_op jit(solution)/shard_map/rd,rf->df/dot_general | solution.py:284
  333.7 5.7 %fusion.128 = f32[1152,2176]{1,0:T(8,128)} fusion(bf16[192,1152]{1,0:T(8,128)(2,1)S(1)} %copy-done.46, bf16[368,2176]{1,0:T(8,128)(2,1)S(1)} %copy-done.38), kind=kOutput, calls=%fused_computation.206 | convolution fusion | flops 962592768 | bytes 11304960 | tf_op jit(solution)/shard_map/rd,rf->df/dot_general | solution.py:284
  339.4 6.6 %fusion.132 = f32[1152,2176]{1,0:T(8,128)} fusion(bf16[192,2176]{1,0:T(8,128)(2,1)S(1)} %copy-done.26, bf16[368,1152]{1,0:T(8,128)(2,1)} %collective-permute-done.12), kind=kOutput, calls=%fused_computation.211 | convolution fusion | flops 962592768 | bytes 11304960 | tf_op jit(solution)/shard_map/rd,rf->df/dot_general | solution.py:285
  346.0 9.3 %fusion.2 = bf16[1152,2176]{1,0:T(8,128)(2,1)S(1)} fusion(f32[1152,2176]{1,0:T(8,128)} %fusion.128, f32[1152,2176]{1,0:T(8,128)} %fusion.151, bf16[176,1152]{1,0:T(8,128)(2,1)S(1)} %copy-done.53, bf16[368,2176]{1,0:T(8,128)(2,1)} %copy-done.37), kind=kOutput, calls=%fused_computation.7 | convolution fusion | flops 889896960 | bytes 26238976 | tf_op jit(solution)/shard_map/rd,rf->df/dot_general | solution.py:284
  355.3 8.7 %fusion.3 = bf16[1152,2176]{1,0:T(8,128)(2,1)} fusion(f32[1152,2176]{1,0:T(8,128)} %fusion.132, f32[1152,2176]{1,0:T(8,128)S(1)} %fusion.161, bf16[176,2176]{1,0:T(8,128)(2,1)S(1)} %copy-done.31, bf16[368,1152]{1,0:T(8,128)(2,1)} %collective-permute-done.12), kind=kOutput, calls=%fused_computation.8 | convolution fusion | flops 889896960 | bytes 26238976 | tf_op jit(solution)/shard_map/rd,rf->df/dot_general | solution.py:285
  364.0 7.0 %pad_maximum_fusion = bf16[1152,4352]{1,0:T(8,128)(2,1)} fusion(bf16[1152,2176]{1,0:T(8,128)(2,1)S(1)} %fusion.2, bf16[1152,2176]{1,0:T(8,128)(2,1)} %fusion.3), kind=kLoop, calls=%fused_computation.11 | loop fusion | flops 20054016 | bytes 20054016 | tf_op jit(solution)/shard_map/concatenate | solution.py:290
  372.3 6.4 %convolution_bitcast_fusion.1 = f32[2,368,1152]{2,1,0:T(8,128)S(1)} fusion(bf16[3,1152,8,72,1]{1,3,2,4,0:T(8,128)(2,1)} %bitcast.313, bf16[1,2,8,368,72]{3,4,2,1,0:T(8,128)(2,1)S(1)} %bitcast.321, bf16[1,2,8,368,72]{3,4,2,1,0:T(8,128)(2,1)} %copy-done.42, bf16[1,1,8,368,72]{3,4,2,1,0:T(8,128)(2,1)S(1)} %bitcast.323, bf16[1,1,8,368,72]{3,4,2,1,0:T(8,128)(2,1)} %bitcast.326), kind=kOutput, calls=%fused_computation.53 | convolution fusion | flops 2934061056 | bytes 9916416 | tf_op jit(solution)/shard_map/toaks,tzas->okz/dot_general | solution.py:359
  385.1 16.2 %collective-permute-done.20 = bf16[368,1152]{1,0:T(8,128)(2,1)S(1)} collective-permute-done((bf16[368,1152]{1,0:T(8,128)(2,1)}, bf16[368,1152]{1,0:T(8,128)(2,1)S(1)}, u32[]{:S(2)}, u32[]{:S(2)}) %collective-permute-start.20) | collective-permute-done | bytes 847904 | tf_op jit(solution)/shard_map/ppermute | solution.py:49
  435.8 82.2 %reduce-scatter.5.cloned.1.call-done = bf16[72,4352]{1,0:T(8,128)(2,1)} async-done(((bf16[1152,4352]{1,0:T(8,128)(2,1)}), bf16[72,4352]{1,0:T(8,128)(2,1)}) %reduce-scatter.5.cloned.1.call-update) | async-done | bytes 626704 | tf_op jit(solution)/shard_map/reduce_scatter | solution.py:291
  (343 shorter events, 199.3 us)
Async XLA Ops:
  7.3 65.8 %all-gather.3.cloned.1.call-start = ((), (), s32[]{:S(2)}) async-start(), calls=%async_computation.2 | async-start | bytes 6266880 | tf_op jit(solution)/shard_map/all_gather | solution.py:180
  9.2 153.1 %all-gather.5.cloned.1.call-start = ((), (), s32[]{:S(2)}) async-start(), calls=%async_computation.3 | async-start | bytes 10653696 | tf_op jit(solution)/shard_map/all_gather | solution.py:182
  11.3 420.9 %reduce-scatter.7.cloned.1.call-start = ((), (), s32[]{:S(2)}) async-start(), calls=%async_computation.5 | async-start | bytes 5953536
  11.4 19.6 %collective-permute-start.4 = (bf16[72,6]{0,1:T(8,128)(2,1)S(1)}, bf16[72,6]{0,1:T(8,128)(2,1)S(1)}, u32[]{:S(2)}, u32[]{:S(2)}) collective-permute-start(bf16[72,6]{0,1:T(8,128)(2,1)S(1)} %stack.100), channel_id=1, source_target_pairs={{0,2},{2,0},{1,3},{3,1},{4,6},{6,4},{5,7},{7,5},{8,10},{10,8},{9,1... | collective-permute-start | bytes 2600 | tf_op jit(solution)/shard_map/ppermute | solution.py:49
  38.5 4.7 collective-permute-start.7
  43.7 41.3 %collective-permute-start.8 = (bf16[368,1152]{1,0:T(8,128)(2,1)S(1)}, bf16[368,1152]{1,0:T(8,128)(2,1)S(1)}, u32[]{:S(2)}, u32[]{:S(2)}) collective-permute-start(bf16[368,1152]{1,0:T(8,128)(2,1)S(1)} %fusion.66), channel_id=1, source_target_pairs={{0,1},{1,0},{2,3},{3,2},{4,5},{5,4},{6,7},{7,6},{8,9},{9,8},{10,11... | collective-permute-start | bytes 2543624 | tf_op jit(solution)/shard_map/ppermute | solution.py:49
  93.9 5.8 %collective-permute-start.9 = (bf16[2,8,368,72]{2,3,0,1:T(8,128)(2,1)}, bf16[2,8,368,72]{2,3,0,1:T(8,128)(2,1)}, u32[]{:S(2)}, u32[]{:S(2)}) collective-permute-start(bf16[2,8,368,72]{2,3,0,1:T(8,128)(2,1)} %get-tuple-element.51), channel_id=1, source_target_pairs={{0,2},{2,0},{1,3},{3,1},{4,6},{6,4},{5,7},{7,5},{8,10},{10,8},{9,1... | collective-permute-start | bytes 2543624 | tf_op jit(solution)/shard_map/ppermute | solution.py:49
  94.2 15.2 %collective-permute-start.10 = (bf16[2,8,368,72]{2,3,0,1:T(8,128)(2,1)S(1)}, bf16[2,8,368,72]{2,3,0,1:T(8,128)(2,1)S(1)}, u32[]{:S(2)}, u32[]{:S(2)}) collective-permute-start(bf16[2,8,368,72]{2,3,0,1:T(8,128)(2,1)S(1)} %get-tuple-element.50), channel_id=1, source_target_pairs={{0,2},{2,0},{1,3},{3,1},{4,6},{6,4},{5,7},{7,5},{8,10},{10,8},{9,1... | collective-permute-start | bytes 2543624 | tf_op jit(solution)/shard_map/ppermute | solution.py:49
  119.9 21.0 %collective-permute-start.11 = (bf16[368,1152]{1,0:T(8,128)(2,1)S(1)}, bf16[368,1152]{1,0:T(8,128)(2,1)S(1)}, u32[]{:S(2)}, u32[]{:S(2)}) collective-permute-start(bf16[368,1152]{1,0:T(8,128)(2,1)S(1)} %fusion.124), channel_id=1, source_target_pairs={{0,1},{1,0},{2,3},{3,2},{4,5},{5,4},{6,7},{7,6},{8,9},{9,8},{10,11... | collective-permute-start | bytes 2543624 | tf_op jit(solution)/shard_map/ppermute | solution.py:49
  142.0 20.3 %collective-permute-start.12 = (bf16[368,1152]{1,0:T(8,128)(2,1)S(1)}, bf16[368,1152]{1,0:T(8,128)(2,1)}, u32[]{:S(2)}, u32[]{:S(2)}) collective-permute-start(bf16[368,1152]{1,0:T(8,128)(2,1)S(1)} %add_convert_fusion.1), channel_id=1, source_target_pairs={{0,1},{1,0},{2,3},{3,2},{4,5},{5,4},{6,7},{7,6},{8,9},{9,8},{10,11... | collective-permute-start | bytes 2543624 | tf_op jit(solution)/shard_map/ppermute | solution.py:49
  170.4 19.4 %collective-permute-start.13 = (bf16[368,1152]{1,0:T(8,128)(2,1)S(1)}, bf16[368,1152]{1,0:T(8,128)(2,1)S(1)}, u32[]{:S(2)}, u32[]{:S(2)}) collective-permute-start(bf16[368,1152]{1,0:T(8,128)(2,1)S(1)} %convolution_convert_fusion), channel_id=1, source_target_pairs={{0,1},{1,0},{2,3},{3,2},{4,5},{5,4},{6,7},{7,6},{8,9},{9,8},{10,11... | collective-permute-start | bytes 2543624 | tf_op jit(solution)/shard_map/ppermute | solution.py:49
  191.4 12.3 %collective-permute-start.14 = (bf16[176,1152]{1,0:T(8,128)(2,1)S(1)}, bf16[176,1152]{1,0:T(8,128)(2,1)S(1)}, u32[]{:S(2)}, u32[]{:S(2)}) collective-permute-start(bf16[176,1152]{1,0:T(8,128)(2,1)S(1)} %slice.243), channel_id=1, source_target_pairs={{0,1},{1,0},{2,3},{3,2},{4,5},{5,4},{6,7},{7,6},{8,9},{9,8},{10,11... | collective-permute-start | bytes 1216520 | tf_op jit(solution)/shard_map/ppermute | solution.py:49
  193.9 16.0 %collective-permute-start.15 = (bf16[192,1152]{1,0:T(8,128)(2,1)S(1)}, bf16[192,1152]{1,0:T(8,128)(2,1)S(1)}, u32[]{:S(2)}, u32[]{:S(2)}) collective-permute-start(bf16[192,1152]{1,0:T(8,128)(2,1)S(1)} %slice.245), channel_id=1, source_target_pairs={{0,1},{1,0},{2,3},{3,2},{4,5},{5,4},{6,7},{7,6},{8,9},{9,8},{10,11... | collective-permute-start | bytes 1327112 | tf_op jit(solution)/shard_map/ppermute | solution.py:49
  213.5 17.7 %collective-permute-start.16 = (bf16[368,1152]{1,0:T(8,128)(2,1)S(1)}, bf16[368,1152]{1,0:T(8,128)(2,1)S(1)}, u32[]{:S(2)}, u32[]{:S(2)}) collective-permute-start(bf16[368,1152]{1,0:T(8,128)(2,1)S(1)} %pad_maximum_fusion.9), channel_id=1, source_target_pairs={{0,1},{1,0},{2,3},{3,2},{4,5},{5,4},{6,7},{7,6},{8,9},{9,8},{10,11... | collective-permute-start | bytes 2543624 | tf_op jit(solution)/shard_map/ppermute | solution.py:49
  234.8 17.0 %collective-permute-start.17 = (bf16[368,1152]{1,0:T(8,128)(2,1)S(1)}, bf16[368,1152]{1,0:T(8,128)(2,1)}, u32[]{:S(2)}, u32[]{:S(2)}) collective-permute-start(bf16[368,1152]{1,0:T(8,128)(2,1)S(1)} %convert_element_type.208), channel_id=1, source_target_pairs={{0,1},{1,0},{2,3},{3,2},{4,5},{5,4},{6,7},{7,6},{8,9},{9,8},{10,11... | collective-permute-start | bytes 2543624 | tf_op jit(solution)/shard_map/ppermute | solution.py:49
  258.7 41.6 %collective-permute-start.19 = (bf16[2,8,368,72]{2,3,1,0:T(8,128)(2,1)}, bf16[2,8,368,72]{2,3,1,0:T(8,128)(2,1)}, u32[]{:S(2)}, u32[]{:S(2)}) collective-permute-start(bf16[2,8,368,72]{2,3,1,0:T(8,128)(2,1)} %fusion.61), channel_id=1, source_target_pairs={{0,2},{2,0},{1,3},{3,1},{4,6},{6,4},{5,7},{7,5},{8,10},{10,8},{9,1... | collective-permute-start | bytes 2543624 | tf_op jit(solution)/shard_map/ppermute | solution.py:49
  287.1 15.6 %collective-permute-start.18 = (bf16[2,8,368,72]{2,3,1,0:T(8,128)(2,1)}, bf16[2,8,368,72]{2,3,1,0:T(8,128)(2,1)}, u32[]{:S(2)}, u32[]{:S(2)}) collective-permute-start(bf16[2,8,368,72]{2,3,1,0:T(8,128)(2,1)} %fusion.62), channel_id=1, source_target_pairs={{0,2},{2,0},{1,3},{3,1},{4,6},{6,4},{5,7},{7,5},{8,10},{10,8},{9,1... | collective-permute-start | bytes 2543624 | tf_op jit(solution)/shard_map/ppermute | solution.py:49
  321.9 196.2 %reduce-scatter.5.cloned.1.call-start = ((), (), s32[]{:S(2)}) async-start(), calls=%async_computation.4 | async-start | bytes 10653696 | tf_op jit(solution)/shard_map/reduce_scatter | solution.py:291
  379.9 21.4 %collective-permute-start.20 = (bf16[368,1152]{1,0:T(8,128)(2,1)}, bf16[368,1152]{1,0:T(8,128)(2,1)S(1)}, u32[]{:S(2)}, u32[]{:S(2)}) collective-permute-start(bf16[368,1152]{1,0:T(8,128)(2,1)} %fusion.125), channel_id=1, source_target_pairs={{0,1},{1,0},{2,3},{3,2},{4,5},{5,4},{6,7},{7,6},{8,9},{9,8},{10,11... | collective-permute-start | bytes 2543624 | tf_op jit(solution)/shard_map/ppermute | solution.py:49
  384.2 19.6 %collective-permute-start.27 = (f32[3304]{0:T(1024)S(1)}, f32[3304]{0:T(1024)S(1)}, u32[]{:S(2)}, u32[]{:S(2)}) collective-permute-start(f32[3304]{0:T(1024)S(1)} %add.378), channel_id=1, source_target_pairs={{0,4},{4,0},{8,12},{12,8},{16,20},{20,16},{24,28},{28,24},{1,5},{5... | collective-permute-start | bytes 39656 | tf_op jit(solution)/shard_map/ppermute | solution.py:114
  403.8 8.6 %collective-permute-start.21 = (f32[6913]{0:T(1024)S(1)}, f32[6913]{0:T(1024)S(1)}, u32[]{:S(2)}, u32[]{:S(2)}) collective-permute-start(f32[6913]{0:T(1024)S(1)} %constant_dynamic-update-slice_fusion), channel_id=1, source_target_pairs={{0,2},{2,0},{1,3},{3,1},{4,6},{6,4},{5,7},{7,5},{8,10},{10,8},{9,1... | collective-permute-start | bytes 82964 | tf_op jit(solution)/shard_map/ppermute | solution.py:114
  407.7 4.6 collective-permute-start.29
  420.5 4.8 collective-permute-start.24
  425.3 5.1 collective-permute-start.25
  (91 other events, 860.9 us)
Sparse Core Ops, SparseCore 0:
  10.8 62.2 all-gather.2
  75.9 83.2 all-gather.4
  322.0 79.1 reduce-scatter.6
  405.2 112.8 reduce-scatter.4

commit v11 on v8

--- a/solution.py
+++ b/solution.py
@@ -260,8 +260,11 @@
     for g, a_part, n_part, p_grad in zip(
         grad_parts, active_parts, normed_two_parts, before_grad_parts
     ):
-        down_term = jnp.einsum("rd,rf->df", g, a_part, preferred_element_type=F32)
-        up_term = jnp.einsum("rd,rf->df", n_part, p_grad, preferred_element_type=F32)
+        term_type = BF if down_grad_t is None else F32
+        down_term = jnp.einsum("rd,rf->df", g, a_part, preferred_element_type=term_type)
+        up_term = jnp.einsum("rd,rf->df", n_part, p_grad, preferred_element_type=term_type)
+        if down_grad_t is None:
+            down_term, up_term = lax.optimization_barrier((down_term, up_term))
         down_grad_t = down_term if down_grad_t is None else down_grad_t + down_term
         up_grad = up_term if up_grad is None else up_grad + up_term
     before_grad = jnp.concatenate(before_grad_parts)
@@ -281,6 +284,10 @@
     out_grad_t = None
     query_parts, key_parts, value_parts = [], [], []
     for i, token_grad in enumerate(hidden_token_parts):
+        if i == 1 and n_t == 2:
+            own_done = (out_grad_t, query_parts[0], key_parts[0], value_parts[0])
+            own_done, token_grad = lax.optimization_barrier((own_done, token_grad))
+            out_grad_t, query_parts[0], key_parts[0], value_parts[0] = own_done
         sl = slice(i * own_images, (i + 1) * own_images)
         token_grad = token_grad.reshape(own_images, half_len, width)
         mixed_i = mixed_per_head[sl]

time: 537 us -> 526 us (0.980)
  waiting for transfers between devices: 261 us -> 254 us
    ppermute x13, waiting for transfers between devices: 102 us -> 92.6 us  [swap(): return lax.ppermute(values, axis, [(0, 1), (1, 0)])]
    unnamed x141 -> x143, local copies, waits for them, and re-layouts: 14 us -> 12.8 us
    another operation x3 -> x4, other arithmetic: 12.5 us -> 12.1 us
  transfers between devices with their start and end apart: 33 -> 33, of which waited for: 22 -> 21; matrix products, arithmetic and copies ran while one was open for 29% -> 28% of each run, Pallas kernels for 0% -> 0%
where the time goes in v11:
time: 526 us; the launch traced here: 521 us
  waiting for transfers between devices  254 us (48%)
  matrix products  111 us (21%)
  other arithmetic  52.6 us (10%)
  local copies, waits for them, and re-layouts  44.5 us (8%)
  starting transfers between devices  38 us (7%)
  between operations  21.1 us (4%)
    reduce_scatter x1, waiting for transfers between devices, on_device_body(): lax.psum_scatter(mlp_grad_pack, ('dp', 'ctx'), scatter_dimension=0, tiled...  109 us
    ppermute x13, waiting for transfers between devices, swap(): return lax.ppermute(values, axis, [(0, 1), (1, 0)])  92.6 us
    all_gather x1, waiting for transfers between devices, on_device_body(): attn_full = lax.all_gather(attn_pack, ('dp', 'ctx'), axis=1, tiled=True)  26.9 us
    ppermute x10, waiting for transfers between devices, tree_sum(): values = jax.tree.map(lambda v: v + lax.ppermute(v, axis, perm), values)  20.4 us
    ppermute x6, starting transfers between devices, gather_vectors(): their_blocks, their_count = lax.ppermute((blocks, count), 'dp', perm)  18.2 us
    unnamed x143, local copies, waits for them, and re-layouts  12.8 us
    ppermute x13, starting transfers between devices, swap(): return lax.ppermute(values, axis, [(0, 1), (1, 0)])  12.7 us
    another operation x4, other arithmetic  12.1 us
  transfers between devices with their start and end apart: 33, of which 21 were waited for; matrix products, arithmetic and copies ran while one was open for 28% of the time, Pallas kernels for 0%

profile of v11, /device:TPU:0, one launch (start us, length us, event | category | flops | bytes accessed | tf_op | source)
XLA Modules:
  0.0 521.3 jit_solution(18052612095481886196)
XLA Ops:
  45.9 26.9 %all-gather.3.cloned.1.call-done = bf16[4,1152,576]{2,1,0:T(8,128)(2,1)} async-done(((bf16[4,72,576]{2,1,0:T(8,128)(2,1)}), bf16[4,1152,576]{2,1,0:T(8,128)(2,1)}) %all-gather.3.cloned.1.call-update) | async-done | bytes 5308432 | tf_op jit(solution)/shard_map/all_gather | solution.py:180
  72.8 4.8 slice.186
  77.6 7.1 %copy.74 = bf16[3,1152,576]{1,2,0:T(8,128)(2,1)} copy(bf16[3,1152,576]{2,1,0:T(8,128)(2,1)} %slice.186) | data formatting | bytes 7962624 | tf_op jit(solution)/shard_map/slice | solution.py:183
  85.6 5.8 %fusion.42 = bf16[3,2,8,368,72]{3,4,1,2,0:T(8,128)(2,1)S(1)} fusion(f32[3,8,72]{2,1,0:T(8,128)S(1)} %maximum_bitcast_fusion, bf16[3,1152,8,72,1]{1,3,4,2,0:T(8,128)(2,1)} %bitcast.307, bf16[1,368,1152]{2,1,0:T(8,128)(2,1)S(1)} %bitcast.336, bf16[1,368,1152]{2,1,0:T(8,128)(2,1)S(1)} %fusion.74), kind=kOutput, calls=%fused_computation.75 | convolution fusion | flops 2936180736 | bytes 8227584 | tf_op jit(solution)/shard_map/pro,tojx->tpjrx/dot_general | solution.py:201
  97.2 5.6 %fusion.140 = (f32[2,8,368]{2,1,0:T(8,128)S(1)}, f32[2,8,368,736]{3,2,1,0:T(8,128)S(1)}) fusion(bf16[2,8,368,72]{2,3,0,1:T(8,128)(2,1)} %get-tuple-element.59, pred[736]{0:T(1024)(128)(4,1)S(1)} %fusion.117, bf16[2,8,368,72]{2,3,0,1:T(8,128)(2,1)} %collective-permute-done.9, bf16[2,8,368,72]{2,3,0,1:T(8,128)(2,1)} %get-tuple-element.61), kind=kOutput, calls=%fused_computation.250 | convolution fusion | flops 640420096 | bytes 19902176 | tf_op jit(solution)/shard_map/bhqe,bhke->bhqk/dot_general | solution.py:210
  118.6 19.5 %collective-permute-done.11 = bf16[368,1152]{1,0:T(8,128)(2,1)S(1)} collective-permute-done((bf16[368,1152]{1,0:T(8,128)(2,1)S(1)}, bf16[368,1152]{1,0:T(8,128)(2,1)S(1)}, u32[]{:S(2)}, u32[]{:S(2)}) %collective-permute-start.11) | collective-permute-done | bytes 847904 | tf_op jit(solution)/shard_map/ppermute | solution.py:49
  140.9 18.8 %collective-permute-done.12 = bf16[368,1152]{1,0:T(8,128)(2,1)} collective-permute-done((bf16[368,1152]{1,0:T(8,128)(2,1)S(1)}, bf16[368,1152]{1,0:T(8,128)(2,1)}, u32[]{:S(2)}, u32[]{:S(2)}) %collective-permute-start.12) | collective-permute-done | bytes 847904 | tf_op jit(solution)/shard_map/ppermute | solution.py:49
  159.8 5.2 convolution_add_fusion.2
  175.1 13.3 %collective-permute-done.13 = bf16[368,1152]{1,0:T(8,128)(2,1)S(1)} collective-permute-done((bf16[368,1152]{1,0:T(8,128)(2,1)S(1)}, bf16[368,1152]{1,0:T(8,128)(2,1)S(1)}, u32[]{:S(2)}, u32[]{:S(2)}) %collective-permute-start.13) | collective-permute-done | bytes 847904 | tf_op jit(solution)/shard_map/ppermute | solution.py:49
  192.9 16.9 %collective-permute-done.14 = bf16[368,1152]{1,0:T(8,128)(2,1)S(1)} collective-permute-done((bf16[368,1152]{1,0:T(8,128)(2,1)S(1)}, bf16[368,1152]{1,0:T(8,128)(2,1)S(1)}, u32[]{:S(2)}, u32[]{:S(2)}) %collective-permute-start.14) | collective-permute-done | bytes 847904 | tf_op jit(solution)/shard_map/ppermute | solution.py:49
  221.4 5.4 %fusion.27 = f32[368,1152]{1,0:T(8,128)S(1)} fusion(bf16[368,2176]{1,0:T(8,128)(2,1)S(1)} %fusion.24, bf16[2,1152,2176]{2,1,0:T(8,128)(2,1)} %all-gather.5.cloned.1.call-done), kind=kOutput, calls=%fused_computation.57 | convolution fusion | flops 1844969472 | bytes 8310784 | tf_op jit(solution)/shard_map/rf,df->rd/dot_general | solution.py:255
  226.9 7.7 %collective-permute-done.15 = bf16[368,1152]{1,0:T(8,128)(2,1)S(1)} collective-permute-done((bf16[368,1152]{1,0:T(8,128)(2,1)S(1)}, bf16[368,1152]{1,0:T(8,128)(2,1)S(1)}, u32[]{:S(2)}, u32[]{:S(2)}) %collective-permute-start.15) | collective-permute-done | bytes 847904 | tf_op jit(solution)/shard_map/ppermute | solution.py:49
  242.0 5.0 fusion.9
  247.1 4.8 fusion.20
  272.7 5.1 fusion.7
  277.8 4.6 fusion.21
  297.8 5.2 %bitcast_convert_fusion = bf16[1152,3,8,72]{0,3,2,1:T(8,128)(2,1)} fusion(bf16[1,368,1152]{2,1,0:T(8,128)(2,1)S(1)} %bitcast.337, bf16[1,368,1152]{2,1,0:T(8,128)(2,1)S(1)} %copy-done.35, bf16[1,2,8,368,72]{3,4,2,1,0:T(8,128)(2,1)S(1)} %bitcast.315, bf16[1,2,8,368,72]{3,4,2,1,0:T(8,128)(2,1)S(1)} %fusion.94, bf16[1,1,8,368,72]{3,4,2,1,0:T(8,128)(2,1)S(1)} %bitcast.319, ...), kind=kOutput, calls=%fused_computation.24 | convolution fusion | flops 2945802240 | bytes 8220672 | tf_op jit(solution)/shard_map/okz,toaks->ztas/dot_general | solution.py:333
  303.0 6.5 %copy.85 = bf16[1152,1728]{1,0:T(8,128)(2,1)} copy(bf16[1152,1728]{0,1:T(8,128)(2,1)} %bitcast.309) | data formatting | bytes 7962624 | tf_op jit(solution)/shard_map/convert_element_type | solution.py:338
  309.5 5.3 %fusion.13 = bf16[1152,2368]{1,0:T(8,128)(2,1)} fusion(bf16[1152,576]{1,0:T(8,128)(2,1)S(1)} %copy.92, bf16[1152,1728]{1,0:T(8,128)(2,1)} %copy.85), kind=kLoop, calls=%fused_computation.28 | loop fusion | flops 16367616 | bytes 10764288 | tf_op jit(solution)/shard_map/concatenate | solution.py:337
  335.8 6.4 %convolution_bitcast_fusion.1 = f32[2,368,1152]{2,1,0:T(8,128)S(1)} fusion(bf16[3,1152,8,72,1]{1,3,2,4,0:T(8,128)(2,1)} %bitcast.308, bf16[1,2,8,368,72]{3,4,2,1,0:T(8,128)(2,1)S(1)} %bitcast.316, bf16[1,2,8,368,72]{3,4,2,1,0:T(8,128)(2,1)} %copy-done.31, bf16[1,1,8,368,72]{3,4,2,1,0:T(8,128)(2,1)} %bitcast.320, bf16[1,1,8,368,72]{3,4,2,1,0:T(8,128)(2,1)S(1)} %bitcast.318), kind=kOutput, calls=%fused_computation.51 | convolution fusion | flops 2934061056 | bytes 9916416 | tf_op jit(solution)/shard_map/toaks,tzas->okz/dot_general | solution.py:345
  350.4 15.9 %collective-permute-done.19 = bf16[368,1152]{1,0:T(8,128)(2,1)S(1)} collective-permute-done((bf16[368,1152]{1,0:T(8,128)(2,1)}, bf16[368,1152]{1,0:T(8,128)(2,1)S(1)}, u32[]{:S(2)}, u32[]{:S(2)}) %collective-permute-start.19) | collective-permute-done | bytes 847904 | tf_op jit(solution)/shard_map/ppermute | solution.py:49
  382.0 5.2 collective-permute-done.22
  387.3 5.2 %collective-permute-done.23 = f32[6913]{0:T(1024)S(1)} collective-permute-done((f32[6913]{0:T(1024)S(1)}, f32[6913]{0:T(1024)S(1)}, u32[]{:S(2)}, u32[]{:S(2)}) %collective-permute-start.23) | collective-permute-done | bytes 27684 | tf_op jit(solution)/shard_map/ppermute | solution.py:114
  401.7 108.5 %reduce-scatter.5.cloned.1.call-done = bf16[72,4352]{1,0:T(8,128)(2,1)} async-done(((bf16[1152,4352]{1,0:T(8,128)(2,1)}), bf16[72,4352]{1,0:T(8,128)(2,1)}) %reduce-scatter.5.cloned.1.call-update) | async-done | bytes 626704 | tf_op jit(solution)/shard_map/reduce_scatter | solution.py:273
  (308 shorter events, 185.4 us)
Async XLA Ops:
  7.2 65.6 %all-gather.3.cloned.1.call-start = ((), (), s32[]{:S(2)}) async-start(), calls=%async_computation.2 | async-start | bytes 6266880 | tf_op jit(solution)/shard_map/all_gather | solution.py:180
  9.2 150.6 %all-gather.5.cloned.1.call-start = ((), (), s32[]{:S(2)}) async-start(), calls=%async_computation.3 | async-start | bytes 10653696 | tf_op jit(solution)/shard_map/all_gather | solution.py:182
  11.2 387.0 %reduce-scatter.7.cloned.1.call-start = ((), (), s32[]{:S(2)}) async-start(), calls=%async_computation.5 | async-start | bytes 5953536
  11.2 4.7 collective-permute-start
  15.1 15.4 %collective-permute-start.4 = (bf16[72,6]{0,1:T(8,128)(2,1)S(1)}, bf16[72,6]{0,1:T(8,128)(2,1)S(1)}, u32[]{:S(2)}, u32[]{:S(2)}) collective-permute-start(bf16[72,6]{0,1:T(8,128)(2,1)S(1)} %stack.100), channel_id=1, source_target_pairs={{0,2},{2,0},{1,3},{3,1},{4,6},{6,4},{5,7},{7,5},{8,10},{10,8},{9,1... | collective-permute-start | bytes 2600 | tf_op jit(solution)/shard_map/ppermute | solution.py:49
  25.1 4.6 collective-permute-start.3
  37.9 4.7 collective-permute-start.7
  43.2 41.5 %collective-permute-start.8 = (bf16[368,1152]{1,0:T(8,128)(2,1)S(1)}, bf16[368,1152]{1,0:T(8,128)(2,1)S(1)}, u32[]{:S(2)}, u32[]{:S(2)}) collective-permute-start(bf16[368,1152]{1,0:T(8,128)(2,1)S(1)} %fusion.62), channel_id=1, source_target_pairs={{0,1},{1,0},{2,3},{3,2},{4,5},{5,4},{6,7},{7,6},{8,9},{9,8},{10,11... | collective-permute-start | bytes 2543624 | tf_op jit(solution)/shard_map/ppermute | solution.py:49
  96.5 10.4 %collective-permute-start.10 = (bf16[2,8,368,72]{2,3,0,1:T(8,128)(2,1)S(1)}, bf16[2,8,368,72]{2,3,0,1:T(8,128)(2,1)S(1)}, u32[]{:S(2)}, u32[]{:S(2)}) collective-permute-start(bf16[2,8,368,72]{2,3,0,1:T(8,128)(2,1)S(1)} %get-tuple-element.60), channel_id=1, source_target_pairs={{0,2},{2,0},{1,3},{3,1},{4,6},{6,4},{5,7},{7,5},{8,10},{10,8},{9,1... | collective-permute-start | bytes 2543624 | tf_op jit(solution)/shard_map/ppermute | solution.py:49
  117.1 21.1 %collective-permute-start.11 = (bf16[368,1152]{1,0:T(8,128)(2,1)S(1)}, bf16[368,1152]{1,0:T(8,128)(2,1)S(1)}, u32[]{:S(2)}, u32[]{:S(2)}) collective-permute-start(bf16[368,1152]{1,0:T(8,128)(2,1)S(1)} %fusion.110), channel_id=1, source_target_pairs={{0,1},{1,0},{2,3},{3,2},{4,5},{5,4},{6,7},{7,6},{8,9},{9,8},{10,11... | collective-permute-start | bytes 2543624 | tf_op jit(solution)/shard_map/ppermute | solution.py:49
  139.3 20.4 %collective-permute-start.12 = (bf16[368,1152]{1,0:T(8,128)(2,1)S(1)}, bf16[368,1152]{1,0:T(8,128)(2,1)}, u32[]{:S(2)}, u32[]{:S(2)}) collective-permute-start(bf16[368,1152]{1,0:T(8,128)(2,1)S(1)} %add_convert_fusion.2), channel_id=1, source_target_pairs={{0,1},{1,0},{2,3},{3,2},{4,5},{5,4},{6,7},{7,6},{8,9},{9,8},{10,11... | collective-permute-start | bytes 2543624 | tf_op jit(solution)/shard_map/ppermute | solution.py:49
  168.3 20.2 %collective-permute-start.13 = (bf16[368,1152]{1,0:T(8,128)(2,1)S(1)}, bf16[368,1152]{1,0:T(8,128)(2,1)S(1)}, u32[]{:S(2)}, u32[]{:S(2)}) collective-permute-start(bf16[368,1152]{1,0:T(8,128)(2,1)S(1)} %fusion.40), channel_id=1, source_target_pairs={{0,1},{1,0},{2,3},{3,2},{4,5},{5,4},{6,7},{7,6},{8,9},{9,8},{10,11... | collective-permute-start | bytes 2543624 | tf_op jit(solution)/shard_map/ppermute | solution.py:49
  190.5 19.3 %collective-permute-start.14 = (bf16[368,1152]{1,0:T(8,128)(2,1)S(1)}, bf16[368,1152]{1,0:T(8,128)(2,1)S(1)}, u32[]{:S(2)}, u32[]{:S(2)}) collective-permute-start(bf16[368,1152]{1,0:T(8,128)(2,1)S(1)} %multiply_convert_fusion.2), channel_id=1, source_target_pairs={{0,1},{1,0},{2,3},{3,2},{4,5},{5,4},{6,7},{7,6},{8,9},{9,8},{10,11... | collective-permute-start | bytes 2543624 | tf_op jit(solution)/shard_map/ppermute | solution.py:49
  216.1 18.5 %collective-permute-start.15 = (bf16[368,1152]{1,0:T(8,128)(2,1)S(1)}, bf16[368,1152]{1,0:T(8,128)(2,1)S(1)}, u32[]{:S(2)}, u32[]{:S(2)}) collective-permute-start(bf16[368,1152]{1,0:T(8,128)(2,1)S(1)} %fusion.41), channel_id=1, source_target_pairs={{0,1},{1,0},{2,3},{3,2},{4,5},{5,4},{6,7},{7,6},{8,9},{9,8},{10,11... | collective-permute-start | bytes 2543624 | tf_op jit(solution)/shard_map/ppermute | solution.py:49
  238.4 25.8 %collective-permute-start.16 = (bf16[368,1152]{1,0:T(8,128)(2,1)}, bf16[368,1152]{1,0:T(8,128)(2,1)}, u32[]{:S(2)}, u32[]{:S(2)}) collective-permute-start(bf16[368,1152]{1,0:T(8,128)(2,1)} %convert_element_type.207), channel_id=1, source_target_pairs={{0,1},{1,0},{2,3},{3,2},{4,5},{5,4},{6,7},{7,6},{8,9},{9,8},{10,11... | collective-permute-start | bytes 2543624 | tf_op jit(solution)/shard_map/ppermute | solution.py:49
  270.6 23.3 %collective-permute-start.18 = (bf16[2,8,368,72]{2,3,1,0:T(8,128)(2,1)}, bf16[2,8,368,72]{2,3,1,0:T(8,128)(2,1)}, u32[]{:S(2)}, u32[]{:S(2)}) collective-permute-start(bf16[2,8,368,72]{2,3,1,0:T(8,128)(2,1)} %fusion.57), channel_id=1, source_target_pairs={{0,2},{2,0},{1,3},{3,1},{4,6},{6,4},{5,7},{7,5},{8,10},{10,8},{9,1... | collective-permute-start | bytes 2543624 | tf_op jit(solution)/shard_map/ppermute | solution.py:49
  287.3 8.4 %collective-permute-start.17 = (bf16[2,8,368,72]{2,3,1,0:T(8,128)(2,1)}, bf16[2,8,368,72]{2,3,1,0:T(8,128)(2,1)}, u32[]{:S(2)}, u32[]{:S(2)}) collective-permute-start(bf16[2,8,368,72]{2,3,1,0:T(8,128)(2,1)} %fusion.58), channel_id=1, source_target_pairs={{0,2},{2,0},{1,3},{3,1},{4,6},{6,4},{5,7},{7,5},{8,10},{10,8},{9,1... | collective-permute-start | bytes 2543624 | tf_op jit(solution)/shard_map/ppermute | solution.py:49
  314.8 195.4 %reduce-scatter.5.cloned.1.call-start = ((), (), s32[]{:S(2)}) async-start(), calls=%async_computation.4 | async-start | bytes 10653696 | tf_op jit(solution)/shard_map/reduce_scatter | solution.py:273
  344.9 21.4 %collective-permute-start.19 = (bf16[368,1152]{1,0:T(8,128)(2,1)}, bf16[368,1152]{1,0:T(8,128)(2,1)S(1)}, u32[]{:S(2)}, u32[]{:S(2)}) collective-permute-start(bf16[368,1152]{1,0:T(8,128)(2,1)} %fusion.111), channel_id=1, source_target_pairs={{0,1},{1,0},{2,3},{3,2},{4,5},{5,4},{6,7},{7,6},{8,9},{9,8},{10,11... | collective-permute-start | bytes 2543624 | tf_op jit(solution)/shard_map/ppermute | solution.py:49
  349.5 19.4 %collective-permute-start.26 = (f32[3304]{0:T(1024)S(1)}, f32[3304]{0:T(1024)S(1)}, u32[]{:S(2)}, u32[]{:S(2)}) collective-permute-start(f32[3304]{0:T(1024)S(1)} %add.342), channel_id=1, source_target_pairs={{0,4},{4,0},{8,12},{12,8},{16,20},{20,16},{24,28},{28,24},{1,5},{5... | collective-permute-start | bytes 39656 | tf_op jit(solution)/shard_map/ppermute | solution.py:114
  368.8 8.6 %collective-permute-start.20 = (f32[6913]{0:T(1024)S(1)}, f32[6913]{0:T(1024)S(1)}, u32[]{:S(2)}, u32[]{:S(2)}) collective-permute-start(f32[6913]{0:T(1024)S(1)} %constant_dynamic-update-slice_fusion), channel_id=1, source_target_pairs={{0,2},{2,0},{1,3},{3,1},{4,6},{6,4},{5,7},{7,5},{8,10},{10,8},{9,1... | collective-permute-start | bytes 82964 | tf_op jit(solution)/shard_map/ppermute | solution.py:114
  372.7 4.6 collective-permute-start.28
  381.9 5.4 %collective-permute-start.22 = (f32[6913]{0:T(1024)S(1)}, f32[6913]{0:T(1024)S(1)}, u32[]{:S(2)}, u32[]{:S(2)}) collective-permute-start(f32[6913]{0:T(1024)S(1)} %add.333), channel_id=1, source_target_pairs={{0,8},{4,12},{8,0},{12,4},{16,24},{20,28},{24,16},{28,20},{1,9},{5... | collective-permute-start | bytes 82964 | tf_op jit(solution)/shard_map/ppermute | solution.py:114
  387.2 5.3 %collective-permute-start.23 = (f32[6913]{0:T(1024)S(1)}, f32[6913]{0:T(1024)S(1)}, u32[]{:S(2)}, u32[]{:S(2)}) collective-permute-start(f32[6913]{0:T(1024)S(1)} %add.334), channel_id=1, source_target_pairs={{0,16},{4,20},{8,24},{12,28},{16,0},{20,4},{24,8},{28,12},{1,17},{... | collective-permute-start | bytes 82964 | tf_op jit(solution)/shard_map/ppermute | solution.py:114
  (78 other events, 825.0 us)
Sparse Core Ops, SparseCore 0:
  10.8 61.9 all-gather.2
  75.6 83.2 all-gather.4
  314.9 78.6 reduce-scatter.6
  397.6 112.5 reduce-scatter.4

commit v12 on v11

--- a/solution.py
+++ b/solution.py
@@ -171,7 +171,6 @@
     images = n_t * own_images
 
     pad_hidden = (-hidden_width) % 128
-    pad_out = (-head_width) % 128
     vector_rows = jnp.stack([ln1_gain, ln1_bias, b_o, ln2_gain, ln2_bias, b_down], axis=1)
     vectors, valid_count = gather_vectors(vector_rows, jnp.sum(valid_len.astype(jnp.int32)))
     valid_count = valid_count.astype(F32)
@@ -335,7 +334,7 @@
     ).reshape(width, 3 * head_width)
     attn_grads = lax.psum_scatter(
         jnp.concatenate(
-            [jnp.pad(out_grad_t.astype(BF), ((0, 0), (0, pad_out))), qkv_weight_grad.astype(BF)],
+            [qkv_weight_grad.astype(BF), out_grad_t.astype(BF)],
             axis=1,
         ),
         ("dp", "ctx"),
@@ -375,11 +374,7 @@
     up_bias_sum = head_sums[2 * head_width :]
     attn_grads = attn_grads.astype(F32)
     mlp_grads = mlp_grads.astype(F32)
-    out_cols = head_width + pad_out
-    attn_grads = [
-        attn_grads[:, out_cols + i * head_width : out_cols + (i + 1) * head_width]
-        for i in range(3)
-    ] + [attn_grads[:, :head_width]]
+    attn_grads = [attn_grads[:, i * head_width : (i + 1) * head_width] for i in range(4)]
     hidden_cols = hidden_width + pad_hidden
     mlp_grads = [
         mlp_grads[:, :hidden_width],

time: 526 us -> 524 us (level)
    unnamed x143 -> x142, local copies, waits for them, and re-layouts: 12.8 us -> 11.7 us
where the time goes in v12:
time: 524 us; the launch traced here: 520 us
  waiting for transfers between devices  252 us (48%)
  matrix products  111 us (21%)
  other arithmetic  52.9 us (10%)
  local copies, waits for them, and re-layouts  44.6 us (9%)
  starting transfers between devices  37.8 us (7%)
  between operations  21.1 us (4%)
    reduce_scatter x1, waiting for transfers between devices, on_device_body(): lax.psum_scatter(mlp_grad_pack, ('dp', 'ctx'), scatter_dimension=0, tiled...  107 us
    ppermute x13, waiting for transfers between devices, swap(): return lax.ppermute(values, axis, [(0, 1), (1, 0)])  92.6 us
    all_gather x1, waiting for transfers between devices, on_device_body(): attn_full = lax.all_gather(attn_pack, ('dp', 'ctx'), axis=1, tiled=True)  26.9 us
    ppermute x10, waiting for transfers between devices, tree_sum(): values = jax.tree.map(lambda v: v + lax.ppermute(v, axis, perm), values)  19.7 us
    ppermute x6, starting transfers between devices, gather_vectors(): their_blocks, their_count = lax.ppermute((blocks, count), 'dp', perm)  18.2 us
    ppermute x13, starting transfers between devices, swap(): return lax.ppermute(values, axis, [(0, 1), (1, 0)])  12.7 us
    another operation x4, other arithmetic  12.1 us
    slice x2, local copies, waits for them, and re-layouts, on_device_body(): qkv_w = attn_full[:3].reshape(3, width, local_heads, HD)  11.9 us
  transfers between devices with their start and end apart: 33, of which 21 were waited for; matrix products, arithmetic and copies ran while one was open for 28% of the time, Pallas kernels for 0%

profile of v12, /device:TPU:0, one launch (start us, length us, event | category | flops | bytes accessed | tf_op | source)
XLA Modules:
  0.0 519.6 jit_solution(7397484327318829371)
XLA Ops:
  45.9 26.9 %all-gather.3.cloned.1.call-done = bf16[4,1152,576]{2,1,0:T(8,128)(2,1)} async-done(((bf16[4,72,576]{2,1,0:T(8,128)(2,1)}), bf16[4,1152,576]{2,1,0:T(8,128)(2,1)}) %all-gather.3.cloned.1.call-update) | async-done | bytes 5308432 | tf_op jit(solution)/shard_map/all_gather | solution.py:179
  72.8 4.8 slice.186
  77.6 7.1 %copy.65 = bf16[3,1152,576]{1,2,0:T(8,128)(2,1)} copy(bf16[3,1152,576]{2,1,0:T(8,128)(2,1)} %slice.186) | data formatting | bytes 7962624 | tf_op jit(solution)/shard_map/slice | solution.py:182
  85.6 5.8 %fusion.40 = bf16[3,2,8,368,72]{3,4,1,2,0:T(8,128)(2,1)S(1)} fusion(f32[3,8,72]{2,1,0:T(8,128)S(1)} %maximum_bitcast_fusion, bf16[3,1152,8,72,1]{1,3,4,2,0:T(8,128)(2,1)} %bitcast.306, bf16[1,368,1152]{2,1,0:T(8,128)(2,1)S(1)} %bitcast.335, bf16[1,368,1152]{2,1,0:T(8,128)(2,1)S(1)} %fusion.72), kind=kOutput, calls=%fused_computation.73 | convolution fusion | flops 2936180736 | bytes 8227584 | tf_op jit(solution)/shard_map/pro,tojx->tpjrx/dot_general | solution.py:200
  97.2 5.6 %fusion.138 = (f32[2,8,368]{2,1,0:T(8,128)S(1)}, f32[2,8,368,736]{3,2,1,0:T(8,128)S(1)}) fusion(bf16[2,8,368,72]{2,3,0,1:T(8,128)(2,1)} %get-tuple-element.59, pred[736]{0:T(1024)(128)(4,1)S(1)} %fusion.115, bf16[2,8,368,72]{2,3,0,1:T(8,128)(2,1)} %collective-permute-done.9, bf16[2,8,368,72]{2,3,0,1:T(8,128)(2,1)} %get-tuple-element.61), kind=kOutput, calls=%fused_computation.248 | convolution fusion | flops 640420096 | bytes 19902176 | tf_op jit(solution)/shard_map/bhqe,bhke->bhqk/dot_general | solution.py:209
  109.0 4.6 fusion.83
  118.6 19.5 %collective-permute-done.11 = bf16[368,1152]{1,0:T(8,128)(2,1)S(1)} collective-permute-done((bf16[368,1152]{1,0:T(8,128)(2,1)S(1)}, bf16[368,1152]{1,0:T(8,128)(2,1)S(1)}, u32[]{:S(2)}, u32[]{:S(2)}) %collective-permute-start.11) | collective-permute-done | bytes 847904 | tf_op jit(solution)/shard_map/ppermute | solution.py:49
  140.9 18.8 %collective-permute-done.12 = bf16[368,1152]{1,0:T(8,128)(2,1)} collective-permute-done((bf16[368,1152]{1,0:T(8,128)(2,1)S(1)}, bf16[368,1152]{1,0:T(8,128)(2,1)}, u32[]{:S(2)}, u32[]{:S(2)}) %collective-permute-start.12) | collective-permute-done | bytes 847904 | tf_op jit(solution)/shard_map/ppermute | solution.py:49
  159.8 5.2 convolution_add_fusion.2
  175.1 13.3 %collective-permute-done.13 = bf16[368,1152]{1,0:T(8,128)(2,1)S(1)} collective-permute-done((bf16[368,1152]{1,0:T(8,128)(2,1)S(1)}, bf16[368,1152]{1,0:T(8,128)(2,1)S(1)}, u32[]{:S(2)}, u32[]{:S(2)}) %collective-permute-start.13) | collective-permute-done | bytes 847904 | tf_op jit(solution)/shard_map/ppermute | solution.py:49
  192.9 16.9 %collective-permute-done.14 = bf16[368,1152]{1,0:T(8,128)(2,1)S(1)} collective-permute-done((bf16[368,1152]{1,0:T(8,128)(2,1)S(1)}, bf16[368,1152]{1,0:T(8,128)(2,1)S(1)}, u32[]{:S(2)}, u32[]{:S(2)}) %collective-permute-start.14) | collective-permute-done | bytes 847904 | tf_op jit(solution)/shard_map/ppermute | solution.py:49
  221.4 5.4 %fusion.25 = f32[368,1152]{1,0:T(8,128)S(1)} fusion(bf16[368,2176]{1,0:T(8,128)(2,1)S(1)} %fusion.22, bf16[2,1152,2176]{2,1,0:T(8,128)(2,1)} %all-gather.5.cloned.1.call-done), kind=kOutput, calls=%fused_computation.55 | convolution fusion | flops 1844969472 | bytes 8310784 | tf_op jit(solution)/shard_map/rf,df->rd/dot_general | solution.py:254
  226.9 7.7 %collective-permute-done.15 = bf16[368,1152]{1,0:T(8,128)(2,1)S(1)} collective-permute-done((bf16[368,1152]{1,0:T(8,128)(2,1)S(1)}, bf16[368,1152]{1,0:T(8,128)(2,1)S(1)}, u32[]{:S(2)}, u32[]{:S(2)}) %collective-permute-start.15) | collective-permute-done | bytes 847904 | tf_op jit(solution)/shard_map/ppermute | solution.py:49
  242.0 5.0 fusion.8
  247.1 4.8 fusion.18
  272.7 5.1 fusion.6
  277.8 4.6 fusion.19
  297.8 5.2 %bitcast_convert_fusion = bf16[1152,3,8,72]{0,3,2,1:T(8,128)(2,1)} fusion(bf16[1,368,1152]{2,1,0:T(8,128)(2,1)S(1)} %bitcast.336, bf16[1,368,1152]{2,1,0:T(8,128)(2,1)S(1)} %copy-done.35, bf16[1,2,8,368,72]{3,4,2,1,0:T(8,128)(2,1)S(1)} %bitcast.314, bf16[1,2,8,368,72]{3,4,2,1,0:T(8,128)(2,1)S(1)} %fusion.92, bf16[1,1,8,368,72]{3,4,2,1,0:T(8,128)(2,1)S(1)} %bitcast.318, ...), kind=kOutput, calls=%fused_computation.22 | convolution fusion | flops 2945802240 | bytes 8220672 | tf_op jit(solution)/shard_map/okz,toaks->ztas/dot_general | solution.py:332
  303.0 6.5 %copy.75 = bf16[1152,1728]{1,0:T(8,128)(2,1)} copy(bf16[1152,1728]{0,1:T(8,128)(2,1)} %bitcast.308) | data formatting | bytes 7962624 | tf_op jit(solution)/shard_map/convert_element_type | solution.py:337
  309.5 5.6 %pad_maximum_fusion.1 = bf16[1152,2304]{1,0:T(8,128)(2,1)} fusion(bf16[1152,576]{1,0:T(8,128)(2,1)S(1)} %copy.76, bf16[1152,1728]{1,0:T(8,128)(2,1)} %copy.75), kind=kLoop, calls=%fused_computation.26 | loop fusion | flops 10616832 | bytes 10616832 | tf_op jit(solution)/shard_map/concatenate | solution.py:336
  336.0 6.4 %convolution_bitcast_fusion.1 = f32[2,368,1152]{2,1,0:T(8,128)S(1)} fusion(bf16[3,1152,8,72,1]{1,3,2,4,0:T(8,128)(2,1)} %bitcast.307, bf16[1,2,8,368,72]{3,4,2,1,0:T(8,128)(2,1)S(1)} %bitcast.315, bf16[1,2,8,368,72]{3,4,2,1,0:T(8,128)(2,1)} %copy-done.31, bf16[1,1,8,368,72]{3,4,2,1,0:T(8,128)(2,1)} %bitcast.319, bf16[1,1,8,368,72]{3,4,2,1,0:T(8,128)(2,1)S(1)} %bitcast.317), kind=kOutput, calls=%fused_computation.49 | convolution fusion | flops 2934061056 | bytes 9916416 | tf_op jit(solution)/shard_map/toaks,tzas->okz/dot_general | solution.py:344
  350.7 15.9 %collective-permute-done.19 = bf16[368,1152]{1,0:T(8,128)(2,1)S(1)} collective-permute-done((bf16[368,1152]{1,0:T(8,128)(2,1)}, bf16[368,1152]{1,0:T(8,128)(2,1)S(1)}, u32[]{:S(2)}, u32[]{:S(2)}) %collective-permute-start.19) | collective-permute-done | bytes 847904 | tf_op jit(solution)/shard_map/ppermute | solution.py:49
  382.0 5.2 %collective-permute-done.22 = f32[6913]{0:T(1024)S(1)} collective-permute-done((f32[6913]{0:T(1024)S(1)}, f32[6913]{0:T(1024)S(1)}, u32[]{:S(2)}, u32[]{:S(2)}) %collective-permute-start.22) | collective-permute-done | bytes 27684 | tf_op jit(solution)/shard_map/ppermute | solution.py:114
  401.3 107.2 %reduce-scatter.5.cloned.1.call-done = bf16[72,4352]{1,0:T(8,128)(2,1)} async-done(((bf16[1152,4352]{1,0:T(8,128)(2,1)}), bf16[72,4352]{1,0:T(8,128)(2,1)}) %reduce-scatter.5.cloned.1.call-update) | async-done | bytes 626704 | tf_op jit(solution)/shard_map/reduce_scatter | solution.py:272
  (308 shorter events, 185.2 us)
Async XLA Ops:
  7.2 65.6 %all-gather.3.cloned.1.call-start = ((), (), s32[]{:S(2)}) async-start(), calls=%async_computation.2 | async-start | bytes 6266880 | tf_op jit(solution)/shard_map/all_gather | solution.py:179
  9.2 150.6 %all-gather.5.cloned.1.call-start = ((), (), s32[]{:S(2)}) async-start(), calls=%async_computation.3 | async-start | bytes 10653696 | tf_op jit(solution)/shard_map/all_gather | solution.py:181
  11.2 386.5 %reduce-scatter.3.cloned.1.call-start = ((), (), s32[]{:S(2)}) async-start(), calls=%async_computation.4 | async-start | bytes 5640192 | tf_op jit(solution)/shard_map/reduce_scatter | solution.py:335
  11.2 4.7 collective-permute-start
  15.1 15.4 %collective-permute-start.4 = (bf16[72,6]{0,1:T(8,128)(2,1)S(1)}, bf16[72,6]{0,1:T(8,128)(2,1)S(1)}, u32[]{:S(2)}, u32[]{:S(2)}) collective-permute-start(bf16[72,6]{0,1:T(8,128)(2,1)S(1)} %stack.100), channel_id=1, source_target_pairs={{0,2},{2,0},{1,3},{3,1},{4,6},{6,4},{5,7},{7,5},{8,10},{10,8},{9,1... | collective-permute-start | bytes 2600 | tf_op jit(solution)/shard_map/ppermute | solution.py:49
  25.1 4.6 collective-permute-start.3
  37.9 4.7 collective-permute-start.7
  43.2 41.5 %collective-permute-start.8 = (bf16[368,1152]{1,0:T(8,128)(2,1)S(1)}, bf16[368,1152]{1,0:T(8,128)(2,1)S(1)}, u32[]{:S(2)}, u32[]{:S(2)}) collective-permute-start(bf16[368,1152]{1,0:T(8,128)(2,1)S(1)} %fusion.60), channel_id=1, source_target_pairs={{0,1},{1,0},{2,3},{3,2},{4,5},{5,4},{6,7},{7,6},{8,9},{9,8},{10,11... | collective-permute-start | bytes 2543624 | tf_op jit(solution)/shard_map/ppermute | solution.py:49
  96.5 10.4 %collective-permute-start.10 = (bf16[2,8,368,72]{2,3,0,1:T(8,128)(2,1)S(1)}, bf16[2,8,368,72]{2,3,0,1:T(8,128)(2,1)S(1)}, u32[]{:S(2)}, u32[]{:S(2)}) collective-permute-start(bf16[2,8,368,72]{2,3,0,1:T(8,128)(2,1)S(1)} %get-tuple-element.60), channel_id=1, source_target_pairs={{0,2},{2,0},{1,3},{3,1},{4,6},{6,4},{5,7},{7,5},{8,10},{10,8},{9,1... | collective-permute-start | bytes 2543624 | tf_op jit(solution)/shard_map/ppermute | solution.py:49
  117.1 21.1 %collective-permute-start.11 = (bf16[368,1152]{1,0:T(8,128)(2,1)S(1)}, bf16[368,1152]{1,0:T(8,128)(2,1)S(1)}, u32[]{:S(2)}, u32[]{:S(2)}) collective-permute-start(bf16[368,1152]{1,0:T(8,128)(2,1)S(1)} %fusion.108), channel_id=1, source_target_pairs={{0,1},{1,0},{2,3},{3,2},{4,5},{5,4},{6,7},{7,6},{8,9},{9,8},{10,11... | collective-permute-start | bytes 2543624 | tf_op jit(solution)/shard_map/ppermute | solution.py:49
  139.3 20.4 %collective-permute-start.12 = (bf16[368,1152]{1,0:T(8,128)(2,1)S(1)}, bf16[368,1152]{1,0:T(8,128)(2,1)}, u32[]{:S(2)}, u32[]{:S(2)}) collective-permute-start(bf16[368,1152]{1,0:T(8,128)(2,1)S(1)} %add_convert_fusion.2), channel_id=1, source_target_pairs={{0,1},{1,0},{2,3},{3,2},{4,5},{5,4},{6,7},{7,6},{8,9},{9,8},{10,11... | collective-permute-start | bytes 2543624 | tf_op jit(solution)/shard_map/ppermute | solution.py:49
  168.3 20.2 %collective-permute-start.13 = (bf16[368,1152]{1,0:T(8,128)(2,1)S(1)}, bf16[368,1152]{1,0:T(8,128)(2,1)S(1)}, u32[]{:S(2)}, u32[]{:S(2)}) collective-permute-start(bf16[368,1152]{1,0:T(8,128)(2,1)S(1)} %fusion.38), channel_id=1, source_target_pairs={{0,1},{1,0},{2,3},{3,2},{4,5},{5,4},{6,7},{7,6},{8,9},{9,8},{10,11... | collective-permute-start | bytes 2543624 | tf_op jit(solution)/shard_map/ppermute | solution.py:49
  190.5 19.3 %collective-permute-start.14 = (bf16[368,1152]{1,0:T(8,128)(2,1)S(1)}, bf16[368,1152]{1,0:T(8,128)(2,1)S(1)}, u32[]{:S(2)}, u32[]{:S(2)}) collective-permute-start(bf16[368,1152]{1,0:T(8,128)(2,1)S(1)} %multiply_convert_fusion.2), channel_id=1, source_target_pairs={{0,1},{1,0},{2,3},{3,2},{4,5},{5,4},{6,7},{7,6},{8,9},{9,8},{10,11... | collective-permute-start | bytes 2543624 | tf_op jit(solution)/shard_map/ppermute | solution.py:49
  216.1 18.5 %collective-permute-start.15 = (bf16[368,1152]{1,0:T(8,128)(2,1)S(1)}, bf16[368,1152]{1,0:T(8,128)(2,1)S(1)}, u32[]{:S(2)}, u32[]{:S(2)}) collective-permute-start(bf16[368,1152]{1,0:T(8,128)(2,1)S(1)} %fusion.39), channel_id=1, source_target_pairs={{0,1},{1,0},{2,3},{3,2},{4,5},{5,4},{6,7},{7,6},{8,9},{9,8},{10,11... | collective-permute-start | bytes 2543624 | tf_op jit(solution)/shard_map/ppermute | solution.py:49
  238.4 25.8 %collective-permute-start.16 = (bf16[368,1152]{1,0:T(8,128)(2,1)}, bf16[368,1152]{1,0:T(8,128)(2,1)}, u32[]{:S(2)}, u32[]{:S(2)}) collective-permute-start(bf16[368,1152]{1,0:T(8,128)(2,1)} %convert_element_type.205), channel_id=1, source_target_pairs={{0,1},{1,0},{2,3},{3,2},{4,5},{5,4},{6,7},{7,6},{8,9},{9,8},{10,11... | collective-permute-start | bytes 2543624 | tf_op jit(solution)/shard_map/ppermute | solution.py:49
  270.6 23.3 %collective-permute-start.18 = (bf16[2,8,368,72]{2,3,1,0:T(8,128)(2,1)}, bf16[2,8,368,72]{2,3,1,0:T(8,128)(2,1)}, u32[]{:S(2)}, u32[]{:S(2)}) collective-permute-start(bf16[2,8,368,72]{2,3,1,0:T(8,128)(2,1)} %fusion.55), channel_id=1, source_target_pairs={{0,2},{2,0},{1,3},{3,1},{4,6},{6,4},{5,7},{7,5},{8,10},{10,8},{9,1... | collective-permute-start | bytes 2543624 | tf_op jit(solution)/shard_map/ppermute | solution.py:49
  287.3 8.4 %collective-permute-start.17 = (bf16[2,8,368,72]{2,3,1,0:T(8,128)(2,1)}, bf16[2,8,368,72]{2,3,1,0:T(8,128)(2,1)}, u32[]{:S(2)}, u32[]{:S(2)}) collective-permute-start(bf16[2,8,368,72]{2,3,1,0:T(8,128)(2,1)} %fusion.56), channel_id=1, source_target_pairs={{0,2},{2,0},{1,3},{3,1},{4,6},{6,4},{5,7},{7,5},{8,10},{10,8},{9,1... | collective-permute-start | bytes 2543624 | tf_op jit(solution)/shard_map/ppermute | solution.py:49
  315.1 193.4 %reduce-scatter.5.cloned.1.call-start = ((), (), s32[]{:S(2)}) async-start(), calls=%async_computation.5 | async-start | bytes 10653696 | tf_op jit(solution)/shard_map/reduce_scatter | solution.py:272
  345.2 21.4 %collective-permute-start.19 = (bf16[368,1152]{1,0:T(8,128)(2,1)}, bf16[368,1152]{1,0:T(8,128)(2,1)S(1)}, u32[]{:S(2)}, u32[]{:S(2)}) collective-permute-start(bf16[368,1152]{1,0:T(8,128)(2,1)} %fusion.109), channel_id=1, source_target_pairs={{0,1},{1,0},{2,3},{3,2},{4,5},{5,4},{6,7},{7,6},{8,9},{9,8},{10,11... | collective-permute-start | bytes 2543624 | tf_op jit(solution)/shard_map/ppermute | solution.py:49
  349.8 19.4 %collective-permute-start.26 = (f32[3304]{0:T(1024)S(1)}, f32[3304]{0:T(1024)S(1)}, u32[]{:S(2)}, u32[]{:S(2)}) collective-permute-start(f32[3304]{0:T(1024)S(1)} %add.340), channel_id=1, source_target_pairs={{0,4},{4,0},{8,12},{12,8},{16,20},{20,16},{24,28},{28,24},{1,5},{5... | collective-permute-start | bytes 39656 | tf_op jit(solution)/shard_map/ppermute | solution.py:114
  369.1 8.9 %collective-permute-start.20 = (f32[6913]{0:T(1024)S(1)}, f32[6913]{0:T(1024)S(1)}, u32[]{:S(2)}, u32[]{:S(2)}) collective-permute-start(f32[6913]{0:T(1024)S(1)} %constant_dynamic-update-slice_fusion), channel_id=1, source_target_pairs={{0,2},{2,0},{1,3},{3,1},{4,6},{6,4},{5,7},{7,5},{8,10},{10,8},{9,1... | collective-permute-start | bytes 82964 | tf_op jit(solution)/shard_map/ppermute | solution.py:114
  373.0 4.9 collective-permute-start.28
  381.9 5.2 %collective-permute-start.22 = (f32[6913]{0:T(1024)S(1)}, f32[6913]{0:T(1024)S(1)}, u32[]{:S(2)}, u32[]{:S(2)}) collective-permute-start(f32[6913]{0:T(1024)S(1)} %add.331), channel_id=1, source_target_pairs={{0,8},{4,12},{8,0},{12,4},{16,24},{20,28},{24,16},{28,20},{1,9},{5... | collective-permute-start | bytes 82964 | tf_op jit(solution)/shard_map/ppermute | solution.py:114
  387.2 4.8 collective-permute-start.23
  (78 other events, 823.8 us)
Sparse Core Ops, SparseCore 0:
  10.8 61.9 all-gather.2
  75.6 83.2 all-gather.4
  315.2 76.1 reduce-scatter.2
  395.4 113.0 reduce-scatter.4
